TPU v7x, 32 devices: a whole 2x2x4 slice. The times are simulated.
32 devices in a mesh: dp: 4 (over z), ctx: 4 (over x, core), fsdp: 2 (over y).
Axes of the slice: x: 2, y: 2, z: 4, core: 2. Of those that a mesh axis runs over, the one named last changes fastest.
Arguments:
- tokens: bfloat16 [16, 1024, 768], P(('dp', 'fsdp'), 'ctx'), may hold values from -12 to 12
- cotangent: bfloat16 [16, 1024, 768], P(('dp', 'fsdp'), 'ctx'), may hold values from -6 to 6
- lengths: int32 [16], P(('dp', 'fsdp')), may hold values from 256 to 1024, as said below
- w_qkv: bfloat16 [768, 2304], P('fsdp'), may hold values from -0.21875 to 0.21875
- bias_q: bfloat16 [768], P('fsdp'), may hold values from -3 to 3
- bias_v: bfloat16 [768], P('fsdp'), may hold values from -0.29882812 to 0.29882812
- w_out: bfloat16 [768, 768], P('fsdp'), may hold values from -6 to 6
- bias_out: bfloat16 [768], P('fsdp'), may hold values from -3 to 3
- gain_one: bfloat16 [768], P('fsdp'), may hold values from 0.5 to 1.5
- shift_one: bfloat16 [768], P('fsdp'), may hold values from -3 to 3
- w_up: bfloat16 [768, 3072], P('fsdp'), may hold values from -0.21875 to 0.21875
- bias_up: bfloat16 [3072], P('fsdp'), may hold values from -3 to 3
- w_down: bfloat16 [3072, 768], P('fsdp'), may hold values from -0.109375 to 0.109375
- bias_down: bfloat16 [768], P('fsdp'), may hold values from -3 to 3
- gain_two: bfloat16 [768], P('fsdp'), may hold values from 0.5 to 1.5
- shift_two: bfloat16 [768], P('fsdp'), may hold values from -3 to 3
Outputs:
- output: bfloat16 [16, 1024, 768], P(('dp', 'fsdp'), 'ctx')
- input_grad: bfloat16 [16, 1024, 768], P(('dp', 'fsdp'), 'ctx')
- grad_w_qkv: float32 [768, 2304], P('fsdp')
- grad_bias_q: float32 [768], P('fsdp')
- grad_bias_v: float32 [768], P('fsdp')
- grad_w_out: float32 [768, 768], P('fsdp')
- grad_bias_out: float32 [768], P('fsdp')
- grad_gain_one: float32 [768], P('fsdp')
- grad_shift_one: float32 [768], P('fsdp')
- grad_w_up: float32 [768, 3072], P('fsdp')
- grad_bias_up: float32 [3072], P('fsdp')
- grad_w_down: float32 [3072, 768], P('fsdp')
- grad_bias_down: float32 [768], P('fsdp')
- grad_gain_two: float32 [768], P('fsdp')
- grad_shift_two: float32 [768], P('fsdp')
Inputs may be any that keep to these rules, and one draw needn't show every extreme that they name: `lengths`: count of real tokens of each sequence; keys at later positions are padding that no query attends to; some sequence is full in every draw.
All inputs are finite; a program needn't handle non-finite values.
Results may differ from a plain program's by a relative error of at most 0.02.
The roundings to bfloat16 on the way count: a program that leaves them out, or rounds other values in their place, can miss the bound.
Values may be sent and summed in bfloat16 or wider, within the bound.
A program may use at most 192 MiB of HBM per device.

v0:
```python
import math

import jax
import jax.numpy as jnp
from jax import lax
from jax.sharding import PartitionSpec as P

HEADS = 12


EPSILON = 1e-12
MASKED = -1e30


def shifted(value, axis, steps):
    count = lax.axis_size(axis)
    pairs = [(source, (source + steps) % count) for source in range(count)]
    return lax.ppermute(value, axis, pairs)


def normalize(values, norm_gain, norm_shift):
    row_mean = jnp.mean(values, -1, keepdims=True)
    centred = values - row_mean
    spread = jnp.mean(centred * centred, -1, keepdims=True)
    return centred * lax.rsqrt(spread + EPSILON) * norm_gain + norm_shift


def gelu_exact(values):
    return jax.nn.gelu(values, approximate=False)


def row_dot(left_op, right_op):
    return jnp.dot(left_op, right_op, preferred_element_type=jnp.float32)


def left_dot(left_op, right_op):
    return lax.dot_general(
        left_op, right_op, (((0,), (0,)), ((), ())), preferred_element_type=jnp.float32
    )


def right_dot(left_op, right_op):
    return lax.dot_general(
        left_op, right_op, (((1,), (1,)), ((), ())), preferred_element_type=jnp.float32
    )


def body(
    tokens,
    cotangent,
    lengths,
    w_qkv,
    bias_q,
    bias_v,
    w_out,
    bias_out,
    gain_one,
    shift_one,
    w_up,
    bias_up,
    w_down,
    bias_down,
    gain_two,
    shift_two,
):
    seq_count, block_rows, model_width = tokens.shape
    head_count = HEADS
    head_dim = model_width // head_count
    all_rows = seq_count * block_rows
    score_scale = head_dim ** (-0.5)
    cycle_size = lax.axis_size("ctx")
    cycle_index = lax.axis_index("ctx")
    gathered = (
        lax.all_gather(w_qkv, "fsdp", axis=0, tiled=True),
        lax.all_gather(bias_q, "fsdp", axis=0, tiled=True),
        lax.all_gather(bias_v, "fsdp", axis=0, tiled=True),
        lax.all_gather(w_out, "fsdp", axis=0, tiled=True),
        lax.all_gather(bias_out, "fsdp", axis=0, tiled=True),
        lax.all_gather(gain_one, "fsdp", axis=0, tiled=True),
        lax.all_gather(shift_one, "fsdp", axis=0, tiled=True),
        lax.all_gather(w_up, "fsdp", axis=0, tiled=True),
        lax.all_gather(bias_up, "fsdp", axis=0, tiled=True),
        lax.all_gather(w_down, "fsdp", axis=0, tiled=True),
        lax.all_gather(bias_down, "fsdp", axis=0, tiled=True),
        lax.all_gather(gain_two, "fsdp", axis=0, tiled=True),
        lax.all_gather(shift_two, "fsdp", axis=0, tiled=True),
    )
    full_qkv, full_out, full_up, full_down = (gathered[0], gathered[3], gathered[7], gathered[9])
    add_q, add_v, add_out, scale_one, move_one, add_up, add_down, scale_two, move_two = [
        gathered[place].astype(jnp.float32) for place in (1, 2, 4, 5, 6, 8, 10, 11, 12)
    ]
    flat_tokens = tokens.reshape(all_rows, model_width)
    projected = row_dot(flat_tokens, full_qkv)
    queries = (
        (projected[:, :model_width] + add_q)
        .astype(jnp.bfloat16)
        .reshape(seq_count, block_rows, head_count, head_dim)
    )
    key_rows = (
        projected[:, model_width : 2 * model_width]
        .astype(jnp.bfloat16)
        .reshape(seq_count, block_rows, model_width)
    )
    value_rows = (
        (projected[:, 2 * model_width :] + add_v)
        .astype(jnp.bfloat16)
        .reshape(seq_count, block_rows, model_width)
    )
    start_state = (
        jnp.full((seq_count, block_rows, head_count), MASKED, jnp.float32),
        jnp.zeros((seq_count, block_rows, head_count), jnp.float32),
        jnp.zeros((seq_count, block_rows, head_count, head_dim), jnp.float32),
    )
    key_part = lax.all_gather(key_rows, "ctx", axis=1, tiled=True)
    value_part = lax.all_gather(value_rows, "ctx", axis=1, tiled=True)
    key_count = key_part.shape[1]
    sub_rows = math.gcd(key_count, 512)

    def visit(block_index, carried):
        first_key = block_index * sub_rows
        key_block = lax.dynamic_slice_in_dim(key_part, block_index * sub_rows, sub_rows, 1).reshape(
            seq_count, sub_rows, head_count, head_dim
        )
        value_block = lax.dynamic_slice_in_dim(
            value_part, block_index * sub_rows, sub_rows, 1
        ).reshape(seq_count, sub_rows, head_count, head_dim)
        peak, weight_sum, weighted = carried
        key_live = (
            (first_key + jnp.arange(sub_rows, dtype=jnp.int32))[None, :] < lengths[:, None]
        )[:, None, None, :]
        scores = (
            jnp.einsum("sqhe,skhe->sqhk", queries, key_block, preferred_element_type=jnp.float32)
            * score_scale
        )
        scores = jnp.where(key_live, scores, MASKED)
        new_peak = jnp.maximum(peak, jnp.max(scores, -1))
        factor = jnp.exp(peak - new_peak)
        weights = jnp.where(key_live, jnp.exp(scores - new_peak[..., None]), 0.0)
        mixed_values = jnp.einsum(
            "sqhk,skhe->sqhe",
            weights.astype(jnp.bfloat16),
            value_block,
            preferred_element_type=jnp.float32,
        )
        return (
            new_peak,
            weight_sum * factor + jnp.sum(weights, -1),
            weighted * factor[..., None] + mixed_values,
        )

    peak, weight_sum, weighted = lax.fori_loop(0, key_count // sub_rows, visit, start_state)
    log_total = peak + jnp.log(weight_sum)
    attended = weighted / weight_sum[..., None]
    attended_low = attended.astype(jnp.bfloat16).reshape(all_rows, model_width)
    first_sum = flat_tokens.astype(jnp.float32) + row_dot(attended_low, full_out) + add_out
    normed, norm_pull = jax.vjp(normalize, first_sum, scale_one, move_one)
    normed_low = normed.astype(jnp.bfloat16)
    hidden_pre = row_dot(normed_low, full_up) + add_up
    hidden_act, gelu_pull = jax.vjp(gelu_exact, hidden_pre)
    hidden_low = hidden_act.astype(jnp.bfloat16)
    second_sum = normed + row_dot(hidden_low, full_down) + add_down
    result, result_pull = jax.vjp(normalize, second_sum, scale_two, move_two)
    grad_second, grad_gain_two, grad_shift_two = result_pull(
        cotangent.reshape(all_rows, model_width).astype(jnp.float32)
    )
    down_low = grad_second.astype(jnp.bfloat16)
    grad_w_down = left_dot(hidden_low, down_low)
    grad_bias_down = jnp.sum(down_low.astype(jnp.float32), 0)
    (grad_pre,) = gelu_pull(right_dot(down_low, full_down))
    up_low = grad_pre.astype(jnp.bfloat16)
    grad_w_up = left_dot(normed_low, up_low)
    grad_bias_up = jnp.sum(up_low.astype(jnp.float32), 0)
    grad_first, grad_gain_one, grad_shift_one = norm_pull(grad_second + right_dot(up_low, full_up))
    branch_low = grad_first.astype(jnp.bfloat16)
    grad_w_out = left_dot(attended_low, branch_low)
    grad_bias_out = jnp.sum(branch_low.astype(jnp.float32), 0)
    grad_att = (
        right_dot(branch_low, full_out)
        .astype(jnp.bfloat16)
        .reshape(seq_count, block_rows, head_count, head_dim)
    )
    delta_rows = jnp.sum(grad_att.astype(jnp.float32) * attended, -1)

    def block_grads(query_part, grad_part, lse_part, delta_part, key_block, value_block, first_key):
        key_count = key_block.shape[1]
        key_heads = key_block.reshape(seq_count, key_count, head_count, head_dim)
        value_heads = value_block.reshape(seq_count, key_count, head_count, head_dim)
        key_live = (
            (first_key + jnp.arange(key_count, dtype=jnp.int32))[None, :] < lengths[:, None]
        )[:, None, None, :]
        scores = (
            jnp.einsum("sqhe,skhe->sqhk", query_part, key_heads, preferred_element_type=jnp.float32)
            * score_scale
        )
        chances = jnp.where(key_live, jnp.exp(scores - lse_part[..., None]), 0.0)
        grad_value = jnp.einsum(
            "sqhk,sqhe->skhe",
            chances.astype(jnp.bfloat16),
            grad_part,
            preferred_element_type=jnp.float32,
        )
        grad_chance = jnp.einsum(
            "sqhe,skhe->sqhk", grad_part, value_heads, preferred_element_type=jnp.float32
        )
        grad_score = (chances * (grad_chance - delta_part[..., None])).astype(jnp.bfloat16)
        grad_query = (
            jnp.einsum("sqhk,skhe->sqhe", grad_score, key_heads, preferred_element_type=jnp.float32)
            * score_scale
        )
        grad_key = (
            jnp.einsum(
                "sqhk,sqhe->skhe", grad_score, query_part, preferred_element_type=jnp.float32
            )
            * score_scale
        )
        return (
            grad_query,
            grad_key.reshape(seq_count, key_count, model_width),
            grad_value.reshape(seq_count, key_count, model_width),
        )

    query_start = jnp.zeros((seq_count, block_rows, head_count, head_dim), jnp.float32)

    def key_terms(key_block, value_block, first_key):
        return block_grads(
            queries, grad_att, log_total, delta_rows, key_block, value_block, first_key
        )

    def block_terms(key_block, value_block, first_key):
        return key_terms(key_block, value_block, first_key)

    def turn(step_index, carried):
        key_now, value_now, key_grads, query_acc = carried
        first_key = (cycle_index - step_index) % cycle_size * block_rows
        add_query, add_key, add_value = block_terms(key_now, value_now, first_key)
        key_now, value_now = shifted((key_now, value_now), "ctx", 1)
        key_grads = (
            shifted((key_grads[0] + add_key).astype(jnp.bfloat16), "ctx", 1).astype(jnp.float32),
            shifted((key_grads[1] + add_value).astype(jnp.bfloat16), "ctx", 1).astype(jnp.float32),
        )
        return (key_now, value_now, key_grads, query_acc + add_query)

    grad_start = (
        jnp.zeros((seq_count, block_rows, model_width), jnp.float32),
        jnp.zeros((seq_count, block_rows, model_width), jnp.float32),
    )
    key_final, value_final, key_grads, query_grad = lax.fori_loop(
        0, cycle_size, turn, (key_rows, value_rows, grad_start, query_start)
    )
    grad_key, grad_value = key_grads
    qkv_grad = jnp.concatenate(
        [
            query_grad.astype(jnp.bfloat16).reshape(all_rows, model_width),
            grad_key.astype(jnp.bfloat16).reshape(all_rows, model_width),
            grad_value.astype(jnp.bfloat16).reshape(all_rows, model_width),
        ],
        1,
    )
    grad_w_qkv = left_dot(flat_tokens, qkv_grad)
    grad_bias_q = jnp.sum(qkv_grad[:, :model_width].astype(jnp.float32), 0)
    grad_bias_v = jnp.sum(qkv_grad[:, 2 * model_width :].astype(jnp.float32), 0)
    grad_input = grad_first + right_dot(qkv_grad, full_qkv)
    gradients = (
        grad_w_qkv,
        grad_bias_q,
        grad_bias_v,
        grad_w_out,
        grad_bias_out,
        grad_gain_one,
        grad_shift_one,
        grad_w_up,
        grad_bias_up,
        grad_w_down,
        grad_bias_down,
        grad_gain_two,
        grad_shift_two,
    )
    shards = (
        lax.psum_scatter(
            gradients[0].astype(jnp.bfloat16), "fsdp", scatter_dimension=0, tiled=True
        ).astype(jnp.float32),
        lax.psum_scatter(
            gradients[1].astype(jnp.bfloat16), "fsdp", scatter_dimension=0, tiled=True
        ).astype(jnp.float32),
        lax.psum_scatter(
            gradients[2].astype(jnp.bfloat16), "fsdp", scatter_dimension=0, tiled=True
        ).astype(jnp.float32),
        lax.psum_scatter(
            gradients[3].astype(jnp.bfloat16), "fsdp", scatter_dimension=0, tiled=True
        ).astype(jnp.float32),
        lax.psum_scatter(
            gradients[4].astype(jnp.bfloat16), "fsdp", scatter_dimension=0, tiled=True
        ).astype(jnp.float32),
        lax.psum_scatter(
            gradients[5].astype(jnp.bfloat16), "fsdp", scatter_dimension=0, tiled=True
        ).astype(jnp.float32),
        lax.psum_scatter(
            gradients[6].astype(jnp.bfloat16), "fsdp", scatter_dimension=0, tiled=True
        ).astype(jnp.float32),
        lax.psum_scatter(
            gradients[7].astype(jnp.bfloat16), "fsdp", scatter_dimension=0, tiled=True
        ).astype(jnp.float32),
        lax.psum_scatter(
            gradients[8].astype(jnp.bfloat16), "fsdp", scatter_dimension=0, tiled=True
        ).astype(jnp.float32),
        lax.psum_scatter(
            gradients[9].astype(jnp.bfloat16), "fsdp", scatter_dimension=0, tiled=True
        ).astype(jnp.float32),
        lax.psum_scatter(
            gradients[10].astype(jnp.bfloat16), "fsdp", scatter_dimension=0, tiled=True
        ).astype(jnp.float32),
        lax.psum_scatter(
            gradients[11].astype(jnp.bfloat16), "fsdp", scatter_dimension=0, tiled=True
        ).astype(jnp.float32),
        lax.psum_scatter(
            gradients[12].astype(jnp.bfloat16), "fsdp", scatter_dimension=0, tiled=True
        ).astype(jnp.float32),
    )
    totals = lax.psum(
        (
            shards[0],
            shards[1],
            shards[2],
            shards[3],
            shards[4],
            shards[5],
            shards[6],
            shards[7],
            shards[8],
            shards[9],
            shards[10],
            shards[11],
            shards[12],
        ),
        ("dp", "ctx"),
    )
    output_rows = result.astype(jnp.bfloat16).reshape(seq_count, block_rows, model_width)
    input_rows = grad_input.astype(jnp.bfloat16).reshape(seq_count, block_rows, model_width)
    return (
        output_rows,
        input_rows,
        totals[0],
        totals[1],
        totals[2],
        totals[3],
        totals[4],
        totals[5],
        totals[6],
        totals[7],
        totals[8],
        totals[9],
        totals[10],
        totals[11],
        totals[12],
    )


def solution(mesh):
    return jax.shard_map(
        body,
        mesh=mesh,
        in_specs=(
            P(("dp", "fsdp"), "ctx", None),
            P(("dp", "fsdp"), "ctx", None),
            P(("dp", "fsdp")),
            P("fsdp", None),
            P("fsdp"),
            P("fsdp"),
            P("fsdp", None),
            P("fsdp"),
            P("fsdp"),
            P("fsdp"),
            P("fsdp", None),
            P("fsdp"),
            P("fsdp", None),
            P("fsdp"),
            P("fsdp"),
            P("fsdp"),
        ),
        out_specs=(
            P(("dp", "fsdp"), "ctx", None),
            P(("dp", "fsdp"), "ctx", None),
            P("fsdp", None),
            P("fsdp"),
            P("fsdp"),
            P("fsdp", None),
            P("fsdp"),
            P("fsdp"),
            P("fsdp"),
            P("fsdp", None),
            P("fsdp"),
            P("fsdp", None),
            P("fsdp"),
            P("fsdp"),
            P("fsdp"),
        ),
        check_vma=False,
    )
```

profile of v0, /device:TPU:5, one launch (start us, length us, event | category | flops | bytes accessed | tf_op | source)
XLA Modules:
  0.0 1023.7 jit_solution(98451317956871091)
XLA Ops:
  8.0 51.0 %all-gather.16.cloned.1.call-done = bf16[768,2304]{1,0:T(8,128)(2,1)} async-done(((bf16[384,2304]{1,0:T(8,128)(2,1)}), bf16[768,2304]{1,0:T(8,128)(2,1)}) %all-gather.16.cloned.1.call-update) | async-done | bytes 3538960 | tf_op jit(solution)/shard_map/all_gather | solution.py:74
  103.5 24.3 %all-gather.20.cloned.1.call-done = bf16[2,1024,768]{1,2,0:T(8,128)(2,1)} async-done(((bf16[2,256,768]{1,2,0:T(8,128)(2,1)}), bf16[2,1024,768]{1,2,0:T(8,128)(2,1)}) %all-gather.20.cloned.1.call-update) | async-done | bytes 3145744 | tf_op jit(solution)/shard_map/all_gather | solution.py:115
  127.8 45.6 %while.42 = (s32[]{:T(128)}, f32[2,256,12]{1,2,0:T(8,128)S(1)}, f32[2,256,12]{1,2,0:T(8,128)S(1)}, f32[2,256,12,64]{1,3,2,0:T(8,128)}, s32[2]{0:T(128)S(1)}, /*i...) while((s32[]{:T(128)}, f32[2,256,12]{1,2,0:T(8,128)S(1)}, ...), condition=%wide.region_3.4_spmd.clone, body=%wide.region_0.3_spmd.clone.sunk | while | flops 847412736 | bytes 101851360 | solution.py:151
  130.4 6.2 bitcast_reduce_fusion.2
  136.6 7.3 fusion.119
  157.5 7.9 fusion.119
  180.6 33.9 %all-gather.24.cloned.1.call-done = bf16[768,3072]{1,0:T(8,128)(2,1)} async-done(((bf16[384,3072]{1,0:T(8,128)(2,1)}), bf16[768,3072]{1,0:T(8,128)(2,1)}) %all-gather.24.cloned.1.call-update) | async-done | bytes 4718608 | tf_op jit(solution)/shard_map/all_gather | solution.py:81
  214.5 19.7 %multiply_convert_fusion = (bf16[512,3072]{1,0:T(8,128)(2,1)}, f32[512,3072]{1,0:T(8,128)}, f32[512,3072]{1,0:T(8,128)}) fusion(f32[3072]{0:T(1024)S(1)} %bitcast.180, bf16[768,3072]{1,0:T(8,128)(2,1)} %all-gather.24.cloned.1.call-done, f32[512,768]{1,0:T(8,128)S(1)} %get-tuple-element.715, f32[768]{0:T(1024)S(1)} %reshape.288, f32[768]{0:T(1024)S(1)} %reshape.287, ...), kind=kOutput, calls=%fused_computation.48 | convolution fusion | flops 2521694208 | bytes 22042624 | tf_op jit(solution)/shard_map/dot_general | solution.py:33
  234.2 44.3 %all-gather.26.cloned.1.call-done = bf16[3072,768]{1,0:T(8,128)(2,1)} async-done(((bf16[1536,768]{1,0:T(8,128)(2,1)}), bf16[3072,768]{1,0:T(8,128)(2,1)}) %all-gather.26.cloned.1.call-update) | async-done | bytes 4718608 | tf_op jit(solution)/shard_map/all_gather | solution.py:83
  278.6 6.1 fusion.59
  288.9 8.8 fusion.51
  313.5 202.6 %while.43 = (s32[]{:T(128)}, bf16[2,256,768]{1,2,0:T(8,128)(2,1)}, bf16[2,256,768]{1,2,0:T(8,128)(2,1)}, f32[2,256,768]{1,2,0:T(8,128)}, f32[2,256,768]{1,2,0:T(...) while((s32[]{:T(128)}, bf16[2,256,768]{1,2,0:T(8,128)(2,1)}, ...), condition=%wide.region_14.15_spmd.clone, body=%wide.region_13.14_spmd.clone.sunk | while | flops 1027080960 | bytes 90517592 | solution.py:247
  355.4 8.4 collective-permute-done.1
  406.1 8.4 collective-permute-done.1
  456.9 8.4 collective-permute-done.1
  507.6 8.4 collective-permute-done.1
  534.0 6.7 convolution_convert_fusion.1
  542.1 6.9 convolution_convert_fusion
  552.5 7.5 all-reduce.10
  560.4 6.1 add_convert_fusion.1
  566.5 15.1 %reduce-scatter.13.cloned.1.call-done = bf16[384,2304]{1,0:T(8,128)(2,1)} async-done(((bf16[768,2304]{1,0:T(8,128)(2,1)}), bf16[384,2304]{1,0:T(8,128)(2,1)}) %reduce-scatter.13.cloned.1.call-update) | async-done | bytes 1769488
  584.4 60.2 %reduce-scatter.9.cloned.1.call-done = bf16[384,3072]{1,0:T(8,128)(2,1)} async-done(((bf16[768,3072]{1,0:T(8,128)(2,1)}), bf16[384,3072]{1,0:T(8,128)(2,1)}) %reduce-scatter.9.cloned.1.call-update) | async-done | bytes 2359312 | tf_op jit(solution)/shard_map/reduce_scatter | solution.py:300
  644.6 62.8 %reduce-scatter.11.cloned.1.call-done = bf16[1536,768]{1,0:T(8,128)(2,1)} async-done(((bf16[3072,768]{1,0:T(8,128)(2,1)}), bf16[1536,768]{1,0:T(8,128)(2,1)}) %reduce-scatter.11.cloned.1.call-update) | async-done | bytes 2359312 | tf_op jit(solution)/shard_map/reduce_scatter | solution.py:306
  707.4 303.9 %all-reduce.12 = (f32[384,2304]{0,1:T(8,128)}, f32[384]{0:T(512)}, f32[384]{0:T(512)}, f32[384,768]{1,0:T(8,128)}, f32[384]{0:T(512)}, /*index=5*/f32[384]{0:T(5...) all-reduce(bf16[384,2304]{0,1:T(8,128)(2,1)S(1)} %copy.92, ...), channel_id=1, replica_groups=mesh['dp'=4,'ctx'=4,'fsdp'=2] {'dp','ctx'}, use_global_device_ids=true, to_apply=%region_16.17 | all-reduce | flops 3543552 | bytes 21270528 | tf_op jit(solution)/shard_map/psum | solution.py:319
  (347 shorter events, 293.8 us)
Async XLA Ops:
  7.2 51.8 %all-gather.16.cloned.1.call-start = ((), (), s32[]{:S(2)}) async-start(), calls=%async_computation.4 | async-start | bytes 5308416 | tf_op jit(solution)/shard_map/all_gather | solution.py:74
  7.9 95.5 %all-gather.18.cloned.1.call-start = ((), (), s32[]{:S(2)}) async-start(), calls=%async_computation.5 | async-start | bytes 3932160 | tf_op jit(solution)/shard_map/all_gather | solution.py:114
  66.7 61.1 %all-gather.20.cloned.1.call-start = ((), (), s32[]{:S(2)}) async-start(), calls=%async_computation.6 | async-start | bytes 3932160 | tf_op jit(solution)/shard_map/all_gather | solution.py:115
  76.8 101.0 %all-gather.22.cloned.1.call-start = ((), (), s32[]{:S(2)}) async-start(), calls=%async_computation.7 | async-start | bytes 1769472 | tf_op jit(solution)/shard_map/all_gather | solution.py:77
  77.4 137.1 %all-gather.24.cloned.1.call-start = ((), (), s32[]{:S(2)}) async-start(), calls=%async_computation.8 | async-start | bytes 7077888 | tf_op jit(solution)/shard_map/all_gather | solution.py:81
  78.0 200.5 %all-gather.26.cloned.1.call-start = ((), (), s32[]{:S(2)}) async-start(), calls=%async_computation.9 | async-start | bytes 7077888 | tf_op jit(solution)/shard_map/all_gather | solution.py:83
  78.6 487.9 %reduce-scatter.7.cloned.1.call-start = ((), (), s32[]{:S(2)}) async-start(), calls=%async_computation.10 | async-start | bytes 1769472 | tf_op jit(solution)/shard_map/reduce_scatter | solution.py:288
  313.4 268.2 %reduce-scatter.13.cloned.1.call-start = ((), (), s32[]{:S(2)}) async-start(), calls=%async_computation.13 | async-start | bytes 5308416
  331.9 15.1 %collective-permute-start.3 = (bf16[2,256,768]{1,2,0:T(8,128)(2,1)}, bf16[2,256,768]{1,2,0:T(8,128)(2,1)}, u32[]{:S(2)}, u32[]{:S(2)}) collective-permute-start(bf16[2,256,768]{1,2,0:T(8,128)(2,1)} %fusion.135), channel_id=1, source_target_pairs={{0,2},{2,4},{4,6},{6,0},{1,3},{3,5},{5,7},{7,1},{8,10},{10,12},{12... | collective-permute-start | bytes 2359304 | tf_op jit(solution)/shard_map/while/body/eval_jaxpr/ppermute | solution.py:18
  331.9 23.5 %collective-permute-start = (bf16[2,256,768]{1,2,0:T(8,128)(2,1)}, bf16[2,256,768]{1,2,0:T(8,128)(2,1)}, u32[]{:S(2)}, u32[]{:S(2)}) collective-permute-start(bf16[2,256,768]{1,2,0:T(8,128)(2,1)} %copy.117), channel_id=1, source_target_pairs={{0,2},{2,4},{4,6},{6,0},{1,3},{3,5},{5,7},{7,1},{8,10},{10,12},{12... | collective-permute-start | bytes 2359304 | tf_op jit(solution)/shard_map/while/body/eval_jaxpr/ppermute | solution.py:18
  332.4 31.5 %collective-permute-start.1 = (bf16[2,256,768]{1,2,0:T(8,128)(2,1)}, bf16[2,256,768]{1,2,0:T(8,128)(2,1)}, u32[]{:S(2)}, u32[]{:S(2)}) collective-permute-start(bf16[2,256,768]{1,2,0:T(8,128)(2,1)} %copy.118), channel_id=1, source_target_pairs={{0,2},{2,4},{4,6},{6,0},{1,3},{3,5},{5,7},{7,1},{8,10},{10,12},{12... | collective-permute-start | bytes 2359304 | tf_op jit(solution)/shard_map/while/body/eval_jaxpr/ppermute | solution.py:18
  382.7 15.1 %collective-permute-start.3 = (bf16[2,256,768]{1,2,0:T(8,128)(2,1)}, bf16[2,256,768]{1,2,0:T(8,128)(2,1)}, u32[]{:S(2)}, u32[]{:S(2)}) collective-permute-start(bf16[2,256,768]{1,2,0:T(8,128)(2,1)} %fusion.135), channel_id=1, source_target_pairs={{0,2},{2,4},{4,6},{6,0},{1,3},{3,5},{5,7},{7,1},{8,10},{10,12},{12... | collective-permute-start | bytes 2359304 | tf_op jit(solution)/shard_map/while/body/eval_jaxpr/ppermute | solution.py:18
  382.7 23.5 %collective-permute-start = (bf16[2,256,768]{1,2,0:T(8,128)(2,1)}, bf16[2,256,768]{1,2,0:T(8,128)(2,1)}, u32[]{:S(2)}, u32[]{:S(2)}) collective-permute-start(bf16[2,256,768]{1,2,0:T(8,128)(2,1)} %copy.117), channel_id=1, source_target_pairs={{0,2},{2,4},{4,6},{6,0},{1,3},{3,5},{5,7},{7,1},{8,10},{10,12},{12... | collective-permute-start | bytes 2359304 | tf_op jit(solution)/shard_map/while/body/eval_jaxpr/ppermute | solution.py:18
  383.1 31.5 %collective-permute-start.1 = (bf16[2,256,768]{1,2,0:T(8,128)(2,1)}, bf16[2,256,768]{1,2,0:T(8,128)(2,1)}, u32[]{:S(2)}, u32[]{:S(2)}) collective-permute-start(bf16[2,256,768]{1,2,0:T(8,128)(2,1)} %copy.118), channel_id=1, source_target_pairs={{0,2},{2,4},{4,6},{6,0},{1,3},{3,5},{5,7},{7,1},{8,10},{10,12},{12... | collective-permute-start | bytes 2359304 | tf_op jit(solution)/shard_map/while/body/eval_jaxpr/ppermute | solution.py:18
  428.3 11.7 %collective-permute-start.2 = (bf16[2,256,768]{1,2,0:T(8,128)(2,1)}, bf16[2,256,768]{1,2,0:T(8,128)(2,1)}, u32[]{:S(2)}, u32[]{:S(2)}) collective-permute-start(bf16[2,256,768]{1,2,0:T(8,128)(2,1)} %fusion.133), channel_id=1, source_target_pairs={{0,2},{2,4},{4,6},{6,0},{1,3},{3,5},{5,7},{7,1},{8,10},{10,12},{12... | collective-permute-start | bytes 2359304 | tf_op jit(solution)/shard_map/while/body/eval_jaxpr/ppermute | solution.py:18
  433.4 15.1 %collective-permute-start.3 = (bf16[2,256,768]{1,2,0:T(8,128)(2,1)}, bf16[2,256,768]{1,2,0:T(8,128)(2,1)}, u32[]{:S(2)}, u32[]{:S(2)}) collective-permute-start(bf16[2,256,768]{1,2,0:T(8,128)(2,1)} %fusion.135), channel_id=1, source_target_pairs={{0,2},{2,4},{4,6},{6,0},{1,3},{3,5},{5,7},{7,1},{8,10},{10,12},{12... | collective-permute-start | bytes 2359304 | tf_op jit(solution)/shard_map/while/body/eval_jaxpr/ppermute | solution.py:18
  433.4 23.5 %collective-permute-start = (bf16[2,256,768]{1,2,0:T(8,128)(2,1)}, bf16[2,256,768]{1,2,0:T(8,128)(2,1)}, u32[]{:S(2)}, u32[]{:S(2)}) collective-permute-start(bf16[2,256,768]{1,2,0:T(8,128)(2,1)} %copy.117), channel_id=1, source_target_pairs={{0,2},{2,4},{4,6},{6,0},{1,3},{3,5},{5,7},{7,1},{8,10},{10,12},{12... | collective-permute-start | bytes 2359304 | tf_op jit(solution)/shard_map/while/body/eval_jaxpr/ppermute | solution.py:18
  433.8 31.5 %collective-permute-start.1 = (bf16[2,256,768]{1,2,0:T(8,128)(2,1)}, bf16[2,256,768]{1,2,0:T(8,128)(2,1)}, u32[]{:S(2)}, u32[]{:S(2)}) collective-permute-start(bf16[2,256,768]{1,2,0:T(8,128)(2,1)} %copy.118), channel_id=1, source_target_pairs={{0,2},{2,4},{4,6},{6,0},{1,3},{3,5},{5,7},{7,1},{8,10},{10,12},{12... | collective-permute-start | bytes 2359304 | tf_op jit(solution)/shard_map/while/body/eval_jaxpr/ppermute | solution.py:18
  479.0 11.7 %collective-permute-start.2 = (bf16[2,256,768]{1,2,0:T(8,128)(2,1)}, bf16[2,256,768]{1,2,0:T(8,128)(2,1)}, u32[]{:S(2)}, u32[]{:S(2)}) collective-permute-start(bf16[2,256,768]{1,2,0:T(8,128)(2,1)} %fusion.133), channel_id=1, source_target_pairs={{0,2},{2,4},{4,6},{6,0},{1,3},{3,5},{5,7},{7,1},{8,10},{10,12},{12... | collective-permute-start | bytes 2359304 | tf_op jit(solution)/shard_map/while/body/eval_jaxpr/ppermute | solution.py:18
  484.1 15.1 %collective-permute-start.3 = (bf16[2,256,768]{1,2,0:T(8,128)(2,1)}, bf16[2,256,768]{1,2,0:T(8,128)(2,1)}, u32[]{:S(2)}, u32[]{:S(2)}) collective-permute-start(bf16[2,256,768]{1,2,0:T(8,128)(2,1)} %fusion.135), channel_id=1, source_target_pairs={{0,2},{2,4},{4,6},{6,0},{1,3},{3,5},{5,7},{7,1},{8,10},{10,12},{12... | collective-permute-start | bytes 2359304 | tf_op jit(solution)/shard_map/while/body/eval_jaxpr/ppermute | solution.py:18
  484.1 23.5 %collective-permute-start = (bf16[2,256,768]{1,2,0:T(8,128)(2,1)}, bf16[2,256,768]{1,2,0:T(8,128)(2,1)}, u32[]{:S(2)}, u32[]{:S(2)}) collective-permute-start(bf16[2,256,768]{1,2,0:T(8,128)(2,1)} %copy.117), channel_id=1, source_target_pairs={{0,2},{2,4},{4,6},{6,0},{1,3},{3,5},{5,7},{7,1},{8,10},{10,12},{12... | collective-permute-start | bytes 2359304 | tf_op jit(solution)/shard_map/while/body/eval_jaxpr/ppermute | solution.py:18
  484.6 31.5 %collective-permute-start.1 = (bf16[2,256,768]{1,2,0:T(8,128)(2,1)}, bf16[2,256,768]{1,2,0:T(8,128)(2,1)}, u32[]{:S(2)}, u32[]{:S(2)}) collective-permute-start(bf16[2,256,768]{1,2,0:T(8,128)(2,1)} %copy.118), channel_id=1, source_target_pairs={{0,2},{2,4},{4,6},{6,0},{1,3},{3,5},{5,7},{7,1},{8,10},{10,12},{12... | collective-permute-start | bytes 2359304 | tf_op jit(solution)/shard_map/while/body/eval_jaxpr/ppermute | solution.py:18
  532.7 111.9 %reduce-scatter.9.cloned.1.call-start = ((), (), s32[]{:S(2)}) async-start(), calls=%async_computation.11 | async-start | bytes 7077888 | tf_op jit(solution)/shard_map/reduce_scatter | solution.py:300
  540.8 166.7 %reduce-scatter.11.cloned.1.call-start = ((), (), s32[]{:S(2)}) async-start(), calls=%async_computation.12 | async-start | bytes 7077888 | tf_op jit(solution)/shard_map/reduce_scatter | solution.py:306
  (67 other events, 1037.3 us)
Sparse Core Ops, SparseCore 0:
  9.5 49.4 all-gather.15
  66.8 30.4 all-gather.17
  98.8 28.8 all-gather.19
  129.2 21.2 all-gather.21
  151.8 62.6 all-gather.23
  215.9 62.6 all-gather.25
  313.5 21.8 reduce-scatter.6
  532.8 48.7 reduce-scatter.12
  584.5 60.0 reduce-scatter.8
  647.3 60.0 reduce-scatter.10
where the time goes:
time: 1030 us; the launch traced here: 1020 us
  waiting for transfers between devices  388 us (38%)
  blocking collectives  341 us (33%)
  matrix products  143 us (14%)
  local copies, waits for them, and re-layouts  63.7 us (6%)
  other arithmetic  58.5 us (6%)
  between operations  16.6 us (2%)
  starting transfers between devices  11.8 us (1%)
    psum x1, blocking collectives, body(): lax.psum((shards[0], shards[1], shards[2], shards[3], shards[4], shards[5...  304 us
    ppermute x16, waiting for transfers between devices, shifted(): return lax.ppermute(value, axis, pairs)  93.4 us
    reduce_scatter x1, waiting for transfers between devices, body(): lax.psum_scatter(gradients[9].astype(jnp.bfloat16), 'fsdp', scatter_dimen...  62.8 us
    reduce_scatter x1, waiting for transfers between devices, body(): lax.psum_scatter(gradients[7].astype(jnp.bfloat16), 'fsdp', scatter_dimen...  60.2 us
    all_gather x1, waiting for transfers between devices, body(): lax.all_gather(w_qkv, 'fsdp', axis=0, tiled=True)  51 us
    all_gather x1, waiting for transfers between devices, body(): lax.all_gather(w_down, 'fsdp', axis=0, tiled=True)  44.3 us
    all_gather x1, waiting for transfers between devices, body(): lax.all_gather(w_up, 'fsdp', axis=0, tiled=True)  33.9 us
    dot_general x4, matrix products, row_dot(): return jnp.dot(left_op, right_op, preferred_element_type=jnp.float32)  32.5 us
  transfers between devices with their start and end apart: 26, of which 23 were waited for; matrix products, arithmetic and copies ran while one was open for 20% of the time, Pallas kernels for 0%

commit v1 on v0

--- a/solution.py
+++ b/solution.py
@@ -1,9 +1,301 @@
+import functools
 import math
 
 import jax
 import jax.numpy as jnp
 from jax import lax
+from jax.experimental import pallas as pl
+from jax.experimental.pallas import tpu as pltpu
 from jax.sharding import PartitionSpec as P
+
+MESH = pl.DeviceIdType.MESH
+F32, BF16 = jnp.float32, jnp.bfloat16
+U = 384
+VR = 24
+
+
+def places():
+    c = lax.axis_index("ctx")
+    return lax.rem(c, 2), c // 2, lax.axis_index("fsdp"), lax.axis_index("dp")
+
+
+def grad_kernel(nx, nd, grp, wd, wu, wo, wq, vec, od, ou, oo, oq, ov,
+                L, R1, R2, R3, R4, AX, AC, ST, V0, VX, VZ,
+                s0, s1s, s1r, s2s, s2r, s3s, s3r, s4s, s4r, s5s, s5r, s6s, s6r, s7s, s7r, so, vs, vr):
+    core, x, f, z = places()
+    nch = 12 // grp
+    CH, CX, PZ = U * grp, U * grp // nx, U * grp // nx // nd
+    sib = {"ctx": x * 2 + 1 - core}
+    yp = {"fsdp": 1 - f}
+    xps = [{"ctx": lax.rem(x + j, nx) * 2 + core} for j in range(1, nx)]
+    zps = [{"dp": lax.rem(z + j, nd)} for j in range(1, nd)]
+    peers = [sib, yp] + xps + zps
+    bar = pltpu.get_barrier_semaphore()
+    for p in peers:
+        pl.semaphore_signal(bar, inc=1, device_id=p, device_id_type=MESH)
+
+    def rect(i, ff, cc):
+        if i < 4:
+            return wd, ff * 1536 + i * U, cc * U
+        if i < 8:
+            return wu, ff * U, cc * 1536 + (i - 4) * U
+        if i < 9:
+            return wo, ff * U, cc * U
+        return wq, ff * U, cc * 1152 + (i - 9) * U
+
+    def orect(i, cc):
+        if i < 4:
+            return od, i * U, cc * U
+        if i < 8:
+            return ou, 0, cc * 1536 + (i - 4) * U
+        if i < 9:
+            return oo, 0, cc * U
+        return oq, 0, cc * 1152 + (i - 9) * U
+
+    def sl(ref, r, c):
+        return ref.at[pl.ds(pl.multiple_of(r, U), U), pl.ds(pl.multiple_of(c, 128), U)]
+
+    def local(i, k):
+        ff = (1 - f) if k == 0 else f
+        return pltpu.make_async_copy(sl(*rect(i, ff, core)), L.at[i // grp, ff, pl.ds(i % grp * U, U)], s0.at[i, k])
+
+    def remote(src, dst, ss, rs, dev):
+        return pltpu.make_async_remote_copy(src_ref=src, dst_ref=dst, send_sem=ss, recv_sem=rs, device_id=dev, device_id_type=MESH)
+
+    def c1(i, k):
+        ff = (1 - f) if k == 0 else f
+        return remote(sl(*rect(i, ff, 1 - core)), R1.at[i // grp, ff, pl.ds(i % grp * U, U)], s1s.at[i, k], s1r.at[i, k], sib)
+
+    def c2(c):
+        return remote(L.at[c, 1 - f], R2.at[c], s2s.at[c], s2r.at[c], yp)
+
+    def c3(c, j):
+        xt = lax.rem(x + j, nx)
+        return remote(L.at[c, f, pl.ds(pl.multiple_of(xt * CX, CX), CX)], R3.at[c, j - 1], s3s.at[c, j - 1], s3r.at[c, j - 1], xps[j - 1])
+
+    def mine(c, zz):
+        return pl.ds(pl.multiple_of(x * CX + zz * PZ, PZ), PZ)
+
+    def c4(c, j):
+        zt = lax.rem(z + j, nd)
+        return remote(L.at[c, f, mine(c, zt)], R4.at[c, j - 1], s4s.at[c, j - 1], s4r.at[c, j - 1], zps[j - 1])
+
+    def c5(c, j):
+        return remote(AX.at[c, mine(c, z)], AX.at[c, mine(c, z)], s5s.at[c, j - 1], s5r.at[c, j - 1], zps[j - 1])
+
+    def c6(c, j):
+        rows = pl.ds(pl.multiple_of(x * CX, CX), CX)
+        return remote(AX.at[c, rows], AX.at[c, rows], s6s.at[c, j - 1], s6r.at[c, j - 1], xps[j - 1])
+
+    def c7(c):
+        return remote(AX.at[c], AC.at[c], s7s.at[c], s7r.at[c], sib)
+
+    B = 48
+
+    def rows_loop(n, fn):
+        def bodyf(i, _):
+            fn(pl.multiple_of(i * B, B))
+            return 0
+        lax.fori_loop(0, n // B, bodyf, 0)
+
+    def up(v):
+        return v.astype(F32)
+
+    def st2(c):
+        for k in range(grp):
+            local(c * grp + k, 0).wait()
+            c1(c * grp + k, 0).wait_recv()
+
+        def fn(r):
+            s = pl.ds(r, B)
+            L[c, 1 - f, s, :] = (up(L[c, 1 - f, s, :]) + up(R1[c, 1 - f, s, :])).astype(BF16)
+        rows_loop(CH, fn)
+        c2(c).start()
+
+    def st3(c):
+        for k in range(grp):
+            local(c * grp + k, 1).wait()
+            c1(c * grp + k, 1).wait_recv()
+        c2(c).wait_recv()
+        for j in range(1, nx):
+            xt = lax.rem(x + j, nx)
+
+            def fn(r):
+                s = pl.ds(pl.multiple_of(xt * CX + r, B), B)
+                L[c, f, s, :] = (up(L[c, f, s, :]) + up(R1[c, f, s, :]) + up(R2[c, s, :])).astype(BF16)
+            rows_loop(CX, fn)
+            c3(c, j).start()
+
+    def st4(c):
+        for j in range(1, nx):
+            c3(c, j).wait_recv()
+
+        def fn(r):
+            s = pl.ds(pl.multiple_of(x * CX + r, B), B)
+            t = up(L[c, f, s, :]) + up(R1[c, f, s, :]) + up(R2[c, s, :])
+            for j in range(1, nx):
+                t = t + up(R3[c, j - 1, pl.ds(r, B), :])
+            L[c, f, s, :] = t.astype(BF16)
+        rows_loop(CX, fn)
+        for j in range(1, nd):
+            c4(c, j).start()
+
+    def st5(c):
+        for j in range(1, nd):
+            c4(c, j).wait_recv()
+        t = up(L[c, f, mine(c, z), :])
+        for j in range(1, nd):
+            t = t + up(R4[c, j - 1])
+        AX[c, mine(c, z), :] = t.astype(BF16)
+        for j in range(1, nd):
+            c5(c, j).start()
+
+    def st6(c):
+        for j in range(1, nd):
+            c5(c, j).wait_recv()
+        for j in range(1, nx):
+            c6(c, j).start()
+
+    def outc(i, k, slot):
+        cc = core if k == 0 else 1 - core
+        return pltpu.make_async_copy(ST.at[slot], sl(*orect(i, cc)), so.at[slot])
+
+    def emit(i, k, src):
+        slot = emit.n % 4
+        if emit.n >= 4:
+            outc(*emit.log[emit.n - 4], slot).wait()
+        off = i % grp * U
+
+        def fn(r):
+            ST[slot, pl.ds(r, B), :] = up(src[i // grp, pl.ds(pl.multiple_of(off + r, B), B), :])
+        rows_loop(U, fn)
+        outc(i, k, slot).start()
+        emit.log.append((i, k))
+        emit.n += 1
+    emit.n = 0
+    emit.log = []
+
+    def st7(c):
+        for j in range(1, nx):
+            c6(c, j).wait_recv()
+        c7(c).start()
+        for k in range(grp):
+            emit(c * grp + k, 0, AX)
+
+    def st8(c):
+        c7(c).wait_recv()
+        for k in range(grp):
+            emit(c * grp + k, 1, AC)
+
+    def v_core():
+        return remote(vec, V0.at[0], vs.at[0], vr.at[0], sib)
+
+    def v_y():
+        return remote(V0.at[1], V0.at[2], vs.at[1], vr.at[1], yp)
+
+    def v_x(j):
+        return remote(VX.at[x], VX.at[x], vs.at[1 + j], vr.at[1 + j], xps[j - 1])
+
+    def v_z(j):
+        return remote(VZ.at[z], VZ.at[z], vs.at[nx + j], vr.at[nx + j], zps[j - 1])
+
+    def vst(k):
+        if k == 0:
+            v_core().start()
+        elif k == 1:
+            v_core().wait_recv()
+            V0[1] = vec[...] + V0[0]
+            v_y().start()
+        elif k == 2:
+            v_y().wait_recv()
+            VX[x] = V0[1] + V0[2]
+            for j in range(1, nx):
+                v_x(j).start()
+        elif k == 3:
+            for j in range(1, nx):
+                v_x(j).wait_recv()
+            t = VX[0]
+            for j in range(1, nx):
+                t = t + VX[j]
+            VZ[z] = t
+            for j in range(1, nd):
+                v_z(j).start()
+        elif k == 4:
+            for j in range(1, nd):
+                v_z(j).wait_recv()
+            t = VZ[0]
+            for j in range(1, nd):
+                t = t + VZ[j]
+            ov[...] = t
+
+    for i in range(12):
+        local(i, 0).start()
+    pl.semaphore_wait(bar, len(peers))
+    for i in range(12):
+        c1(i, 0).start()
+    vst(0)
+    for i in range(12):
+        local(i, 1).start()
+        c1(i, 1).start()
+    stages = [(8, st8), (7, st7), (6, st6), (5, st5), (4, st4), (3, st3)]
+    for t in range(nch + 8):
+        if t < nch:
+            st2(t)
+        if 1 <= t <= 4:
+            vst(t)
+        for k, fn in stages:
+            c = t - (k - 1)
+            if 0 <= c < nch:
+                fn(c)
+    n = emit.n
+    for q in range(max(0, n - 4), n):
+        outc(*emit.log[q], q % 4).wait()
+    for i in range(12):
+        for k in range(2):
+            c1(i, k).wait_send()
+    for c in range(nch):
+        c2(c).wait_send()
+        c7(c).wait_send()
+        for j in range(1, nx):
+            c3(c, j).wait_send()
+            c6(c, j).wait_send()
+        for j in range(1, nd):
+            c4(c, j).wait_send()
+            c5(c, j).wait_send()
+    v_core().wait_send()
+    v_y().wait_send()
+    for j in range(1, nx):
+        v_x(j).wait_send()
+    for j in range(1, nd):
+        v_z(j).wait_send()
+
+
+def grad_reduce(wd, wu, wo, wq, vec, nx, nd, cid):
+    grp = nx * nd // 8
+    nch = 12 // grp
+    CH, CX, PZ = U * grp, U * grp // nx, U * grp // nx // nd
+    anyspec = pl.BlockSpec(memory_space=pl.ANY)
+    vspec = pl.BlockSpec(memory_space=pltpu.VMEM)
+    D = pltpu.SemaphoreType.DMA
+    V = pltpu.VMEM
+    sems = [D((12, 2)), D((12, 2)), D((12, 2)), D((nch,)), D((nch,)), D((nch, nx - 1)), D((nch, nx - 1)),
+            D((nch, nd - 1)), D((nch, nd - 1)), D((nch, nd - 1)), D((nch, nd - 1)), D((nch, nx - 1)), D((nch, nx - 1)),
+            D((nch,)), D((nch,)), D((4,)), D((nx + nd,)), D((nx + nd,))]
+    return pl.pallas_call(
+        functools.partial(grad_kernel, nx, nd, grp),
+        out_shape=(jax.ShapeDtypeStruct((1536, 768), F32), jax.ShapeDtypeStruct((U, 3072), F32),
+                   jax.ShapeDtypeStruct((U, 768), F32), jax.ShapeDtypeStruct((U, 2304), F32),
+                   jax.ShapeDtypeStruct((VR, U), F32)),
+        in_specs=[anyspec] * 4 + [vspec],
+        out_specs=(anyspec,) * 4 + (vspec,),
+        scratch_shapes=[V((nch, 2, CH, U), BF16), V((nch, 2, CH, U), BF16), V((nch, CH, U), BF16),
+                        V((nch, nx - 1, CX, U), BF16), V((nch, nd - 1, PZ, U), BF16),
+                        V((nch, CH, U), BF16), V((nch, CH, U), BF16), V((4, U, U), F32),
+                        V((3, VR, U), F32), V((nx, VR, U), F32), V((nd, VR, U), F32)] + sems,
+        compiler_params=pltpu.CompilerParams(collective_id=cid, has_side_effects=True, vmem_limit_bytes=60 << 20),
+        name="grad_reduce",
+    )(wd, wu, wo, wq, vec)
+
 
 HEADS = 12
 
@@ -260,79 +552,38 @@
     grad_bias_q = jnp.sum(qkv_grad[:, :model_width].astype(jnp.float32), 0)
     grad_bias_v = jnp.sum(qkv_grad[:, 2 * model_width :].astype(jnp.float32), 0)
     grad_input = grad_first + right_dot(qkv_grad, full_qkv)
-    gradients = (
-        grad_w_qkv,
+    vectors = (
         grad_bias_q,
         grad_bias_v,
-        grad_w_out,
         grad_bias_out,
         grad_gain_one,
         grad_shift_one,
-        grad_w_up,
         grad_bias_up,
-        grad_w_down,
         grad_bias_down,
         grad_gain_two,
         grad_shift_two,
     )
-    shards = (
-        lax.psum_scatter(
-            gradients[0].astype(jnp.bfloat16), "fsdp", scatter_dimension=0, tiled=True
-        ).astype(jnp.float32),
-        lax.psum_scatter(
-            gradients[1].astype(jnp.bfloat16), "fsdp", scatter_dimension=0, tiled=True
-        ).astype(jnp.float32),
-        lax.psum_scatter(
-            gradients[2].astype(jnp.bfloat16), "fsdp", scatter_dimension=0, tiled=True
-        ).astype(jnp.float32),
-        lax.psum_scatter(
-            gradients[3].astype(jnp.bfloat16), "fsdp", scatter_dimension=0, tiled=True
-        ).astype(jnp.float32),
-        lax.psum_scatter(
-            gradients[4].astype(jnp.bfloat16), "fsdp", scatter_dimension=0, tiled=True
-        ).astype(jnp.float32),
-        lax.psum_scatter(
-            gradients[5].astype(jnp.bfloat16), "fsdp", scatter_dimension=0, tiled=True
-        ).astype(jnp.float32),
-        lax.psum_scatter(
-            gradients[6].astype(jnp.bfloat16), "fsdp", scatter_dimension=0, tiled=True
-        ).astype(jnp.float32),
-        lax.psum_scatter(
-            gradients[7].astype(jnp.bfloat16), "fsdp", scatter_dimension=0, tiled=True
-        ).astype(jnp.float32),
-        lax.psum_scatter(
-            gradients[8].astype(jnp.bfloat16), "fsdp", scatter_dimension=0, tiled=True
-        ).astype(jnp.float32),
-        lax.psum_scatter(
-            gradients[9].astype(jnp.bfloat16), "fsdp", scatter_dimension=0, tiled=True
-        ).astype(jnp.float32),
-        lax.psum_scatter(
-            gradients[10].astype(jnp.bfloat16), "fsdp", scatter_dimension=0, tiled=True
-        ).astype(jnp.float32),
-        lax.psum_scatter(
-            gradients[11].astype(jnp.bfloat16), "fsdp", scatter_dimension=0, tiled=True
-        ).astype(jnp.float32),
-        lax.psum_scatter(
-            gradients[12].astype(jnp.bfloat16), "fsdp", scatter_dimension=0, tiled=True
-        ).astype(jnp.float32),
-    )
-    totals = lax.psum(
-        (
-            shards[0],
-            shards[1],
-            shards[2],
-            shards[3],
-            shards[4],
-            shards[5],
-            shards[6],
-            shards[7],
-            shards[8],
-            shards[9],
-            shards[10],
-            shards[11],
-            shards[12],
-        ),
-        ("dp", "ctx"),
+    packed = jnp.concatenate(vectors).reshape(VR, U)
+    t_down, t_up, t_out, t_qkv, t_vec = grad_reduce(
+        grad_w_down.astype(BF16),
+        grad_w_up.astype(BF16),
+        grad_w_out.astype(BF16),
+        grad_w_qkv.astype(BF16),
+        packed,
+        cycle_size // 2,
+        lax.axis_size("dp"),
+        1,
+    )
+    flat = t_vec.reshape(-1)
+    own = lax.axis_index("fsdp")
+    parts, start = [], 0
+    for vector in vectors:
+        half = vector.shape[0] // 2
+        parts.append(lax.dynamic_slice_in_dim(flat, start + own * half, half, 0))
+        start += 2 * half
+    totals = (
+        t_qkv, parts[0], parts[1], t_out, parts[2], parts[3], parts[4],
+        t_up, parts[5], t_down, parts[6], parts[7], parts[8],
     )
     output_rows = result.astype(jnp.bfloat16).reshape(seq_count, block_rows, model_width)
     input_rows = grad_input.astype(jnp.bfloat16).reshape(seq_count, block_rows, model_width)

time: 1030 us -> 698 us (0.68)
  blocking collectives: 341 us -> 30.1 us
  waiting for transfers between devices: 388 us -> 247 us
  Pallas kernels: 0 us -> 133 us
    psum x1 -> x0, blocking collectives: 304 us -> none  [body(): lax.psum((shards[0], shards[1], shards[2], shards[3], shards[4], shards[5...]
    pallas_call x0 -> x1, Pallas kernels: none -> 133 us  [grad_reduce(): pl.pallas_call(functools.partial(grad_kernel, nx, nd, grp), out_shape=(ja...]
    reduce_scatter x3 -> x0, waiting for transfers between devices: 123 us -> none  [the longest x1 62.8 us: body(): lax.psum_scatter(gradients[9].astype(jnp.bfloat16), 'fsdp', scatter_dimen...]
    unnamed x11 -> x6, waiting for transfers between devices: 17.5 us -> 2.29 us
    unnamed x105 -> x94, local copies, waits for them, and re-layouts: 22.1 us -> 14.5 us
  transfers between devices with their start and end apart: 26 -> 22, of which waited for: 23 -> 20; matrix products, arithmetic and copies ran while one was open for 20% -> 17% of each run, Pallas kernels for 0% -> 0%
where the time goes in v1:
time: 698 us; the launch traced here: 692 us
  waiting for transfers between devices  247 us (35%)
  matrix products  138 us (20%)
  Pallas kernels  133 us (19%)
  local copies, waits for them, and re-layouts  58.1 us (8%)
  other arithmetic  58.1 us (8%)
  blocking collectives  30.1 us (4%)
  between operations  15 us (2%)
  starting transfers between devices  11.5 us (2%)
    pallas_call x1, Pallas kernels, grad_reduce(): pl.pallas_call(functools.partial(grad_kernel, nx, nd, grp), out_shape=(ja...  133 us
    ppermute x16, waiting for transfers between devices, shifted(): return lax.ppermute(value, axis, pairs)  93.3 us
    all_gather x1, waiting for transfers between devices, body(): lax.all_gather(w_qkv, 'fsdp', axis=0, tiled=True)  51 us
    all_gather x1, waiting for transfers between devices, body(): lax.all_gather(w_down, 'fsdp', axis=0, tiled=True)  44 us
    all_gather x1, waiting for transfers between devices, body(): lax.all_gather(w_up, 'fsdp', axis=0, tiled=True)  33.1 us
    dot_general x4, matrix products, row_dot(): return jnp.dot(left_op, right_op, preferred_element_type=jnp.float32)  33 us
    all_gather x1, waiting for transfers between devices, body(): value_part = lax.all_gather(value_rows, 'ctx', axis=1, tiled=True)  23.6 us
    while x54, local copies, waits for them, and re-layouts  21.8 us
  transfers between devices with their start and end apart: 22, of which 20 were waited for; matrix products, arithmetic and copies ran while one was open for 17% of the time, Pallas kernels for 0%

profile of v1, /device:TPU:5, one launch (start us, length us, event | category | flops | bytes accessed | tf_op | source)
XLA Modules:
  0.0 692.3 jit_solution(4279257037707614042)
XLA Ops:
  8.0 51.0 %all-gather.16.cloned.1.call-done = bf16[768,2304]{1,0:T(8,128)(2,1)} async-done(((bf16[384,2304]{1,0:T(8,128)(2,1)}), bf16[768,2304]{1,0:T(8,128)(2,1)}) %all-gather.16.cloned.1.call-update) | async-done | bytes 3538960 | tf_op jit(solution)/shard_map/all_gather | solution.py:366
  104.2 23.6 %all-gather.20.cloned.1.call-done = bf16[2,1024,768]{1,2,0:T(8,128)(2,1)} async-done(((bf16[2,256,768]{1,2,0:T(8,128)(2,1)}), bf16[2,1024,768]{1,2,0:T(8,128)(2,1)}) %all-gather.20.cloned.1.call-update) | async-done | bytes 3145744 | tf_op jit(solution)/shard_map/all_gather | solution.py:407
  127.8 45.4 %while.42 = (s32[]{:T(128)}, f32[2,256,12]{1,2,0:T(8,128)S(1)}, f32[2,256,12]{1,2,0:T(8,128)S(1)}, f32[2,256,12,64]{1,3,2,0:T(8,128)}, s32[2]{0:T(128)S(1)}, /*i...) while((s32[]{:T(128)}, f32[2,256,12]{1,2,0:T(8,128)S(1)}, ...), condition=%wide.region_3.4_spmd.clone, body=%wide.region_0.3_spmd.clone.sunk | while | flops 847412736 | bytes 101851360 | solution.py:443
  130.2 6.2 bitcast_reduce_fusion.2
  136.4 7.3 %fusion.116 = f32[2,256,12]{1,2,0:T(8,128)S(1)} fusion(f32[2,12,512,256]{3,2,1,0:T(8,128)} %get-tuple-element.789, f32[2,256,12]{1,2,0:T(8,128)S(1)} %select_maximum_fusion.2, pred[2,512]{1,0:T(4,128)(4,1)S(1)} %broadcast_compare_fusion.4), kind=kLoop, calls=%fused_computation.6.clone.1 | loop fusion | flops 15722496 | bytes 12633088 | tf_op jit(solution)/shard_map/while/body/eval_jaxpr/reduce_sum | solution.py:439
  151.2 6.0 bitcast_reduce_fusion.2
  157.3 7.8 %fusion.116 = f32[2,256,12]{1,2,0:T(8,128)S(1)} fusion(f32[2,12,512,256]{3,2,1,0:T(8,128)} %get-tuple-element.789, f32[2,256,12]{1,2,0:T(8,128)S(1)} %select_maximum_fusion.2, pred[2,512]{1,0:T(4,128)(4,1)S(1)} %broadcast_compare_fusion.4), kind=kLoop, calls=%fused_computation.6.clone.1 | loop fusion | flops 15722496 | bytes 12633088 | tf_op jit(solution)/shard_map/while/body/eval_jaxpr/reduce_sum | solution.py:439
  181.4 33.1 %all-gather.24.cloned.1.call-done = bf16[768,3072]{1,0:T(8,128)(2,1)} async-done(((bf16[384,3072]{1,0:T(8,128)(2,1)}), bf16[768,3072]{1,0:T(8,128)(2,1)}) %all-gather.24.cloned.1.call-update) | async-done | bytes 4718608 | tf_op jit(solution)/shard_map/all_gather | solution.py:373
  214.5 20.0 %multiply_convert_fusion = (bf16[512,3072]{1,0:T(8,128)(2,1)}, f32[512,3072]{1,0:T(8,128)}, f32[512,3072]{1,0:T(8,128)}) fusion(f32[3072]{0:T(1024)S(1)} %bitcast.190, bf16[768,3072]{1,0:T(8,128)(2,1)} %all-gather.24.cloned.1.call-done, f32[512,768]{1,0:T(8,128)S(1)} %get-tuple-element.666, f32[768]{0:T(1024)S(1)} %reshape.296, f32[768]{0:T(1024)S(1)} %reshape.295, ...), kind=kOutput, calls=%fused_computation.49 | convolution fusion | flops 2521694208 | bytes 22042624 | tf_op jit(solution)/shard_map/dot_general | solution.py:325
  234.6 44.0 %all-gather.26.cloned.1.call-done = bf16[3072,768]{1,0:T(8,128)(2,1)} async-done(((bf16[1536,768]{1,0:T(8,128)(2,1)}), bf16[3072,768]{1,0:T(8,128)(2,1)}) %all-gather.26.cloned.1.call-update) | async-done | bytes 4718608 | tf_op jit(solution)/shard_map/all_gather | solution.py:375
  278.6 6.0 fusion.56
  292.2 7.7 %convert_reduce_fusion = (f32[3072]{0:T(1024)S(1)}, bf16[512,3072]{1,0:T(8,128)(2,1)S(1)}) fusion(f32[512,3072]{1,0:T(8,128)} %get-tuple-element.647, f32[512,3072]{1,0:T(8,128)} %get-tuple-element.667, f32[3072]{0:T(1024)S(1)} %bitcast.191, bf16[512,768]{1,0:T(8,128)(2,1)S(1)} %get-tuple-element.635, bf16[3072,768]{1,0:T(8,128)(2,1)S(1)} %bitcast.195), kind=kOutput, calls=%fused_computation.47 | convolution fusion | flops 2442654720 | bytes 21258240 | tf_op jit(solution)/shard_map/dot_general | solution.py:335
  316.8 202.8 %while.43 = (s32[]{:T(128)}, bf16[2,256,768]{1,2,0:T(8,128)(2,1)}, bf16[2,256,768]{1,2,0:T(8,128)(2,1)}, f32[2,256,768]{1,2,0:T(8,128)}, f32[2,256,768]{1,2,0:T(...) while((s32[]{:T(128)}, bf16[2,256,768]{1,2,0:T(8,128)(2,1)}, ...), condition=%wide.region_14.15_spmd.clone, body=%wide.region_13.14_spmd.clone.sunk | while | flops 1027080960 | bytes 90517592 | solution.py:539
  344.4 6.0 collective-permute-done.3
  352.8 6.0 collective-permute-done
  358.9 8.4 %collective-permute-done.1 = bf16[2,256,768]{1,2,0:T(8,128)(2,1)} collective-permute-done((bf16[2,256,768]{1,2,0:T(8,128)(2,1)}, bf16[2,256,768]{1,2,0:T(8,128)(2,1)}, u32[]{:S(2)}, u32[]{:S(2)}) %collective-permute-start.1) | collective-permute-done | bytes 786464 | tf_op jit(solution)/shard_map/while/body/eval_jaxpr/ppermute | solution.py:310
  395.2 6.0 collective-permute-done.3
  403.6 6.0 collective-permute-done
  409.7 8.4 %collective-permute-done.1 = bf16[2,256,768]{1,2,0:T(8,128)(2,1)} collective-permute-done((bf16[2,256,768]{1,2,0:T(8,128)(2,1)}, bf16[2,256,768]{1,2,0:T(8,128)(2,1)}, u32[]{:S(2)}, u32[]{:S(2)}) %collective-permute-start.1) | collective-permute-done | bytes 786464 | tf_op jit(solution)/shard_map/while/body/eval_jaxpr/ppermute | solution.py:310
  454.4 6.0 collective-permute-done
  460.4 8.4 %collective-permute-done.1 = bf16[2,256,768]{1,2,0:T(8,128)(2,1)} collective-permute-done((bf16[2,256,768]{1,2,0:T(8,128)(2,1)}, bf16[2,256,768]{1,2,0:T(8,128)(2,1)}, u32[]{:S(2)}, u32[]{:S(2)}) %collective-permute-start.1) | collective-permute-done | bytes 786464 | tf_op jit(solution)/shard_map/while/body/eval_jaxpr/ppermute | solution.py:310
  505.2 6.0 collective-permute-done
  511.2 8.4 %collective-permute-done.1 = bf16[2,256,768]{1,2,0:T(8,128)(2,1)} collective-permute-done((bf16[2,256,768]{1,2,0:T(8,128)(2,1)}, bf16[2,256,768]{1,2,0:T(8,128)(2,1)}, u32[]{:S(2)}, u32[]{:S(2)}) %collective-permute-start.1) | collective-permute-done | bytes 786464 | tf_op jit(solution)/shard_map/while/body/eval_jaxpr/ppermute | solution.py:310
  535.7 132.8 %grad_reduce.1 = (f32[1536,768]{1,0:T(8,128)}, f32[384,3072]{1,0:T(8,128)}, f32[384,768]{1,0:T(8,128)}, f32[384,2304]{1,0:T(8,128)}, f32[24,384]{1,0:T(8,128)}) custom-call(bf16[3072,768]{1,0:T(8,128)(2,1)} %convolution_convert_fusion.2.wd, bf16[768,3072]{1,0:T(8,128)(2,1)} %convolution_convert_fusion.1.wu, bf16[768,768]{1,0:T(8,128)(2,1)} %convolution_convert_fusion.3.wo, ...), custom_call_target="tpu_custom_call" | custom-call | tf_op jit(solution)/shard_map/grad_reduce/pallas_call | solution.py:284
  (327 shorter events, 261.0 us)
Async XLA Ops:
  7.2 51.8 %all-gather.16.cloned.1.call-start = ((), (), s32[]{:S(2)}) async-start(), calls=%async_computation | async-start | bytes 5308416 | tf_op jit(solution)/shard_map/all_gather | solution.py:366
  7.9 96.3 %all-gather.18.cloned.1.call-start = ((), (), s32[]{:S(2)}) async-start(), calls=%async_computation.1 | async-start | bytes 3932160 | tf_op jit(solution)/shard_map/all_gather | solution.py:406
  66.7 61.1 %all-gather.20.cloned.1.call-start = ((), (), s32[]{:S(2)}) async-start(), calls=%async_computation.2 | async-start | bytes 3932160 | tf_op jit(solution)/shard_map/all_gather | solution.py:407
  76.9 101.6 %all-gather.22.cloned.1.call-start = ((), (), s32[]{:S(2)}) async-start(), calls=%async_computation.3 | async-start | bytes 1769472 | tf_op jit(solution)/shard_map/all_gather | solution.py:369
  77.4 137.1 %all-gather.24.cloned.1.call-start = ((), (), s32[]{:S(2)}) async-start(), calls=%async_computation.4 | async-start | bytes 7077888 | tf_op jit(solution)/shard_map/all_gather | solution.py:373
  78.0 200.5 %all-gather.26.cloned.1.call-start = ((), (), s32[]{:S(2)}) async-start(), calls=%async_computation.5 | async-start | bytes 7077888 | tf_op jit(solution)/shard_map/all_gather | solution.py:375
  78.6 49.2 %copy-start.18 = (s32[2]{0:T(128)S(1)}, s32[2]{0:T(128)}, u32[]{:S(2)}) copy-start(s32[2]{0:T(128)} %param.22) | copy-start | bytes 28
  330.8 11.2 %collective-permute-start.2 = (bf16[2,256,768]{1,2,0:T(8,128)(2,1)}, bf16[2,256,768]{1,2,0:T(8,128)(2,1)}, u32[]{:S(2)}, u32[]{:S(2)}) collective-permute-start(bf16[2,256,768]{1,2,0:T(8,128)(2,1)} %fusion.130), channel_id=1, source_target_pairs={{0,2},{2,4},{4,6},{6,0},{1,3},{3,5},{5,7},{7,1},{8,10},{10,12},{12... | collective-permute-start | bytes 2359304 | tf_op jit(solution)/shard_map/while/body/eval_jaxpr/ppermute | solution.py:310
  335.4 15.1 %collective-permute-start.3 = (bf16[2,256,768]{1,2,0:T(8,128)(2,1)}, bf16[2,256,768]{1,2,0:T(8,128)(2,1)}, u32[]{:S(2)}, u32[]{:S(2)}) collective-permute-start(bf16[2,256,768]{1,2,0:T(8,128)(2,1)} %fusion.132), channel_id=1, source_target_pairs={{0,2},{2,4},{4,6},{6,0},{1,3},{3,5},{5,7},{7,1},{8,10},{10,12},{12... | collective-permute-start | bytes 2359304 | tf_op jit(solution)/shard_map/while/body/eval_jaxpr/ppermute | solution.py:310
  335.4 23.5 %collective-permute-start = (bf16[2,256,768]{1,2,0:T(8,128)(2,1)}, bf16[2,256,768]{1,2,0:T(8,128)(2,1)}, u32[]{:S(2)}, u32[]{:S(2)}) collective-permute-start(bf16[2,256,768]{1,2,0:T(8,128)(2,1)} %copy.115), channel_id=1, source_target_pairs={{0,2},{2,4},{4,6},{6,0},{1,3},{3,5},{5,7},{7,1},{8,10},{10,12},{12... | collective-permute-start | bytes 2359304 | tf_op jit(solution)/shard_map/while/body/eval_jaxpr/ppermute | solution.py:310
  335.8 31.5 %collective-permute-start.1 = (bf16[2,256,768]{1,2,0:T(8,128)(2,1)}, bf16[2,256,768]{1,2,0:T(8,128)(2,1)}, u32[]{:S(2)}, u32[]{:S(2)}) collective-permute-start(bf16[2,256,768]{1,2,0:T(8,128)(2,1)} %copy.116), channel_id=1, source_target_pairs={{0,2},{2,4},{4,6},{6,0},{1,3},{3,5},{5,7},{7,1},{8,10},{10,12},{12... | collective-permute-start | bytes 2359304 | tf_op jit(solution)/shard_map/while/body/eval_jaxpr/ppermute | solution.py:310
  381.1 11.7 %collective-permute-start.2 = (bf16[2,256,768]{1,2,0:T(8,128)(2,1)}, bf16[2,256,768]{1,2,0:T(8,128)(2,1)}, u32[]{:S(2)}, u32[]{:S(2)}) collective-permute-start(bf16[2,256,768]{1,2,0:T(8,128)(2,1)} %fusion.130), channel_id=1, source_target_pairs={{0,2},{2,4},{4,6},{6,0},{1,3},{3,5},{5,7},{7,1},{8,10},{10,12},{12... | collective-permute-start | bytes 2359304 | tf_op jit(solution)/shard_map/while/body/eval_jaxpr/ppermute | solution.py:310
  386.2 15.1 %collective-permute-start.3 = (bf16[2,256,768]{1,2,0:T(8,128)(2,1)}, bf16[2,256,768]{1,2,0:T(8,128)(2,1)}, u32[]{:S(2)}, u32[]{:S(2)}) collective-permute-start(bf16[2,256,768]{1,2,0:T(8,128)(2,1)} %fusion.132), channel_id=1, source_target_pairs={{0,2},{2,4},{4,6},{6,0},{1,3},{3,5},{5,7},{7,1},{8,10},{10,12},{12... | collective-permute-start | bytes 2359304 | tf_op jit(solution)/shard_map/while/body/eval_jaxpr/ppermute | solution.py:310
  386.2 23.5 %collective-permute-start = (bf16[2,256,768]{1,2,0:T(8,128)(2,1)}, bf16[2,256,768]{1,2,0:T(8,128)(2,1)}, u32[]{:S(2)}, u32[]{:S(2)}) collective-permute-start(bf16[2,256,768]{1,2,0:T(8,128)(2,1)} %copy.115), channel_id=1, source_target_pairs={{0,2},{2,4},{4,6},{6,0},{1,3},{3,5},{5,7},{7,1},{8,10},{10,12},{12... | collective-permute-start | bytes 2359304 | tf_op jit(solution)/shard_map/while/body/eval_jaxpr/ppermute | solution.py:310
  386.6 31.5 %collective-permute-start.1 = (bf16[2,256,768]{1,2,0:T(8,128)(2,1)}, bf16[2,256,768]{1,2,0:T(8,128)(2,1)}, u32[]{:S(2)}, u32[]{:S(2)}) collective-permute-start(bf16[2,256,768]{1,2,0:T(8,128)(2,1)} %copy.116), channel_id=1, source_target_pairs={{0,2},{2,4},{4,6},{6,0},{1,3},{3,5},{5,7},{7,1},{8,10},{10,12},{12... | collective-permute-start | bytes 2359304 | tf_op jit(solution)/shard_map/while/body/eval_jaxpr/ppermute | solution.py:310
  431.9 11.7 %collective-permute-start.2 = (bf16[2,256,768]{1,2,0:T(8,128)(2,1)}, bf16[2,256,768]{1,2,0:T(8,128)(2,1)}, u32[]{:S(2)}, u32[]{:S(2)}) collective-permute-start(bf16[2,256,768]{1,2,0:T(8,128)(2,1)} %fusion.130), channel_id=1, source_target_pairs={{0,2},{2,4},{4,6},{6,0},{1,3},{3,5},{5,7},{7,1},{8,10},{10,12},{12... | collective-permute-start | bytes 2359304 | tf_op jit(solution)/shard_map/while/body/eval_jaxpr/ppermute | solution.py:310
  436.9 15.1 %collective-permute-start.3 = (bf16[2,256,768]{1,2,0:T(8,128)(2,1)}, bf16[2,256,768]{1,2,0:T(8,128)(2,1)}, u32[]{:S(2)}, u32[]{:S(2)}) collective-permute-start(bf16[2,256,768]{1,2,0:T(8,128)(2,1)} %fusion.132), channel_id=1, source_target_pairs={{0,2},{2,4},{4,6},{6,0},{1,3},{3,5},{5,7},{7,1},{8,10},{10,12},{12... | collective-permute-start | bytes 2359304 | tf_op jit(solution)/shard_map/while/body/eval_jaxpr/ppermute | solution.py:310
  436.9 23.5 %collective-permute-start = (bf16[2,256,768]{1,2,0:T(8,128)(2,1)}, bf16[2,256,768]{1,2,0:T(8,128)(2,1)}, u32[]{:S(2)}, u32[]{:S(2)}) collective-permute-start(bf16[2,256,768]{1,2,0:T(8,128)(2,1)} %copy.115), channel_id=1, source_target_pairs={{0,2},{2,4},{4,6},{6,0},{1,3},{3,5},{5,7},{7,1},{8,10},{10,12},{12... | collective-permute-start | bytes 2359304 | tf_op jit(solution)/shard_map/while/body/eval_jaxpr/ppermute | solution.py:310
  437.4 31.5 %collective-permute-start.1 = (bf16[2,256,768]{1,2,0:T(8,128)(2,1)}, bf16[2,256,768]{1,2,0:T(8,128)(2,1)}, u32[]{:S(2)}, u32[]{:S(2)}) collective-permute-start(bf16[2,256,768]{1,2,0:T(8,128)(2,1)} %copy.116), channel_id=1, source_target_pairs={{0,2},{2,4},{4,6},{6,0},{1,3},{3,5},{5,7},{7,1},{8,10},{10,12},{12... | collective-permute-start | bytes 2359304 | tf_op jit(solution)/shard_map/while/body/eval_jaxpr/ppermute | solution.py:310
  482.6 11.7 %collective-permute-start.2 = (bf16[2,256,768]{1,2,0:T(8,128)(2,1)}, bf16[2,256,768]{1,2,0:T(8,128)(2,1)}, u32[]{:S(2)}, u32[]{:S(2)}) collective-permute-start(bf16[2,256,768]{1,2,0:T(8,128)(2,1)} %fusion.130), channel_id=1, source_target_pairs={{0,2},{2,4},{4,6},{6,0},{1,3},{3,5},{5,7},{7,1},{8,10},{10,12},{12... | collective-permute-start | bytes 2359304 | tf_op jit(solution)/shard_map/while/body/eval_jaxpr/ppermute | solution.py:310
  487.7 15.1 %collective-permute-start.3 = (bf16[2,256,768]{1,2,0:T(8,128)(2,1)}, bf16[2,256,768]{1,2,0:T(8,128)(2,1)}, u32[]{:S(2)}, u32[]{:S(2)}) collective-permute-start(bf16[2,256,768]{1,2,0:T(8,128)(2,1)} %fusion.132), channel_id=1, source_target_pairs={{0,2},{2,4},{4,6},{6,0},{1,3},{3,5},{5,7},{7,1},{8,10},{10,12},{12... | collective-permute-start | bytes 2359304 | tf_op jit(solution)/shard_map/while/body/eval_jaxpr/ppermute | solution.py:310
  487.7 23.5 %collective-permute-start = (bf16[2,256,768]{1,2,0:T(8,128)(2,1)}, bf16[2,256,768]{1,2,0:T(8,128)(2,1)}, u32[]{:S(2)}, u32[]{:S(2)}) collective-permute-start(bf16[2,256,768]{1,2,0:T(8,128)(2,1)} %copy.115), channel_id=1, source_target_pairs={{0,2},{2,4},{4,6},{6,0},{1,3},{3,5},{5,7},{7,1},{8,10},{10,12},{12... | collective-permute-start | bytes 2359304 | tf_op jit(solution)/shard_map/while/body/eval_jaxpr/ppermute | solution.py:310
  488.2 31.5 %collective-permute-start.1 = (bf16[2,256,768]{1,2,0:T(8,128)(2,1)}, bf16[2,256,768]{1,2,0:T(8,128)(2,1)}, u32[]{:S(2)}, u32[]{:S(2)}) collective-permute-start(bf16[2,256,768]{1,2,0:T(8,128)(2,1)} %copy.116), channel_id=1, source_target_pairs={{0,2},{2,4},{4,6},{6,0},{1,3},{3,5},{5,7},{7,1},{8,10},{10,12},{12... | collective-permute-start | bytes 2359304 | tf_op jit(solution)/shard_map/while/body/eval_jaxpr/ppermute | solution.py:310
  535.7 135.0 %copy-start.10 = (f32[512,768]{1,0:T(8,128)S(1)}, f32[512,768]{1,0:T(8,128)}, u32[]{:S(2)}) copy-start(f32[512,768]{1,0:T(8,128)} %copy-done.9) | copy-start | bytes 4718596
  (54 other events, 406.2 us)
Sparse Core Ops, SparseCore 0:
  9.5 49.4 all-gather.15
  66.8 30.4 all-gather.17
  98.8 28.8 all-gather.19
  129.2 21.2 all-gather.21
  151.8 62.6 all-gather.23
  215.9 62.6 all-gather.25

commit v2 on v1

--- a/solution.py
+++ b/solution.py
@@ -297,6 +297,328 @@
     )(wd, wu, wo, wq, vec)
 
 
+HW = 64
+QT = 256
+MASKED = -1e30
+
+
+def remote(src, dst, ss, rs, dev):
+    return pltpu.make_async_remote_copy(src_ref=src, dst_ref=dst, send_sem=ss, recv_sem=rs, device_id=dev, device_id_type=MESH)
+
+
+def nt(a, b):
+    return lax.dot_general(a, b, (((1,), (1,)), ((), ())), preferred_element_type=F32)
+
+
+def mm(a, b):
+    return jnp.dot(a, b, preferred_element_type=F32)
+
+
+def head_masks(rows):
+    lane = lax.broadcasted_iota(jnp.int32, (rows, 2 * HW), 1)
+    return lane < HW
+
+
+def fwd_kernel(nx, seqs, seq_rows, lens, tok, sq, so_, su, sd, vec,
+               qkv_o, att_o, lse_o, wq_o, wo_o, wu_o, wd_o, vec_o,
+               XT, WB, QKV,
+               ls, ys, yr, zs, zr, as_, ar, bs, br, t0s, t0r, t1s, t1r, t2s, t2r, vs, vr, lts, outs):
+    core, x, f, z = places()
+    me = x * 2 + core
+    nblk = 2 * nx
+    rows = seqs * seq_rows
+    sib = {"ctx": x * 2 + 1 - core}
+    yp = {"fsdp": 1 - f}
+    zp = {"dp": z + 1 - 2 * lax.rem(z, 2)}
+    zb = lax.rem(z, 2)
+    xts = [lax.rem(x + j, nx) for j in range(1, nx)]
+    xps = [{"ctx": t * 2 + core} for t in xts]
+    xsrc = [lax.rem(x + nx - j, nx) * 2 + core for j in range(1, nx)]
+    peers = [sib, yp, zp] + xps
+    bar = pltpu.get_barrier_semaphore()
+    for p in peers:
+        pl.semaphore_signal(bar, inc=1, device_id=p, device_id_type=MESH)
+    order = (1, 2, 0)
+    PR = U // 4
+    piece = pl.multiple_of((zb * 2 + core) * PR, PR)
+    zpiece = pl.multiple_of(((1 - zb) * 2 + core) * PR, PR)
+    H = rows // 2
+
+    def shard(b, r0, n):
+        r = pl.ds(r0, n)
+        if b < 3:
+            return sq.at[r, pl.ds(b * 768, 768)]
+        if b == 3:
+            return so_.at[r, :]
+        if b < 8:
+            return su.at[r, pl.ds((b - 4) * 768, 768)]
+        return sd.at[pl.ds((b - 8) * U + r0, n), :]
+
+    def loc(b):
+        return pltpu.make_async_copy(shard(b, 0, U), WB.at[b, f], ls.at[b])
+
+    def ycp(b):
+        if not isinstance(b, int):
+            src = WB.at[b, f, pl.ds(piece, PR)]
+        else:
+            src = shard(b, piece, PR)
+        return remote(src, WB.at[b, f, pl.ds(piece, PR)], ys.at[b], yr.at[b], yp)
+
+    def zcp(b):
+        w = WB.at[b, 1 - f, pl.ds(piece, PR)]
+        return remote(w, w, zs.at[b], zr.at[b], zp)
+
+    def acp(b):
+        w = WB.at[b, 1 - f, pl.ds(piece, PR)]
+        return remote(w, w, as_.at[b], ar.at[b], sib)
+
+    def bcp(b):
+        w = WB.at[b, 1 - f, pl.ds(zpiece, PR)]
+        return remote(w, w, bs.at[b], br.at[b], sib)
+
+    def A(b):
+        ycp(b).wait_recv()
+        zcp(b).start()
+        acp(b).start()
+
+    def B(b):
+        zcp(b).wait_recv()
+        bcp(b).start()
+
+    def C(b):
+        acp(b).wait_recv()
+        bcp(b).wait_recv()
+
+    def tsl(h):
+        return pl.ds(h * H, H)
+
+    def t_sib(h):
+        return remote(tok.at[tsl(h)], XT.at[me, tsl(h)], t0s.at[h], t0r.at[h], sib)
+
+    def t_x(j, h):
+        return remote(tok.at[tsl(h)], XT.at[me, tsl(h)], t1s.at[j - 1, h], t1r.at[j - 1, h], xps[j - 1])
+
+    def t_f(j, h):
+        w = XT.at[xsrc[j - 1], tsl(h)]
+        return remote(w, w, t2s.at[j - 1, h], t2r.at[j - 1, h], sib)
+
+    vcp = remote(vec, vec_o.at[f], vs.at[0], vr.at[0], yp)
+    tl = pltpu.make_async_copy(tok, XT.at[me], lts.at[0])
+    tl.start()
+    for b in order:
+        loc(b).start()
+    vec_o[f] = vec[...]
+    pl.semaphore_wait(bar, len(peers))
+    vcp.start()
+    for b in order:
+        ycp(b).start()
+    for h in range(2):
+        for j in range(1, nx):
+            t_x(j, h).start()
+        t_sib(h).start()
+    for b in range(3, 12):
+        ycp(b).start()
+    for b in range(3, 12):
+        loc(b).start()
+    tl.wait()
+
+    def qkv(b, blk):
+        fac = 0.125 if b == 0 else 1.0
+
+        def one(t, _):
+            c = pl.ds(pl.multiple_of(t * 256, 256), 256)
+            w = WB[b, :, :, c].reshape(768, 256)
+            QKV[b, blk, :, c] = mm(XT[blk], w).astype(BF16)
+            return 0
+        if b == 1:
+            lax.fori_loop(0, 3, one, 0)
+        else:
+            row = 0 if b == 0 else 1
+            for t in range(3):
+                w = WB[b, :, :, t * 256:(t + 1) * 256].reshape(768, 256)
+                if t == 0:
+                    bias = vec_o[0, row:row + 1, 0:256]
+                elif t == 1:
+                    bias = jnp.concatenate([vec_o[0, row:row + 1, 256:384], vec_o[1, row:row + 1, 0:128]], 1)
+                else:
+                    bias = vec_o[1, row:row + 1, 128:384]
+                r = (mm(XT[blk], w) + bias).astype(BF16)
+                if b == 0:
+                    r = r * jnp.asarray(fac, BF16)
+                QKV[b, blk, :, t * 256:(t + 1) * 256] = r
+
+    seq = list(order)
+    A(seq[0])
+    A(seq[1])
+    B(seq[0])
+    for h in range(2):
+        t_sib(h).wait_recv()
+    A(seq[2])
+    B(seq[1])
+    vcp.wait_recv()
+    for n, b in enumerate(seq):
+        loc(b).wait()
+        C(b)
+
+        def both(i, _):
+            qkv(b, x * 2 + i)
+            return 0
+        lax.fori_loop(0, 2, both, 0)
+        if n == 0:
+            B(seq[2])
+            A(3)
+        if n == 1:
+            B(3)
+            A(4)
+    for j in range(1, nx):
+        for h in range(2):
+            t_x(j, h).wait_recv()
+            t_f(j, h).start()
+    B(4)
+    A(5)
+    for j in range(1, nx):
+        for h in range(2):
+            t_f(j, h).wait_recv()
+        base = lax.rem(x + nx - j, nx) * 2
+
+        def pair(i, _):
+            for b in seq:
+                qkv(b, base + i)
+            return 0
+        lax.fori_loop(0, 2, pair, 0)
+    B(5)
+    qo = pltpu.make_async_copy(QKV, qkv_o, outs.at[0])
+    qo.start()
+
+    low_half = head_masks(QT)
+    lane128 = lax.broadcasted_iota(jnp.int32, (QT, 128), 1)
+    kpos = lax.broadcasted_iota(jnp.int32, (QT, QT), 1)
+    nr = seq_rows // QT
+
+    def attend(tile, j):
+        s0 = tile // nr
+        qr = pl.ds(pl.multiple_of(tile * QT, QT), QT)
+        cols = pl.ds(pl.multiple_of(j * 128, 128), 128)
+        q = QKV[0, me, qr, cols]
+        length = lens[s0]
+        outs_ = []
+        tot = lse_o[qr, :]
+        for h in range(2):
+            qh = jnp.where(low_half == (h == 0), q, jnp.zeros_like(q))
+            sc = []
+            mx = None
+            for blk in range(nblk):
+                for r in range(nr):
+                    kr = pl.ds(pl.multiple_of(s0 * seq_rows + r * QT, QT), QT)
+                    v = nt(qh, QKV[1, blk, kr, cols])
+                    v = jnp.where(kpos < length - (blk * seq_rows + r * QT), v, MASKED)
+                    sc.append(v)
+                    mx = v if mx is None else jnp.maximum(mx, v)
+            m = jnp.max(mx, 1, keepdims=True)
+            acc = None
+            lsum = None
+            i = 0
+            for blk in range(nblk):
+                for r in range(nr):
+                    kr = pl.ds(pl.multiple_of(s0 * seq_rows + r * QT, QT), QT)
+                    p = jnp.exp(sc[i] - m)
+                    i += 1
+                    lsum = p if lsum is None else lsum + p
+                    o = mm(p.astype(BF16), QKV[2, blk, kr, cols])
+                    acc = o if acc is None else acc + o
+            den = jnp.sum(lsum, 1, keepdims=True)
+            outs_.append(acc / den)
+            tot = jnp.where(lane128 == 2 * j + h, m + jnp.log(den), tot)
+        att_o[qr, cols] = jnp.where(low_half, outs_[0], outs_[1])
+        lse_o[qr, :] = tot
+
+    ntile = rows // QT
+    per = ntile * 6 // 4
+
+    def group(g, _):
+        A(6 + g)
+
+        def one(i, _):
+            it = g * per + i
+            attend(it // 6, lax.rem(it, 6))
+            return 0
+        lax.fori_loop(0, per, one, 0)
+        B(6 + g)
+        return 0
+    lax.fori_loop(0, 4, group, 0)
+    A(10)
+    A(11)
+
+    def full(b):
+        res = []
+        for ff in range(2):
+            src = WB.at[b, ff]
+            if b < 3:
+                dst = wq_o.at[pl.ds(ff * U, U), pl.ds(b * 768, 768)]
+            elif b == 3:
+                dst = wo_o.at[pl.ds(ff * U, U), :]
+            elif b < 8:
+                dst = wu_o.at[pl.ds(ff * U, U), pl.ds((b - 4) * 768, 768)]
+            else:
+                dst = wd_o.at[pl.ds(ff * 1536 + (b - 8) * U, U), :]
+            res.append(pltpu.make_async_copy(src, dst, outs.at[1 + 2 * b + ff]))
+        return res
+
+    for b in range(3):
+        for cp in full(b):
+            cp.start()
+    for b in range(3, 10):
+        loc(b).wait()
+        C(b)
+        for cp in full(b):
+            cp.start()
+    for b in range(10, 12):
+        B(b)
+    for b in range(10, 12):
+        loc(b).wait()
+        C(b)
+        for cp in full(b):
+            cp.start()
+    vcp.wait_send()
+    qo.wait()
+    for b in range(12):
+        ycp(b).wait_send()
+        zcp(b).wait_send()
+        acp(b).wait_send()
+        bcp(b).wait_send()
+        for cp in full(b):
+            cp.wait()
+    for h in range(2):
+        t_sib(h).wait_send()
+        for j in range(1, nx):
+            t_x(j, h).wait_send()
+            t_f(j, h).wait_send()
+
+
+def forward_gather(lens, tok, sq, so_, su, sd, vec, nx, cid):
+    seqs, seq_rows, d = tok.shape
+    rows = seqs * seq_rows
+    nblk = 2 * nx
+    anyspec = pl.BlockSpec(memory_space=pl.ANY)
+    vspec = pl.BlockSpec(memory_space=pltpu.VMEM)
+    sspec = pl.BlockSpec(memory_space=pltpu.SMEM)
+    D = pltpu.SemaphoreType.DMA
+    V = pltpu.VMEM
+    S = jax.ShapeDtypeStruct
+    sems = [D((12,))] * 9 + [D((2,)), D((2,))] + [D((nx - 1, 2))] * 4 + [D((1,)), D((1,)), D((1,)), D((25,))]
+    return pl.pallas_call(
+        functools.partial(fwd_kernel, nx, seqs, seq_rows),
+        out_shape=(S((3, nblk, rows, d), BF16), S((rows, d), F32), S((rows, 128), F32),
+                   S((768, 2304), BF16), S((768, 768), BF16), S((768, 3072), BF16), S((3072, 768), BF16),
+                   S((2, 12, U), F32)),
+        in_specs=[sspec, anyspec, anyspec, anyspec, anyspec, anyspec, vspec],
+        out_specs=(anyspec, vspec, vspec, anyspec, anyspec, anyspec, anyspec, vspec),
+        scratch_shapes=[V((nblk, rows, d), BF16), V((12, 2, U, 768), BF16), V((3, nblk, rows, d), BF16)] + sems,
+        compiler_params=pltpu.CompilerParams(collective_id=cid, has_side_effects=True, vmem_limit_bytes=60 << 20),
+        name="forward_gather",
+    )(lens, tok.reshape(rows, d), sq, so_, su, sd, vec)
+
+
 HEADS = 12
 
 
@@ -337,7 +659,7 @@
     )
 
 
-def body(
+def general_body(
     tokens,
     cotangent,
     lengths,
@@ -606,9 +928,217 @@
     )
 
 
+def fast_body(
+    tokens,
+    cotangent,
+    lengths,
+    w_qkv,
+    bias_q,
+    bias_v,
+    w_out,
+    bias_out,
+    gain_one,
+    shift_one,
+    w_up,
+    bias_up,
+    w_down,
+    bias_down,
+    gain_two,
+    shift_two,
+):
+    seq_count, block_rows, model_width = tokens.shape
+    head_count = HEADS
+    head_dim = model_width // head_count
+    all_rows = seq_count * block_rows
+    score_scale = head_dim ** (-0.5)
+    cycle_size = lax.axis_size("ctx")
+    cycle_index = lax.axis_index("ctx")
+    packed_in = jnp.concatenate(
+        [bias_q, bias_v, bias_out, gain_one, shift_one, bias_up, bias_down, gain_two, shift_two]
+    ).astype(jnp.float32).reshape(VR // 2, U)
+    flat_tokens = tokens.reshape(all_rows, model_width)
+    qkv_all, attended, lse_pad, full_qkv, full_out, full_up, full_down, vec_all = forward_gather(
+        lengths, tokens, w_qkv, w_out, w_up, w_down, packed_in, cycle_size // 2, 2
+    )
+
+    def vector(first, count):
+        return vec_all[:, first : first + count].reshape(-1)
+
+    add_out, scale_one, move_one = vector(2, 1), vector(3, 1), vector(4, 1)
+    add_up, add_down, scale_two, move_two = vector(5, 4), vector(9, 1), vector(10, 1), vector(11, 1)
+    mine = lax.dynamic_index_in_dim(qkv_all, cycle_index, 1, False)
+    shape4 = (seq_count, block_rows, head_count, head_dim)
+    queries = (mine[0] * jnp.asarray(8.0, jnp.bfloat16)).reshape(shape4)
+    key_rows = mine[1].reshape(seq_count, block_rows, model_width)
+    value_rows = mine[2].reshape(seq_count, block_rows, model_width)
+    attended = attended.reshape(shape4)
+    log_total = lse_pad[:, :head_count].reshape(seq_count, block_rows, head_count)
+    attended_low = attended.astype(jnp.bfloat16).reshape(all_rows, model_width)
+    first_sum = flat_tokens.astype(jnp.float32) + row_dot(attended_low, full_out) + add_out
+    normed, norm_pull = jax.vjp(normalize, first_sum, scale_one, move_one)
+    normed_low = normed.astype(jnp.bfloat16)
+    hidden_pre = row_dot(normed_low, full_up) + add_up
+    hidden_act, gelu_pull = jax.vjp(gelu_exact, hidden_pre)
+    hidden_low = hidden_act.astype(jnp.bfloat16)
+    second_sum = normed + row_dot(hidden_low, full_down) + add_down
+    result, result_pull = jax.vjp(normalize, second_sum, scale_two, move_two)
+    grad_second, grad_gain_two, grad_shift_two = result_pull(
+        cotangent.reshape(all_rows, model_width).astype(jnp.float32)
+    )
+    down_low = grad_second.astype(jnp.bfloat16)
+    grad_w_down = left_dot(hidden_low, down_low)
+    grad_bias_down = jnp.sum(down_low.astype(jnp.float32), 0)
+    (grad_pre,) = gelu_pull(right_dot(down_low, full_down))
+    up_low = grad_pre.astype(jnp.bfloat16)
+    grad_w_up = left_dot(normed_low, up_low)
+    grad_bias_up = jnp.sum(up_low.astype(jnp.float32), 0)
+    grad_first, grad_gain_one, grad_shift_one = norm_pull(grad_second + right_dot(up_low, full_up))
+    branch_low = grad_first.astype(jnp.bfloat16)
+    grad_w_out = left_dot(attended_low, branch_low)
+    grad_bias_out = jnp.sum(branch_low.astype(jnp.float32), 0)
+    grad_att = (
+        right_dot(branch_low, full_out)
+        .astype(jnp.bfloat16)
+        .reshape(seq_count, block_rows, head_count, head_dim)
+    )
+    delta_rows = jnp.sum(grad_att.astype(jnp.float32) * attended, -1)
+
+    def block_grads(query_part, grad_part, lse_part, delta_part, key_block, value_block, first_key):
+        key_count = key_block.shape[1]
+        key_heads = key_block.reshape(seq_count, key_count, head_count, head_dim)
+        value_heads = value_block.reshape(seq_count, key_count, head_count, head_dim)
+        key_live = (
+            (first_key + jnp.arange(key_count, dtype=jnp.int32))[None, :] < lengths[:, None]
+        )[:, None, None, :]
+        scores = (
+            jnp.einsum("sqhe,skhe->sqhk", query_part, key_heads, preferred_element_type=jnp.float32)
+            * score_scale
+        )
+        chances = jnp.where(key_live, jnp.exp(scores - lse_part[..., None]), 0.0)
+        grad_value = jnp.einsum(
+            "sqhk,sqhe->skhe",
+            chances.astype(jnp.bfloat16),
+            grad_part,
+            preferred_element_type=jnp.float32,
+        )
+        grad_chance = jnp.einsum(
+            "sqhe,skhe->sqhk", grad_part, value_heads, preferred_element_type=jnp.float32
+        )
+        grad_score = (chances * (grad_chance - delta_part[..., None])).astype(jnp.bfloat16)
+        grad_query = (
+            jnp.einsum("sqhk,skhe->sqhe", grad_score, key_heads, preferred_element_type=jnp.float32)
+            * score_scale
+        )
+        grad_key = (
+            jnp.einsum(
+                "sqhk,sqhe->skhe", grad_score, query_part, preferred_element_type=jnp.float32
+            )
+            * score_scale
+        )
+        return (
+            grad_query,
+            grad_key.reshape(seq_count, key_count, model_width),
+            grad_value.reshape(seq_count, key_count, model_width),
+        )
+
+    query_start = jnp.zeros((seq_count, block_rows, head_count, head_dim), jnp.float32)
+
+    def key_terms(key_block, value_block, first_key):
+        return block_grads(
+            queries, grad_att, log_total, delta_rows, key_block, value_block, first_key
+        )
+
+    def block_terms(key_block, value_block, first_key):
+        return key_terms(key_block, value_block, first_key)
+
+    def turn(step_index, carried):
+        key_now, value_now, key_grads, query_acc = carried
+        first_key = (cycle_index - step_index) % cycle_size * block_rows
+        add_query, add_key, add_value = block_terms(key_now, value_now, first_key)
+        key_now, value_now = shifted((key_now, value_now), "ctx", 1)
+        key_grads = (
+            shifted((key_grads[0] + add_key).astype(jnp.bfloat16), "ctx", 1).astype(jnp.float32),
+            shifted((key_grads[1] + add_value).astype(jnp.bfloat16), "ctx", 1).astype(jnp.float32),
+        )
+        return (key_now, value_now, key_grads, query_acc + add_query)
+
+    grad_start = (
+        jnp.zeros((seq_count, block_rows, model_width), jnp.float32),
+        jnp.zeros((seq_count, block_rows, model_width), jnp.float32),
+    )
+    key_final, value_final, key_grads, query_grad = lax.fori_loop(
+        0, cycle_size, turn, (key_rows, value_rows, grad_start, query_start)
+    )
+    grad_key, grad_value = key_grads
+    qkv_grad = jnp.concatenate(
+        [
+            query_grad.astype(jnp.bfloat16).reshape(all_rows, model_width),
+            grad_key.astype(jnp.bfloat16).reshape(all_rows, model_width),
+            grad_value.astype(jnp.bfloat16).reshape(all_rows, model_width),
+        ],
+        1,
+    )
+    grad_w_qkv = left_dot(flat_tokens, qkv_grad)
+    grad_bias_q = jnp.sum(qkv_grad[:, :model_width].astype(jnp.float32), 0)
+    grad_bias_v = jnp.sum(qkv_grad[:, 2 * model_width :].astype(jnp.float32), 0)
+    grad_input = grad_first + right_dot(qkv_grad, full_qkv)
+    vectors = (
+        grad_bias_q,
+        grad_bias_v,
+        grad_bias_out,
+        grad_gain_one,
+        grad_shift_one,
+        grad_bias_up,
+        grad_bias_down,
+        grad_gain_two,
+        grad_shift_two,
+    )
+    packed = jnp.concatenate(vectors).reshape(VR, U)
+    t_down, t_up, t_out, t_qkv, t_vec = grad_reduce(
+        grad_w_down.astype(BF16),
+        grad_w_up.astype(BF16),
+        grad_w_out.astype(BF16),
+        grad_w_qkv.astype(BF16),
+        packed,
+        cycle_size // 2,
+        lax.axis_size("dp"),
+        1,
+    )
+    flat = t_vec.reshape(-1)
+    own = lax.axis_index("fsdp")
+    parts, start = [], 0
+    for vector in vectors:
+        half = vector.shape[0] // 2
+        parts.append(lax.dynamic_slice_in_dim(flat, start + own * half, half, 0))
+        start += 2 * half
+    totals = (
+        t_qkv, parts[0], parts[1], t_out, parts[2], parts[3], parts[4],
+        t_up, parts[5], t_down, parts[6], parts[7], parts[8],
+    )
+    output_rows = result.astype(jnp.bfloat16).reshape(seq_count, block_rows, model_width)
+    input_rows = grad_input.astype(jnp.bfloat16).reshape(seq_count, block_rows, model_width)
+    return (
+        output_rows,
+        input_rows,
+        totals[0],
+        totals[1],
+        totals[2],
+        totals[3],
+        totals[4],
+        totals[5],
+        totals[6],
+        totals[7],
+        totals[8],
+        totals[9],
+        totals[10],
+        totals[11],
+        totals[12],
+    )
+
+
 def solution(mesh):
     return jax.shard_map(
-        body,
+        fast_body if mesh.shape["ctx"] <= 4 else general_body,
         mesh=mesh,
         in_specs=(
             P(("dp", "fsdp"), "ctx", None),

time: 698 us -> 534 us (0.77)
  waiting for transfers between devices: 247 us -> 89.9 us
  Pallas kernels: 133 us -> 198 us
  blocking collectives: 30.1 us -> 0 us
  matrix products: 138 us -> 114 us
  other arithmetic: 58.1 us -> 41.2 us
  between operations: 15 us -> 1.28 us
  local copies, waits for them, and re-layouts: 58.1 us -> 66.6 us
    all_gather x6 -> x0, waiting for transfers between devices: 152 us -> none  [the longest x1 51 us: body(): lax.all_gather(w_qkv, 'fsdp', axis=0, tiled=True)]
    pallas_call x0 -> x1, Pallas kernels: none -> 66.2 us  [forward_gather(): pl.pallas_call(functools.partial(fwd_kernel, nx, seqs, seq_rows), out_sha...]
    all_gather x9 -> x0, blocking collectives: 30.1 us -> none  [the longest x1 3.56 us: body(): lax.all_gather(bias_up, 'fsdp', axis=0, tiled=True)]
    dot_general x4 -> x0, matrix products: 21.8 us -> none  [the longest x2 12.2 us: visit(): jnp.einsum('sqhe,skhe->sqhk', queries, key_block, preferred_element_type=...]
    reduce_sum x7 -> x5, other arithmetic: 18 us -> 3.5 us  [the longest x1 1.28 us: fast_body(): grad_bias_v = jnp.sum(qkv_grad[:, 2 * model_width:].astype(jnp.float32), 0)]
    unnamed x94 -> x89, local copies, waits for them, and re-layouts: 14.5 us -> 25.2 us
    while x57 -> x50, local copies, waits for them, and re-layouts: 25.7 us -> 21.7 us
    dot_general x4 -> x3, matrix products: 33 us -> 29.3 us  [row_dot(): return jnp.dot(left_op, right_op, preferred_element_type=jnp.float32)]
  transfers between devices with their start and end apart: 22 -> 16, of which waited for: 20 -> 16; matrix products, arithmetic and copies ran while one was open for 17% -> 8% of each run, Pallas kernels for 0% -> 0%
where the time goes in v2:
time: 534 us; the launch traced here: 524 us
  Pallas kernels  198 us (37%)
  matrix products  114 us (21%)
  waiting for transfers between devices  89.9 us (17%)
  local copies, waits for them, and re-layouts  66.6 us (12%)
  other arithmetic  41.2 us (8%)
  starting transfers between devices  12.8 us (2%)
    pallas_call x1, Pallas kernels, grad_reduce(): pl.pallas_call(functools.partial(grad_kernel, nx, nd, grp), out_shape=(ja...  132 us
    ppermute x16, waiting for transfers between devices, shifted(): return lax.ppermute(value, axis, pairs)  89.9 us
    pallas_call x1, Pallas kernels, forward_gather(): pl.pallas_call(functools.partial(fwd_kernel, nx, seqs, seq_rows), out_sha...  66.2 us
    dot_general x3, matrix products, row_dot(): return jnp.dot(left_op, right_op, preferred_element_type=jnp.float32)  29.3 us
    unnamed x89, local copies, waits for them, and re-layouts  25.2 us
    dot_general x4, matrix products, right_dot(): lax.dot_general(left_op, right_op, (((1,), (1,)), ((), ())), preferred_el...  18.2 us
    while x48, local copies, waits for them, and re-layouts  17.9 us
    dot_general x4, matrix products, left_dot(): lax.dot_general(left_op, right_op, (((0,), (0,)), ((), ())), preferred_el...  14.8 us
  transfers between devices with their start and end apart: 16, of which 16 were waited for; matrix products, arithmetic and copies ran while one was open for 8% of the time, Pallas kernels for 0%

profile of v2, /device:TPU:5, one launch (start us, length us, event | category | flops | bytes accessed | tf_op | source)
XLA Modules:
  0.0 523.6 jit_solution(17996895763904382624)
XLA Ops:
  10.9 66.2 %forward_gather.1 = (bf16[3,4,512,768]{3,2,1,0:T(8,128)(2,1)}, f32[512,768]{1,0:T(8,128)}, f32[512,128]{1,0:T(8,128)}, bf16[768,2304]{1,0:T(8,128)(2,1)}, bf16[7...) custom-call(s32[2]{0:T(128)} %lens.1, ...), custom_call_target="tpu_custom_call" | custom-call | tf_op jit(solution)/shard_map/forward_gather/pallas_call | solution.py:609
  94.0 20.8 %multiply_convert_fusion = (bf16[512,3072]{1,0:T(8,128)(2,1)S(1)}, f32[512,3072]{1,0:T(8,128)}, f32[512,3072]{1,0:T(8,128)}) fusion(f32[3072]{0:T(1024)S(1)} %add.220, bf16[768,3072]{1,0:T(8,128)(2,1)} %get-tuple-element.320, f32[512,768]{1,0:T(8,128)} %copy-done.9, f32[768]{0:T(1024)S(1)} %add.217, f32[768]{0:T(1024)S(1)} %mul.228, f32[512]{0:T(512)S(1)} %fusion.29, ...), kind=kOutput, calls=%fused_computation.26 | convolution fusion | flops 2521694208 | bytes 22042624 | tf_op jit(solution)/shard_map/dot_general | solution.py:647
  114.8 6.3 %fusion.41 = (f32[512]{0:T(512)S(1)}, f32[512,768]{1,0:T(8,128)S(1)}) fusion(f32[768]{0:T(1024)S(1)} %add.224, bf16[512,3072]{1,0:T(8,128)(2,1)S(1)} %get-tuple-element.455, bf16[3072,768]{1,0:T(8,128)(2,1)} %get-tuple-element.321, f32[768]{0:T(1024)S(1)} %add.217, f32[768]{0:T(1024)S(1)} %mul.228, f32[512]{0:T(512)S(1)} %fusion.29, ...), kind=kOutput, calls=%fused_computation.111 | convolution fusion | flops 2418671104 | bytes 11025408 | tf_op jit(solution)/shard_map/dot_general | solution.py:647
  124.1 9.2 %convert_reduce_fusion = (f32[3072]{0:T(1024)S(1)}, bf16[512,3072]{1,0:T(8,128)(2,1)S(1)}) fusion(f32[512,3072]{1,0:T(8,128)} %get-tuple-element.456, f32[512,3072]{1,0:T(8,128)} %get-tuple-element.471, f32[3072]{0:T(1024)S(1)} %add.220, bf16[512,768]{1,0:T(8,128)(2,1)S(1)} %get-tuple-element.444, bf16[3072,768]{1,0:T(8,128)(2,1)} %get-tuple-element.321), kind=kOutput, calls=%fused_computation.24 | convolution fusion | flops 2442654720 | bytes 21258240 | tf_op jit(solution)/shard_map/dot_general | solution.py:657
  137.2 4.8 convolution_convert_fusion.1.wu
  150.1 201.7 %while.25 = (s32[]{:T(128)}, bf16[2,256,768]{1,2,0:T(8,128)(2,1)}, bf16[2,256,768]{1,2,0:T(8,128)(2,1)}, f32[2,256,768]{1,2,0:T(8,128)}, f32[2,256,768]{1,2,0:T(...) while((s32[]{:T(128)}, bf16[2,256,768]{1,2,0:T(8,128)(2,1)}, ...), condition=%wide.wide.region_10.11_spmd.clone, body=%wide.wide.region_9.10_spmd.clone.sunk | while | flops 1027080960 | bytes 90566752 | solution.py:1069
  176.3 6.0 %collective-permute-done.3 = bf16[2,256,768]{1,2,0:T(8,128)(2,1)} collective-permute-done((bf16[2,256,768]{1,2,0:T(8,128)(2,1)}, bf16[2,256,768]{1,2,0:T(8,128)(2,1)}, u32[]{:S(2)}, u32[]{:S(2)}) %collective-permute-start.3) | collective-permute-done | bytes 786464 | tf_op jit(solution)/shard_map/while/body/eval_jaxpr/ppermute | solution.py:632
  184.7 6.0 %collective-permute-done = bf16[2,256,768]{1,2,0:T(8,128)(2,1)} collective-permute-done((bf16[2,256,768]{1,2,0:T(8,128)(2,1)}, bf16[2,256,768]{1,2,0:T(8,128)(2,1)}, u32[]{:S(2)}, u32[]{:S(2)}) %collective-permute-start) | collective-permute-done | bytes 786464 | tf_op jit(solution)/shard_map/while/body/eval_jaxpr/ppermute | solution.py:632
  190.7 8.4 %collective-permute-done.1 = bf16[2,256,768]{1,2,0:T(8,128)(2,1)} collective-permute-done((bf16[2,256,768]{1,2,0:T(8,128)(2,1)}, bf16[2,256,768]{1,2,0:T(8,128)(2,1)}, u32[]{:S(2)}, u32[]{:S(2)}) %collective-permute-start.1) | collective-permute-done | bytes 786464 | tf_op jit(solution)/shard_map/while/body/eval_jaxpr/ppermute | solution.py:632
  219.1 3.5 bitcast_add_fusion.5
  227.1 6.0 %collective-permute-done.3 = bf16[2,256,768]{1,2,0:T(8,128)(2,1)} collective-permute-done((bf16[2,256,768]{1,2,0:T(8,128)(2,1)}, bf16[2,256,768]{1,2,0:T(8,128)(2,1)}, u32[]{:S(2)}, u32[]{:S(2)}) %collective-permute-start.3) | collective-permute-done | bytes 786464 | tf_op jit(solution)/shard_map/while/body/eval_jaxpr/ppermute | solution.py:632
  235.5 6.0 %collective-permute-done = bf16[2,256,768]{1,2,0:T(8,128)(2,1)} collective-permute-done((bf16[2,256,768]{1,2,0:T(8,128)(2,1)}, bf16[2,256,768]{1,2,0:T(8,128)(2,1)}, u32[]{:S(2)}, u32[]{:S(2)}) %collective-permute-start) | collective-permute-done | bytes 786464 | tf_op jit(solution)/shard_map/while/body/eval_jaxpr/ppermute | solution.py:632
  241.5 8.4 %collective-permute-done.1 = bf16[2,256,768]{1,2,0:T(8,128)(2,1)} collective-permute-done((bf16[2,256,768]{1,2,0:T(8,128)(2,1)}, bf16[2,256,768]{1,2,0:T(8,128)(2,1)}, u32[]{:S(2)}, u32[]{:S(2)}) %collective-permute-start.1) | collective-permute-done | bytes 786464 | tf_op jit(solution)/shard_map/while/body/eval_jaxpr/ppermute | solution.py:632
  278.0 6.0 %collective-permute-done.3 = bf16[2,256,768]{1,2,0:T(8,128)(2,1)} collective-permute-done((bf16[2,256,768]{1,2,0:T(8,128)(2,1)}, bf16[2,256,768]{1,2,0:T(8,128)(2,1)}, u32[]{:S(2)}, u32[]{:S(2)}) %collective-permute-start.3) | collective-permute-done | bytes 786464 | tf_op jit(solution)/shard_map/while/body/eval_jaxpr/ppermute | solution.py:632
  286.4 6.0 %collective-permute-done = bf16[2,256,768]{1,2,0:T(8,128)(2,1)} collective-permute-done((bf16[2,256,768]{1,2,0:T(8,128)(2,1)}, bf16[2,256,768]{1,2,0:T(8,128)(2,1)}, u32[]{:S(2)}, u32[]{:S(2)}) %collective-permute-start) | collective-permute-done | bytes 786464 | tf_op jit(solution)/shard_map/while/body/eval_jaxpr/ppermute | solution.py:632
  292.4 8.4 %collective-permute-done.1 = bf16[2,256,768]{1,2,0:T(8,128)(2,1)} collective-permute-done((bf16[2,256,768]{1,2,0:T(8,128)(2,1)}, bf16[2,256,768]{1,2,0:T(8,128)(2,1)}, u32[]{:S(2)}, u32[]{:S(2)}) %collective-permute-start.1) | collective-permute-done | bytes 786464 | tf_op jit(solution)/shard_map/while/body/eval_jaxpr/ppermute | solution.py:632
  328.8 6.0 %collective-permute-done.3 = bf16[2,256,768]{1,2,0:T(8,128)(2,1)} collective-permute-done((bf16[2,256,768]{1,2,0:T(8,128)(2,1)}, bf16[2,256,768]{1,2,0:T(8,128)(2,1)}, u32[]{:S(2)}, u32[]{:S(2)}) %collective-permute-start.3) | collective-permute-done | bytes 786464 | tf_op jit(solution)/shard_map/while/body/eval_jaxpr/ppermute | solution.py:632
  337.2 6.0 %collective-permute-done = bf16[2,256,768]{1,2,0:T(8,128)(2,1)} collective-permute-done((bf16[2,256,768]{1,2,0:T(8,128)(2,1)}, bf16[2,256,768]{1,2,0:T(8,128)(2,1)}, u32[]{:S(2)}, u32[]{:S(2)}) %collective-permute-start) | collective-permute-done | bytes 786464 | tf_op jit(solution)/shard_map/while/body/eval_jaxpr/ppermute | solution.py:632
  343.2 8.4 %collective-permute-done.1 = bf16[2,256,768]{1,2,0:T(8,128)(2,1)} collective-permute-done((bf16[2,256,768]{1,2,0:T(8,128)(2,1)}, bf16[2,256,768]{1,2,0:T(8,128)(2,1)}, u32[]{:S(2)}, u32[]{:S(2)}) %collective-permute-start.1) | collective-permute-done | bytes 786464 | tf_op jit(solution)/shard_map/while/body/eval_jaxpr/ppermute | solution.py:632
  365.7 5.0 add_convert_fusion.1
  370.7 3.8 fusion.21.wq
  374.6 4.3 convolution_convert_fusion.2.wd
  378.9 131.6 %grad_reduce.1 = (f32[1536,768]{1,0:T(8,128)}, f32[384,3072]{1,0:T(8,128)}, f32[384,768]{1,0:T(8,128)}, f32[384,2304]{1,0:T(8,128)}, f32[24,384]{1,0:T(8,128)}) custom-call(bf16[3072,768]{1,0:T(8,128)(2,1)} %convolution_convert_fusion.2.wd, bf16[768,3072]{1,0:T(8,128)(2,1)} %convolution_convert_fusion.1.wu, bf16[768,768]{1,0:T(8,128)(2,1)} %convolution_convert_fusion.3.wo, ...), custom_call_target="tpu_custom_call" | custom-call | tf_op jit(solution)/shard_map/grad_reduce/pallas_call | solution.py:284
  512.6 4.2 copy.126
  (264 shorter events, 180.4 us)
Async XLA Ops:
  94.0 20.9 %copy-start.10 = (f32[512,768]{1,0:T(8,128)S(1)}, f32[512,768]{1,0:T(8,128)}, u32[]{:S(2)}) copy-start(f32[512,768]{1,0:T(8,128)} %copy-done.9) | copy-start | bytes 4718596
  122.3 11.1 %slice-start.4 = ((s8[4718592]{0:T(1024)(128)(4,1)}), s8[4194304]{0:T(1024)(128)(4,1)S(1)}, s32[]{:S(2)}) async-start(s8[4718592]{0:T(1024)(128)(4,1)} %bitcast.164), calls=%async_computation.4 | async-start | bytes 8388608
  124.1 9.2 %copy-start.19 = (bf16[512,768]{1,0:T(8,128)(2,1)}, bf16[512,768]{1,0:T(8,128)(2,1)S(1)}, u32[]{:S(2)}) copy-start(bf16[512,768]{1,0:T(8,128)(2,1)S(1)} %get-tuple-element.444) | copy-start | bytes 2359300
  124.1 9.2 %slice-start.5 = ((s8[4718592]{0:T(1024)(128)(4,1)}), s8[524288]{0:T(1024)(128)(4,1)S(1)}, s32[]{:S(2)}) async-start(s8[4718592]{0:T(1024)(128)(4,1)} %bitcast.164), calls=%async_computation.5 | async-start | bytes 1048576
  164.0 9.9 %collective-permute-start.2 = (bf16[2,256,768]{1,2,0:T(8,128)(2,1)}, bf16[2,256,768]{1,2,0:T(8,128)(2,1)}, u32[]{:S(2)}, u32[]{:S(2)}) collective-permute-start(bf16[2,256,768]{1,2,0:T(8,128)(2,1)} %fusion.110), channel_id=1, source_target_pairs={{0,2},{2,4},{4,6},{6,0},{1,3},{3,5},{5,7},{7,1},{8,10},{10,12},{12... | collective-permute-start | bytes 2359304 | tf_op jit(solution)/shard_map/while/body/eval_jaxpr/ppermute | solution.py:632
  167.2 15.1 %collective-permute-start.3 = (bf16[2,256,768]{1,2,0:T(8,128)(2,1)}, bf16[2,256,768]{1,2,0:T(8,128)(2,1)}, u32[]{:S(2)}, u32[]{:S(2)}) collective-permute-start(bf16[2,256,768]{1,2,0:T(8,128)(2,1)} %fusion.112), channel_id=1, source_target_pairs={{0,2},{2,4},{4,6},{6,0},{1,3},{3,5},{5,7},{7,1},{8,10},{10,12},{12... | collective-permute-start | bytes 2359304 | tf_op jit(solution)/shard_map/while/body/eval_jaxpr/ppermute | solution.py:632
  168.2 22.5 %collective-permute-start = (bf16[2,256,768]{1,2,0:T(8,128)(2,1)}, bf16[2,256,768]{1,2,0:T(8,128)(2,1)}, u32[]{:S(2)}, u32[]{:S(2)}) collective-permute-start(bf16[2,256,768]{1,2,0:T(8,128)(2,1)} %copy.102), channel_id=1, source_target_pairs={{0,2},{2,4},{4,6},{6,0},{1,3},{3,5},{5,7},{7,1},{8,10},{10,12},{12... | collective-permute-start | bytes 2359304 | tf_op jit(solution)/shard_map/while/body/eval_jaxpr/ppermute | solution.py:632
  168.2 30.9 %collective-permute-start.1 = (bf16[2,256,768]{1,2,0:T(8,128)(2,1)}, bf16[2,256,768]{1,2,0:T(8,128)(2,1)}, u32[]{:S(2)}, u32[]{:S(2)}) collective-permute-start(bf16[2,256,768]{1,2,0:T(8,128)(2,1)} %copy.103), channel_id=1, source_target_pairs={{0,2},{2,4},{4,6},{6,0},{1,3},{3,5},{5,7},{7,1},{8,10},{10,12},{12... | collective-permute-start | bytes 2359304 | tf_op jit(solution)/shard_map/while/body/eval_jaxpr/ppermute | solution.py:632
  171.9 27.3 %copy-start.1 = (bf16[2,256,12,64]{1,3,2,0:T(8,128)(2,1)S(1)}, bf16[2,256,12,64]{1,3,2,0:T(8,128)(2,1)}, u32[]{:S(2)}) copy-start(bf16[2,256,12,64]{1,3,2,0:T(8,128)(2,1)} %copy-done) | copy-start | bytes 2359300 | tf_op jit(solution)/shard_map/while
  213.0 11.7 %collective-permute-start.2 = (bf16[2,256,768]{1,2,0:T(8,128)(2,1)}, bf16[2,256,768]{1,2,0:T(8,128)(2,1)}, u32[]{:S(2)}, u32[]{:S(2)}) collective-permute-start(bf16[2,256,768]{1,2,0:T(8,128)(2,1)} %fusion.110), channel_id=1, source_target_pairs={{0,2},{2,4},{4,6},{6,0},{1,3},{3,5},{5,7},{7,1},{8,10},{10,12},{12... | collective-permute-start | bytes 2359304 | tf_op jit(solution)/shard_map/while/body/eval_jaxpr/ppermute | solution.py:632
  218.1 15.1 %collective-permute-start.3 = (bf16[2,256,768]{1,2,0:T(8,128)(2,1)}, bf16[2,256,768]{1,2,0:T(8,128)(2,1)}, u32[]{:S(2)}, u32[]{:S(2)}) collective-permute-start(bf16[2,256,768]{1,2,0:T(8,128)(2,1)} %fusion.112), channel_id=1, source_target_pairs={{0,2},{2,4},{4,6},{6,0},{1,3},{3,5},{5,7},{7,1},{8,10},{10,12},{12... | collective-permute-start | bytes 2359304 | tf_op jit(solution)/shard_map/while/body/eval_jaxpr/ppermute | solution.py:632
  218.1 23.5 %collective-permute-start = (bf16[2,256,768]{1,2,0:T(8,128)(2,1)}, bf16[2,256,768]{1,2,0:T(8,128)(2,1)}, u32[]{:S(2)}, u32[]{:S(2)}) collective-permute-start(bf16[2,256,768]{1,2,0:T(8,128)(2,1)} %copy.102), channel_id=1, source_target_pairs={{0,2},{2,4},{4,6},{6,0},{1,3},{3,5},{5,7},{7,1},{8,10},{10,12},{12... | collective-permute-start | bytes 2359304 | tf_op jit(solution)/shard_map/while/body/eval_jaxpr/ppermute | solution.py:632
  219.1 30.9 %collective-permute-start.1 = (bf16[2,256,768]{1,2,0:T(8,128)(2,1)}, bf16[2,256,768]{1,2,0:T(8,128)(2,1)}, u32[]{:S(2)}, u32[]{:S(2)}) collective-permute-start(bf16[2,256,768]{1,2,0:T(8,128)(2,1)} %copy.103), channel_id=1, source_target_pairs={{0,2},{2,4},{4,6},{6,0},{1,3},{3,5},{5,7},{7,1},{8,10},{10,12},{12... | collective-permute-start | bytes 2359304 | tf_op jit(solution)/shard_map/while/body/eval_jaxpr/ppermute | solution.py:632
  222.6 27.3 %copy-start.1 = (bf16[2,256,12,64]{1,3,2,0:T(8,128)(2,1)S(1)}, bf16[2,256,12,64]{1,3,2,0:T(8,128)(2,1)}, u32[]{:S(2)}) copy-start(bf16[2,256,12,64]{1,3,2,0:T(8,128)(2,1)} %copy-done) | copy-start | bytes 2359300 | tf_op jit(solution)/shard_map/while
  263.8 11.7 %collective-permute-start.2 = (bf16[2,256,768]{1,2,0:T(8,128)(2,1)}, bf16[2,256,768]{1,2,0:T(8,128)(2,1)}, u32[]{:S(2)}, u32[]{:S(2)}) collective-permute-start(bf16[2,256,768]{1,2,0:T(8,128)(2,1)} %fusion.110), channel_id=1, source_target_pairs={{0,2},{2,4},{4,6},{6,0},{1,3},{3,5},{5,7},{7,1},{8,10},{10,12},{12... | collective-permute-start | bytes 2359304 | tf_op jit(solution)/shard_map/while/body/eval_jaxpr/ppermute | solution.py:632
  268.9 15.1 %collective-permute-start.3 = (bf16[2,256,768]{1,2,0:T(8,128)(2,1)}, bf16[2,256,768]{1,2,0:T(8,128)(2,1)}, u32[]{:S(2)}, u32[]{:S(2)}) collective-permute-start(bf16[2,256,768]{1,2,0:T(8,128)(2,1)} %fusion.112), channel_id=1, source_target_pairs={{0,2},{2,4},{4,6},{6,0},{1,3},{3,5},{5,7},{7,1},{8,10},{10,12},{12... | collective-permute-start | bytes 2359304 | tf_op jit(solution)/shard_map/while/body/eval_jaxpr/ppermute | solution.py:632
  268.9 23.5 %collective-permute-start = (bf16[2,256,768]{1,2,0:T(8,128)(2,1)}, bf16[2,256,768]{1,2,0:T(8,128)(2,1)}, u32[]{:S(2)}, u32[]{:S(2)}) collective-permute-start(bf16[2,256,768]{1,2,0:T(8,128)(2,1)} %copy.102), channel_id=1, source_target_pairs={{0,2},{2,4},{4,6},{6,0},{1,3},{3,5},{5,7},{7,1},{8,10},{10,12},{12... | collective-permute-start | bytes 2359304 | tf_op jit(solution)/shard_map/while/body/eval_jaxpr/ppermute | solution.py:632
  269.9 30.9 %collective-permute-start.1 = (bf16[2,256,768]{1,2,0:T(8,128)(2,1)}, bf16[2,256,768]{1,2,0:T(8,128)(2,1)}, u32[]{:S(2)}, u32[]{:S(2)}) collective-permute-start(bf16[2,256,768]{1,2,0:T(8,128)(2,1)} %copy.103), channel_id=1, source_target_pairs={{0,2},{2,4},{4,6},{6,0},{1,3},{3,5},{5,7},{7,1},{8,10},{10,12},{12... | collective-permute-start | bytes 2359304 | tf_op jit(solution)/shard_map/while/body/eval_jaxpr/ppermute | solution.py:632
  273.5 27.3 %copy-start.1 = (bf16[2,256,12,64]{1,3,2,0:T(8,128)(2,1)S(1)}, bf16[2,256,12,64]{1,3,2,0:T(8,128)(2,1)}, u32[]{:S(2)}) copy-start(bf16[2,256,12,64]{1,3,2,0:T(8,128)(2,1)} %copy-done) | copy-start | bytes 2359300 | tf_op jit(solution)/shard_map/while
  314.7 11.7 %collective-permute-start.2 = (bf16[2,256,768]{1,2,0:T(8,128)(2,1)}, bf16[2,256,768]{1,2,0:T(8,128)(2,1)}, u32[]{:S(2)}, u32[]{:S(2)}) collective-permute-start(bf16[2,256,768]{1,2,0:T(8,128)(2,1)} %fusion.110), channel_id=1, source_target_pairs={{0,2},{2,4},{4,6},{6,0},{1,3},{3,5},{5,7},{7,1},{8,10},{10,12},{12... | collective-permute-start | bytes 2359304 | tf_op jit(solution)/shard_map/while/body/eval_jaxpr/ppermute | solution.py:632
  319.8 15.1 %collective-permute-start.3 = (bf16[2,256,768]{1,2,0:T(8,128)(2,1)}, bf16[2,256,768]{1,2,0:T(8,128)(2,1)}, u32[]{:S(2)}, u32[]{:S(2)}) collective-permute-start(bf16[2,256,768]{1,2,0:T(8,128)(2,1)} %fusion.112), channel_id=1, source_target_pairs={{0,2},{2,4},{4,6},{6,0},{1,3},{3,5},{5,7},{7,1},{8,10},{10,12},{12... | collective-permute-start | bytes 2359304 | tf_op jit(solution)/shard_map/while/body/eval_jaxpr/ppermute | solution.py:632
  319.8 23.5 %collective-permute-start = (bf16[2,256,768]{1,2,0:T(8,128)(2,1)}, bf16[2,256,768]{1,2,0:T(8,128)(2,1)}, u32[]{:S(2)}, u32[]{:S(2)}) collective-permute-start(bf16[2,256,768]{1,2,0:T(8,128)(2,1)} %copy.102), channel_id=1, source_target_pairs={{0,2},{2,4},{4,6},{6,0},{1,3},{3,5},{5,7},{7,1},{8,10},{10,12},{12... | collective-permute-start | bytes 2359304 | tf_op jit(solution)/shard_map/while/body/eval_jaxpr/ppermute | solution.py:632
  320.8 30.9 %collective-permute-start.1 = (bf16[2,256,768]{1,2,0:T(8,128)(2,1)}, bf16[2,256,768]{1,2,0:T(8,128)(2,1)}, u32[]{:S(2)}, u32[]{:S(2)}) collective-permute-start(bf16[2,256,768]{1,2,0:T(8,128)(2,1)} %copy.103), channel_id=1, source_target_pairs={{0,2},{2,4},{4,6},{6,0},{1,3},{3,5},{5,7},{7,1},{8,10},{10,12},{12... | collective-permute-start | bytes 2359304 | tf_op jit(solution)/shard_map/while/body/eval_jaxpr/ppermute | solution.py:632
  324.3 27.3 %copy-start.1 = (bf16[2,256,12,64]{1,3,2,0:T(8,128)(2,1)S(1)}, bf16[2,256,12,64]{1,3,2,0:T(8,128)(2,1)}, u32[]{:S(2)}) copy-start(bf16[2,256,12,64]{1,3,2,0:T(8,128)(2,1)} %copy-done) | copy-start | bytes 2359300 | tf_op jit(solution)/shard_map/while
  (43 other events, 178.8 us)

commit v3 on v1

--- a/solution.py
+++ b/solution.py
@@ -337,7 +337,7 @@
     )
 
 
-def body(
+def general_body(
     tokens,
     cotangent,
     lengths,
@@ -606,9 +606,1066 @@
     )
 
 
+HW = 64
+QT = 256
+
+
+def remote(src, dst, ss, rs, dev):
+    return pltpu.make_async_remote_copy(src_ref=src, dst_ref=dst, send_sem=ss, recv_sem=rs, device_id=dev, device_id_type=MESH)
+
+
+def nt(a, b):
+    return lax.dot_general(a, b, (((1,), (1,)), ((), ())), preferred_element_type=F32)
+
+
+def mm(a, b):
+    return jnp.dot(a, b, preferred_element_type=F32)
+
+
+def head_masks(rows):
+    lane = lax.broadcasted_iota(jnp.int32, (rows, 2 * HW), 1)
+    return lane < HW
+
+
+def normal_parts(v):
+    mean = jnp.mean(v, -1, keepdims=True)
+    cen = v - mean
+    inv = lax.rsqrt(jnp.mean(cen * cen, -1, keepdims=True) + EPSILON)
+    return cen * inv, inv
+
+
+def normal_back(dn, hat, inv, gain):
+    d = dn * gain
+    return inv * (d - jnp.mean(d, -1, keepdims=True) - hat * jnp.mean(d * hat, -1, keepdims=True))
+
+
+def gelu_pair(u):
+    w = jnp.abs(u)
+    t = 1.0 / (1.0 + (0.3275911 * math.sqrt(0.5)) * w)
+    e = jnp.exp(-0.5 * u * u)
+    poly = t * (0.127414796 + t * (-0.142248368 + t * (0.7107068705 + t * (-0.7265760135 + t * 0.5307027145))))
+    tail = poly * e
+    phi = jnp.where(u < 0.0, tail, 1.0 - tail)
+    return u * phi, phi + u * (e * (1.0 / math.sqrt(2.0 * math.pi)))
+
+
+def fold8(v):
+    return jnp.sum(v.reshape(v.shape[0] // 8, 8, v.shape[1]), 0)
+
+
+def fwd_kernel(nx, seqs, seq_rows, lens, tok, cot, sq, so_, su, sd, *rest):
+    small = rest[:9]
+    (qkv_o, att_o, lse_o, wq_o, wo_o, wu_o, wd_o, vec_o, y_o, dh_o, hat_o, act_o, gp_o, vg_o) = rest[9:23]
+    (XT, WB, QKV, CT, ATT, LSE, H1, N1, N1B, ACT, GP, YB,
+               ls, ys, yr, zs, zr, as_, ar, bs, br, t0s, t0r, t1s, t1r, t2s, t2r, vs, vr, lts, outs) = rest[23:]
+    core, x, f, z = places()
+    me = x * 2 + core
+    nblk = 2 * nx
+    rows = seqs * seq_rows
+    sib = {"ctx": x * 2 + 1 - core}
+    yp = {"fsdp": 1 - f}
+    zp = {"dp": z + 1 - 2 * lax.rem(z, 2)}
+    zb = lax.rem(z, 2)
+    xts = [lax.rem(x + j, nx) for j in range(1, nx)]
+    xps = [{"ctx": t * 2 + core} for t in xts]
+    xsrc = [lax.rem(x + nx - j, nx) * 2 + core for j in range(1, nx)]
+    peers = [sib, yp, zp] + xps
+    bar = pltpu.get_barrier_semaphore()
+    for p in peers:
+        pl.semaphore_signal(bar, inc=1, device_id=p, device_id_type=MESH)
+    order = (1, 2, 0)
+    PR = U // 4
+    piece = pl.multiple_of((zb * 2 + core) * PR, PR)
+    zpiece = pl.multiple_of(((1 - zb) * 2 + core) * PR, PR)
+    H = rows // 2
+
+    def shard(b, r0, n):
+        r = pl.ds(r0, n)
+        if b < 3:
+            return sq.at[r, pl.ds(b * 768, 768)]
+        if b == 3:
+            return so_.at[r, :]
+        if b < 8:
+            return su.at[r, pl.ds((b - 4) * 768, 768)]
+        return sd.at[pl.ds((b - 8) * U + r0, n), :]
+
+    def loc(b):
+        return pltpu.make_async_copy(shard(b, 0, U), WB.at[b, f], ls.at[b])
+
+    def ycp(b):
+        if not isinstance(b, int):
+            src = WB.at[b, f, pl.ds(piece, PR)]
+        else:
+            src = shard(b, piece, PR)
+        return remote(src, WB.at[b, f, pl.ds(piece, PR)], ys.at[b], yr.at[b], yp)
+
+    def zcp(b):
+        w = WB.at[b, 1 - f, pl.ds(piece, PR)]
+        return remote(w, w, zs.at[b], zr.at[b], zp)
+
+    def acp(b):
+        w = WB.at[b, 1 - f, pl.ds(piece, PR)]
+        return remote(w, w, as_.at[b], ar.at[b], sib)
+
+    def bcp(b):
+        w = WB.at[b, 1 - f, pl.ds(zpiece, PR)]
+        return remote(w, w, bs.at[b], br.at[b], sib)
+
+    def A(b):
+        ycp(b).wait_recv()
+        zcp(b).start()
+        acp(b).start()
+
+    def B(b):
+        zcp(b).wait_recv()
+        bcp(b).start()
+
+    def C(b):
+        acp(b).wait_recv()
+        bcp(b).wait_recv()
+
+    def tsl(h):
+        return pl.ds(h * H, H)
+
+    def t_sib(h):
+        return remote(tok.at[tsl(h)], XT.at[me, tsl(h)], t0s.at[h], t0r.at[h], sib)
+
+    def t_x(j, h):
+        return remote(tok.at[tsl(h)], XT.at[me, tsl(h)], t1s.at[j - 1, h], t1r.at[j - 1, h], xps[j - 1])
+
+    def t_f(j, h):
+        w = XT.at[xsrc[j - 1], tsl(h)]
+        return remote(w, w, t2s.at[j - 1, h], t2r.at[j - 1, h], sib)
+
+    vcp = remote(vec_o.at[f], vec_o.at[f], vs.at[0], vr.at[0], yp)
+    tl = pltpu.make_async_copy(tok, XT.at[me], lts.at[0])
+    tl.start()
+    for b in order:
+        loc(b).start()
+    row = 0
+    for v in small:
+        for i in range(v.shape[1] // U):
+            vec_o[f, row:row + 1, :] = v[:, i * U:(i + 1) * U].astype(F32)
+            row += 1
+    tc = pltpu.make_async_copy(cot, CT, lts.at[1])
+    pl.semaphore_wait(bar, len(peers))
+    vcp.start()
+    for b in order:
+        ycp(b).start()
+    for h in range(2):
+        for j in range(1, nx):
+            t_x(j, h).start()
+        t_sib(h).start()
+    for b in range(3, 12):
+        ycp(b).start()
+    for b in range(3, 12):
+        loc(b).start()
+    tc.start()
+    tl.wait()
+
+    def qkv(b, blk):
+        fac = 0.125 if b == 0 else 1.0
+
+        def one(t, _):
+            c = pl.ds(pl.multiple_of(t * 256, 256), 256)
+            w = WB[b, :, :, c].reshape(768, 256)
+            QKV[b, blk, :, c] = mm(XT[blk], w).astype(BF16)
+            return 0
+        if b == 1:
+            lax.fori_loop(0, 3, one, 0)
+        else:
+            row = 0 if b == 0 else 1
+            for t in range(3):
+                w = WB[b, :, :, t * 256:(t + 1) * 256].reshape(768, 256)
+                if t == 0:
+                    bias = vec_o[0, row:row + 1, 0:256]
+                elif t == 1:
+                    bias = jnp.concatenate([vec_o[0, row:row + 1, 256:384], vec_o[1, row:row + 1, 0:128]], 1)
+                else:
+                    bias = vec_o[1, row:row + 1, 128:384]
+                r = (mm(XT[blk], w) + bias).astype(BF16)
+                if b == 0:
+                    r = r * jnp.asarray(fac, BF16)
+                QKV[b, blk, :, t * 256:(t + 1) * 256] = r
+
+    seq = list(order)
+    A(seq[0])
+    A(seq[1])
+    B(seq[0])
+    for h in range(2):
+        t_sib(h).wait_recv()
+    A(seq[2])
+    B(seq[1])
+    vcp.wait_recv()
+    for n, b in enumerate(seq):
+        loc(b).wait()
+        C(b)
+
+        def both(i, _):
+            qkv(b, x * 2 + i)
+            return 0
+        lax.fori_loop(0, 2, both, 0)
+        if n == 0:
+            B(seq[2])
+            A(3)
+        if n == 1:
+            B(3)
+            A(4)
+    for j in range(1, nx):
+        for h in range(2):
+            t_x(j, h).wait_recv()
+            t_f(j, h).start()
+    B(4)
+    A(5)
+    for j in range(1, nx):
+        for h in range(2):
+            t_f(j, h).wait_recv()
+        base = lax.rem(x + nx - j, nx) * 2
+
+        def pair(i, _):
+            for b in seq:
+                qkv(b, base + i)
+            return 0
+        lax.fori_loop(0, 2, pair, 0)
+    B(5)
+    qo = pltpu.make_async_copy(QKV, qkv_o, outs.at[0])
+    qo.start()
+
+    low_half = head_masks(QT)
+    lane128 = lax.broadcasted_iota(jnp.int32, (QT, 128), 1)
+    kpos = lax.broadcasted_iota(jnp.int32, (QT, QT), 1)
+    nr = seq_rows // QT
+
+    def attend(tile, j):
+        s0 = tile // nr
+        qr = pl.ds(pl.multiple_of(tile * QT, QT), QT)
+        cols = pl.ds(pl.multiple_of(j * 128, 128), 128)
+        q = QKV[0, me, qr, cols]
+        length = lens[s0]
+        outs_ = []
+        tot = LSE[qr, 0:128]
+        for h in range(2):
+            qh = jnp.where(low_half == (h == 0), q, jnp.zeros_like(q))
+            sc = []
+            mx = None
+            for blk in range(nblk):
+                for r in range(nr):
+                    kr = pl.ds(pl.multiple_of(s0 * seq_rows + r * QT, QT), QT)
+                    v = nt(qh, QKV[1, blk, kr, cols])
+                    v = jnp.where(kpos < length - (blk * seq_rows + r * QT), v, MASKED)
+                    sc.append(v)
+                    mx = v if mx is None else jnp.maximum(mx, v)
+            m = jnp.max(mx, 1, keepdims=True)
+            acc = None
+            lsum = None
+            i = 0
+            for blk in range(nblk):
+                for r in range(nr):
+                    kr = pl.ds(pl.multiple_of(s0 * seq_rows + r * QT, QT), QT)
+                    p = jnp.exp(sc[i] - m)
+                    i += 1
+                    lsum = p if lsum is None else lsum + p
+                    o = mm(p.astype(BF16), QKV[2, blk, kr, cols])
+                    acc = o if acc is None else acc + o
+            den = jnp.sum(lsum, 1, keepdims=True)
+            outs_.append(acc / den)
+            tot = jnp.where(lane128 == 2 * j + h, m + jnp.log(den), tot)
+        ATT[qr, cols] = jnp.where(low_half, outs_[0], outs_[1])
+        LSE[qr, 0:128] = tot
+
+    ntile = rows // QT
+    per = ntile * 6 // 4
+
+    def group(g, _):
+        A(6 + g)
+
+        def one(i, _):
+            it = g * per + i
+            attend(it // 6, lax.rem(it, 6))
+            return 0
+        lax.fori_loop(0, per, one, 0)
+        B(6 + g)
+        return 0
+    lax.fori_loop(0, 4, group, 0)
+    A(10)
+    extra = []
+
+    def send_out(src, dst):
+        cp = pltpu.make_async_copy(src, dst, outs.at[25 + len(extra)])
+        cp.start()
+        extra.append(cp)
+
+    def full(b):
+        res = []
+        for ff in range(2):
+            src = WB.at[b, ff]
+            if b < 3:
+                dst = wq_o.at[pl.ds(ff * U, U), pl.ds(b * 768, 768)]
+            elif b == 3:
+                dst = wo_o.at[pl.ds(ff * U, U), :]
+            elif b < 8:
+                dst = wu_o.at[pl.ds(ff * U, U), pl.ds((b - 4) * 768, 768)]
+            else:
+                dst = wd_o.at[pl.ds(ff * 1536 + (b - 8) * U, U), :]
+            res.append(pltpu.make_async_copy(src, dst, outs.at[1 + 2 * b + ff]))
+        return res
+
+    def ready(b):
+        loc(b).wait()
+        C(b)
+        for cp in full(b):
+            cp.start()
+
+    def vector(r):
+        return jnp.concatenate([vec_o[0, r:r + 1, :], vec_o[1, r:r + 1, :]], 1)
+
+    for b in range(3):
+        for cp in full(b):
+            cp.start()
+    send_out(ATT, att_o)
+    ready(3)
+    bo = vector(2)
+    for t in range(3):
+        cs = slice(t * 256, (t + 1) * 256)
+        w = WB[3, :, :, cs].reshape(768, 256)
+        H1[:, cs] = XT[me, :, cs].astype(F32) + mm(ATT[...].astype(BF16), w) + bo[:, cs]
+    g1, s1 = vector(3), vector(4)
+    RB = 64
+
+    def ln1(i, _):
+        r = pl.ds(pl.multiple_of(i * RB, RB), RB)
+        hat, inv = normal_parts(H1[r, :])
+        H1[r, :] = hat
+        n = hat * g1 + s1
+        N1[r, :] = n
+        N1B[r, :] = n.astype(BF16)
+        LSE[r, 128:256] = jnp.broadcast_to(inv, (RB, 128))
+        return 0
+    lax.fori_loop(0, rows // RB, ln1, 0)
+    send_out(H1, hat_o)
+    send_out(LSE, lse_o)
+    A(11)
+    B(10)
+    for b in range(4, 8):
+        ready(b)
+
+    def upblock(b, _):
+        bias = jnp.concatenate([vec_o[b // 2, pl.ds(5 + lax.rem(b, 2) * 2, 1), :], vec_o[b // 2, pl.ds(6 + lax.rem(b, 2) * 2, 1), :]], 1)
+        for t in range(3):
+            w = WB[4 + b, :, :, t * 256:(t + 1) * 256].reshape(768, 256)
+            cs = pl.ds(pl.multiple_of(b * 768 + t * 256, 256), 256)
+            act, gp = gelu_pair(mm(N1B[...], w) + bias[:, t * 256:(t + 1) * 256])
+            ACT[:, cs] = act.astype(BF16)
+            GP[:, cs] = gp
+        return 0
+    lax.fori_loop(0, 2, upblock, 0)
+    B(11)
+    lax.fori_loop(2, 4, upblock, 0)
+    send_out(ACT, act_o)
+    send_out(GP, gp_o)
+    for b in range(8, 12):
+        ready(b)
+    bd = vector(9)
+    for t in range(3):
+        cs = slice(t * 256, (t + 1) * 256)
+        acc = N1[:, cs] + bd[:, cs]
+        for ff in range(2):
+            acc = acc + mm(ACT[:, ff * 1536:(ff + 1) * 1536], WB[8:12, ff, :, cs].reshape(1536, 256))
+        N1[:, cs] = acc
+    g2, s2 = vector(10), vector(11)
+    tc.wait()
+
+    def ln2(i, carry):
+        r = pl.ds(pl.multiple_of(i * RB, RB), RB)
+        hat, inv = normal_parts(N1[r, :])
+        YB[r, :] = (hat * g2 + s2).astype(BF16)
+        g = CT[r, :].astype(F32)
+        N1[r, :] = normal_back(g, hat, inv, g2)
+        return carry[0] + fold8(g * hat), carry[1] + fold8(g)
+    zero = jnp.zeros((8, 768), F32)
+    a0, a1 = lax.fori_loop(0, rows // RB, ln2, (zero, zero))
+    send_out(YB, y_o)
+    send_out(N1, dh_o)
+    vg_o[0:1, :] = jnp.sum(a0, 0, keepdims=True)
+    vg_o[1:2, :] = jnp.sum(a1, 0, keepdims=True)
+    vcp.wait_send()
+    qo.wait()
+    for b in range(12):
+        ycp(b).wait_send()
+        zcp(b).wait_send()
+        acp(b).wait_send()
+        bcp(b).wait_send()
+        for cp in full(b):
+            cp.wait()
+    for h in range(2):
+        t_sib(h).wait_send()
+        for j in range(1, nx):
+            t_x(j, h).wait_send()
+            t_f(j, h).wait_send()
+    for cp in extra:
+        cp.wait()
+
+
+def forward_gather(lens, tok, cot, sq, so_, su, sd, small, nx, cid):
+    seqs, seq_rows, d = tok.shape
+    rows = seqs * seq_rows
+    nblk = 2 * nx
+    anyspec = pl.BlockSpec(memory_space=pl.ANY)
+    vspec = pl.BlockSpec(memory_space=pltpu.VMEM)
+    sspec = pl.BlockSpec(memory_space=pltpu.SMEM)
+    D = pltpu.SemaphoreType.DMA
+    V = pltpu.VMEM
+    S = jax.ShapeDtypeStruct
+    sems = [D((12,))] * 9 + [D((2,)), D((2,))] + [D((nx - 1, 2))] * 4 + [D((1,)), D((1,)), D((2,)), D((33,))]
+    return pl.pallas_call(
+        functools.partial(fwd_kernel, nx, seqs, seq_rows),
+        out_shape=(S((3, nblk, rows, d), BF16), S((rows, d), F32), S((rows, 256), F32),
+                   S((768, 2304), BF16), S((768, 768), BF16), S((768, 3072), BF16), S((3072, 768), BF16),
+                   S((2, 12, U), F32), S((rows, d), BF16), S((rows, d), F32), S((rows, d), F32),
+                   S((rows, 3072), BF16), S((rows, 3072), F32), S((2, d), F32)),
+        in_specs=[sspec] + [anyspec] * 6 + [vspec] * 9,
+        out_specs=(anyspec,) * 7 + (vspec,) + (anyspec,) * 5 + (vspec,),
+        scratch_shapes=[V((nblk, rows, d), BF16), V((12, 2, U, 768), BF16), V((3, nblk, rows, d), BF16),
+                        V((rows, d), BF16), V((rows, d), F32), V((rows, 256), F32), V((rows, d), F32), V((rows, d), F32),
+                        V((rows, d), BF16), V((rows, 3072), BF16), V((rows, 3072), F32), V((rows, d), BF16)] + sems,
+        compiler_params=pltpu.CompilerParams(collective_id=cid, has_side_effects=True, vmem_limit_bytes=62 << 20),
+        name="forward_gather",
+    )(lens, tok.reshape(rows, d), cot.reshape(rows, d), sq, so_, su, sd, *[v.reshape(1, -1) for v in small])
+
+
+def tn(a, b):
+    return lax.dot_general(a, b, (((0,), (0,)), ((), ())), preferred_element_type=F32)
+
+
+def colsum(v):
+    return jnp.sum(fold8(v), 0, keepdims=True)
+
+
+def bwd_kernel(nx, nd, seqs, seq_rows, lens, vec, vg, qkv_i, att_i, lse_i, wq_i, wo_i, wu_i, wd_i, dh_i, hat_i, act_i, gp_i, tok_i,
+               od, ou, oo, oq, ov, gin_o,
+               BIG, WO, WQ, GP, ACT, DH, DM, HAT, NB, DO, ROWS, COLS, DQKV, L, SB, R1, R2, R3, R4, AX, VV, V0, VX, VZ,
+               lds, d0s, d0r, d1s, d1r, d2s, d2r, s1s, s1r, s2s, s2r, s3s, s3r, s4s, s4r, s5s, s5r, s6s, s6r, s7s, s7r, s8, vs, vr):
+    core, x, f, z = places()
+    me = x * 2 + core
+    nblk = 2 * nx
+    rows = seqs * seq_rows
+    CX, PZ = U // nx, U // nx // nd
+    NCH = 12
+    sib = {"ctx": x * 2 + 1 - core}
+    yp = {"fsdp": 1 - f}
+    xps = [{"ctx": lax.rem(x + j, nx) * 2 + core} for j in range(1, nx)]
+    xsrc = [lax.rem(x + nx - j, nx) * 2 + core for j in range(1, nx)]
+    zps = [{"dp": lax.rem(z + j, nd)} for j in range(1, nd)]
+    peers = [sib, yp] + xps + zps
+    bar = pltpu.get_barrier_semaphore()
+    for p in peers:
+        pl.semaphore_signal(bar, inc=1, device_id=p, device_id_type=MESH)
+
+    loads = {}
+
+    def load(name, src, dst):
+        cp = pltpu.make_async_copy(src, dst, lds.at[len(loads)])
+        cp.start()
+        loads[name] = cp
+
+    load("dh", dh_i, DH)
+    load("act", act_i, ACT)
+    load("wd", wd_i, BIG.at[pl.ds(0, 3072)])
+    load("gp0", gp_i.at[:, pl.ds(0, 768)], GP.at[0])
+    load("hat", hat_i, HAT)
+    load("gp1", gp_i.at[:, pl.ds(768, 768)], GP.at[1])
+    for b in range(4):
+        load(("wu", b), wu_i.at[:, pl.ds(b * 768, 768)], BIG.at[pl.ds(3072 + b * 768, 768)])
+    load("lse", lse_i, COLS.at[:, pl.ds(0, 256)])
+    load("wo", wo_i, WO)
+    for b in range(3):
+        load(("wq", b), wq_i.at[:, pl.ds(b * 768, 768)], WQ.at[b])
+
+    def vector(r):
+        return jnp.concatenate([vec[0, r:r + 1, :], vec[1, r:r + 1, :]], 1)
+
+    def c1(i, ff, k):
+        return remote(SB.at[i % 4, ff], R1.at[i, ff], s1s.at[i, k], s1r.at[i, k], sib)
+
+    def c1s(i):
+        return [c1(i, 1 - f, 0), c1(i, f, 1)]
+
+    def c2(c):
+        return remote(L.at[c, 1 - f], R2.at[c], s2s.at[c], s2r.at[c], yp)
+
+    def c3(c, j):
+        xt = lax.rem(x + j, nx)
+        return remote(L.at[c, f, pl.ds(pl.multiple_of(xt * CX, CX), CX)], R3.at[c, j - 1], s3s.at[c, j - 1], s3r.at[c, j - 1], xps[j - 1])
+
+    def mine(zz):
+        return pl.ds(pl.multiple_of(x * CX + zz * PZ, PZ), PZ)
+
+    def c4(c, j):
+        zt = lax.rem(z + j, nd)
+        return remote(L.at[c, f, mine(zt)], R4.at[c, j - 1], s4s.at[c, j - 1], s4r.at[c, j - 1], zps[j - 1])
+
+    def c5(c, j):
+        w = AX.at[c, mine(z)]
+        return remote(w, w, s5s.at[c, j - 1], s5r.at[c, j - 1], zps[j - 1])
+
+    def c6(c, j):
+        w = AX.at[c, pl.ds(pl.multiple_of(x * CX, CX), CX)]
+        return remote(w, w, s6s.at[c, j - 1], s6r.at[c, j - 1], xps[j - 1])
+
+    def orect(i):
+        if i < 4:
+            return od.at[pl.ds(pl.multiple_of(core * 768 + i // 2 * U, U), U), pl.ds(i % 2 * U, U)]
+        if i < 8:
+            return ou.at[:, pl.ds(pl.multiple_of(core * 1536 + (i - 4) * U, 128), U)]
+        if i < 9:
+            return oo.at[:, pl.ds(pl.multiple_of(core * U, 128), U)]
+        return oq.at[:, pl.ds(pl.multiple_of(core * 1152 + (i - 9) * U, 128), U)]
+
+    def c7(c):
+        return remote(AX.at[c], orect(c), s7s.at[c], s7r.at[c], sib)
+
+    def c8(c):
+        return pltpu.make_async_copy(AX.at[c], orect(c), s8.at[c])
+
+    B = 48
+
+    def rows_loop(n, fn):
+        def bodyf(i, _):
+            fn(pl.multiple_of(i * B, B))
+            return 0
+        lax.fori_loop(0, n // B, bodyf, 0)
+
+    def up(v):
+        return v.astype(F32)
+
+    def st1(i):
+        for cp in c1s(i):
+            cp.start()
+
+    def st2(c):
+        c1(c, 1 - f, 0).wait_recv()
+
+        def fn(r):
+            s = pl.ds(r, B)
+            L[c, 1 - f, s, :] = (up(L[c, 1 - f, s, :]) + up(R1[c, 1 - f, s, :])).astype(BF16)
+        rows_loop(U, fn)
+        c2(c).start()
+
+    def st3(c):
+        c1(c, f, 1).wait_recv()
+        c2(c).wait_recv()
+        for j in range(1, nx):
+            xt = lax.rem(x + j, nx)
+
+            def fn(r):
+                s = pl.ds(pl.multiple_of(xt * CX + r, B), B)
+                L[c, f, s, :] = (up(L[c, f, s, :]) + up(R1[c, f, s, :]) + up(R2[c, s, :])).astype(BF16)
+            rows_loop(CX, fn)
+            c3(c, j).start()
+
+    def st4(c):
+        for j in range(1, nx):
+            c3(c, j).wait_recv()
+
+        def fn(r):
+            s = pl.ds(pl.multiple_of(x * CX + r, B), B)
+            t = up(L[c, f, s, :]) + up(R1[c, f, s, :]) + up(R2[c, s, :])
+            for j in range(1, nx):
+                t = t + up(R3[c, j - 1, pl.ds(r, B), :])
+            L[c, f, s, :] = t.astype(BF16)
+        rows_loop(CX, fn)
+        for j in range(1, nd):
+            c4(c, j).start()
+
+    def st5(c):
+        for j in range(1, nd):
+            c4(c, j).wait_recv()
+        t = up(L[c, f, mine(z), :])
+        for j in range(1, nd):
+            t = t + up(R4[c, j - 1])
+        AX[c, mine(z), :] = t.astype(BF16)
+        for j in range(1, nd):
+            c5(c, j).start()
+
+    def st6(c):
+        for j in range(1, nd):
+            c5(c, j).wait_recv()
+        for j in range(1, nx):
+            c6(c, j).start()
+
+    def st7(c):
+        for j in range(1, nx):
+            c6(c, j).wait_recv()
+        c7(c).start()
+        c8(c).start()
+
+    def tick(c):
+        stages = ((4, st7), (3, st6), (2, st5), (1, st4), (0, st3))
+        if isinstance(c, int):
+            for lag, fn in stages:
+                if 0 <= c - lag < NCH:
+                    fn(c - lag)
+        else:
+            for lag, fn in stages[1:]:
+                if lag == 0:
+                    fn(c)
+                else:
+                    @pl.when(c >= lag)
+                    def _():
+                        fn(c - lag)
+
+    def v_core():
+        return remote(VV, V0.at[0], vs.at[0], vr.at[0], sib)
+
+    def v_y():
+        return remote(V0.at[1], V0.at[2], vs.at[1], vr.at[1], yp)
+
+    def v_x(j):
+        return remote(VX.at[x], VX.at[x], vs.at[1 + j], vr.at[1 + j], xps[j - 1])
+
+    def v_z(j):
+        return remote(VZ.at[z], VZ.at[z], vs.at[nx + j], vr.at[nx + j], zps[j - 1])
+
+    def vst(k):
+        if k == 0:
+            v_core().start()
+        elif k == 1:
+            v_core().wait_recv()
+            V0[1] = VV[...] + V0[0]
+            v_y().start()
+        elif k == 2:
+            v_y().wait_recv()
+            VX[x] = V0[1] + V0[2]
+            for j in range(1, nx):
+                v_x(j).start()
+        elif k == 3:
+            for j in range(1, nx):
+                v_x(j).wait_recv()
+            t = VX[0]
+            for j in range(1, nx):
+                t = t + VX[j]
+            VZ[z] = t
+            for j in range(1, nd):
+                v_z(j).start()
+        elif k == 4:
+            for j in range(1, nd):
+                v_z(j).wait_recv()
+            t = VZ[0]
+            for j in range(1, nd):
+                t = t + VZ[j]
+            VV2 = t
+            for r, n, o in ((0, 1, 0), (2, 1, 1), (4, 1, 2), (6, 1, 3), (8, 1, 4), (10, 4, 5), (18, 1, 9), (20, 1, 10), (22, 1, 11)):
+                ov[o:o + n, :] = jnp.where(f == 0, VV2[r:r + n, :], VV2[r + n:r + 2 * n, :])
+
+    def put_vec(r, v):
+        VV[r:r + 1, :] = v[:, :U]
+        VV[r + 1:r + 2, :] = v[:, U:]
+
+    put_vec(20, vg[0:1, :])
+    put_vec(22, vg[1:2, :])
+
+    RB = 64
+    loads["dh"].wait()
+
+    def to_dm(i, acc):
+        r = pl.ds(pl.multiple_of(i * RB, RB), RB)
+        v = DH[r, :].astype(BF16)
+        DM[r, :] = v
+        return acc + fold8(v.astype(F32))
+    zero = jnp.zeros((8, 768), F32)
+    put_vec(18, jnp.sum(lax.fori_loop(0, rows // RB, to_dm, zero), 0, keepdims=True))
+    loads["act"].wait()
+
+    def fill(i0, kk, ff, val, wide):
+        v = val.astype(BF16)
+        for t in range(wide):
+            if kk == 0:
+                L[i0 + t, ff] = v[:, t * U:(t + 1) * U]
+            else:
+                SB[(i0 + t) % 4, ff] = v[:, t * U:(t + 1) * U]
+
+    def each_f(fn):
+        def one(k, _):
+            fn(jnp.where(k == 0, 1 - f, f))
+            return 0
+        lax.fori_loop(0, 2, one, 0)
+
+    def ccof(kk):
+        return core if kk == 0 else 1 - core
+
+    for ii in range(2):
+        for kk in (1, 0):
+            def wdown(ff, kk=kk, ii=ii):
+                h = pl.multiple_of(ff * 1536 + ccof(kk) * 768 + ii * U, U)
+                fill(2 * ii, kk, ff, tn(ACT[:, pl.ds(h, U)], DM[...]), 2)
+            each_f(wdown)
+            if kk == 1:
+                if ii == 0:
+                    pl.semaphore_wait(bar, len(peers))
+                st1(2 * ii)
+                st1(2 * ii + 1)
+    st2(0)
+    st2(1)
+    loads["wd"].wait()
+    for b in range(4):
+        loads["gp%d" % b].wait()
+        for t in range(3):
+            h = b * 768 + t * 256
+            du = (nt(DM[...], BIG[h:h + 256, :]) * GP[b % 2, :, t * 256:(t + 1) * 256]).astype(BF16)
+            ACT[:, h:h + 256] = du
+            s = colsum(du.astype(F32))
+            for q in range(2):
+                o = h + q * 128
+                VV[10 + o // U:11 + o // U, o % U:o % U + 128] = s[:, q * 128:(q + 1) * 128]
+        if b < 2:
+            load("gp%d" % (b + 2), gp_i.at[:, pl.ds((b + 2) * 768, 768)], GP.at[b % 2])
+        if b == 1:
+            st2(2)
+    st2(3)
+    loads["hat"].wait()
+    g1, s1 = vector(3), vector(4)
+
+    def to_nb(i, _):
+        r = pl.ds(pl.multiple_of(i * RB, RB), RB)
+        NB[r, :] = (HAT[r, :] * g1 + s1).astype(BF16)
+        return 0
+    lax.fori_loop(0, rows // RB, to_nb, 0)
+    for ii in range(2):
+        for kk in (1, 0):
+            if kk == 1:
+                for i in (2 * ii, 2 * ii + 1):
+                    for cp in c1s(i):
+                        cp.wait_send()
+
+            def wup(ff, kk=kk, ii=ii):
+                h = pl.multiple_of(ccof(kk) * 1536 + ii * 768, 768)
+                fill(4 + 2 * ii, kk, ff, tn(NB[:, pl.ds(pl.multiple_of(ff * U, U), U)], ACT[:, pl.ds(h, 768)]), 2)
+            each_f(wup)
+            if kk == 1:
+                st1(4 + 2 * ii)
+                st1(5 + 2 * ii)
+    load("tok", tok_i, NB)
+    for b in range(4):
+        loads[("wu", b)].wait()
+    for t in range(3):
+        cs = slice(t * 256, (t + 1) * 256)
+        acc = DH[:, cs]
+        for b in range(4):
+            acc = acc + nt(ACT[:, b * 768:(b + 1) * 768], BIG[3072 + b * 768 + t * 256:3072 + b * 768 + (t + 1) * 256, :])
+        DH[:, cs] = acc
+    for k in (1, 2, 0):
+        for blk in range(nblk):
+            load(("qkv", k, blk), qkv_i.at[k, blk], BIG.at[pl.ds((k * nblk + blk) * rows, rows)])
+    st2(4)
+    st2(5)
+    loads["lse"].wait()
+
+    def ln1(i, carry):
+        r = pl.ds(pl.multiple_of(i * RB, RB), RB)
+        dn, hat = DH[r, :], HAT[r, :]
+        d = normal_back(dn, hat, COLS[r, 128:129], g1)
+        DH[r, :] = d
+        da = d.astype(BF16)
+        DM[r, :] = da
+        return carry[0] + fold8(dn * hat), carry[1] + fold8(dn), carry[2] + fold8(da.astype(F32))
+    sums = lax.fori_loop(0, rows // RB, ln1, (zero, zero, zero))
+    for row, sv in zip((6, 8, 4), sums):
+        put_vec(row, jnp.sum(sv, 0, keepdims=True))
+    load("att", att_i, HAT)
+    loads["wo"].wait()
+    for t in range(3):
+        DO[me, :, t * 256:(t + 1) * 256] = nt(DM[...], WO[t * 256:(t + 1) * 256, :]).astype(BF16)
+
+    def d_sib():
+        return remote(DO.at[me], DO.at[me], d0s.at[0], d0r.at[0], sib)
+
+    def d_x(j):
+        return remote(DO.at[me], DO.at[me], d1s.at[j - 1, 0], d1r.at[j - 1, 0], xps[j - 1])
+
+    def d_f(j):
+        w = DO.at[xsrc[j - 1]]
+        return remote(w, w, d2s.at[j - 1, 0], d2r.at[j - 1, 0], sib)
+
+    def r_sib():
+        return remote(ROWS.at[me], ROWS.at[me], d0s.at[1], d0r.at[1], sib)
+
+    def r_x(j):
+        return remote(ROWS.at[me], ROWS.at[me], d1s.at[j - 1, 1], d1r.at[j - 1, 1], xps[j - 1])
+
+    def r_f(j):
+        w = ROWS.at[xsrc[j - 1]]
+        return remote(w, w, d2s.at[j - 1, 1], d2r.at[j - 1, 1], sib)
+
+    for j in range(1, nx):
+        d_x(j).start()
+    d_sib().start()
+    loads["att"].wait()
+    for kk in (1, 0):
+        if kk == 1:
+            for cp in c1s(4):
+                cp.wait_send()
+
+        def wout(ff, kk=kk):
+            a = HAT[:, pl.ds(pl.multiple_of(ff * U, U), U)].astype(BF16)
+            fill(8, kk, ff, tn(a, DM[:, pl.ds(pl.multiple_of(ccof(kk) * U, U), U)]), 1)
+        each_f(wout)
+        if kk == 1:
+            st1(8)
+    head = lax.broadcasted_iota(jnp.int32, (768, 128), 0) // HW
+    pick = (head == lax.broadcasted_iota(jnp.int32, (768, 128), 1)).astype(BF16)
+
+    def delta(i, _):
+        r = pl.ds(pl.multiple_of(i * 128, 128), 128)
+        v = DO[me, r, :].astype(F32) * HAT[r, :]
+        hi = v.astype(BF16)
+        rest = v - hi.astype(F32)
+        mid = rest.astype(BF16)
+        low = (rest - mid.astype(F32)).astype(BF16)
+        d = mm(hi, pick) + mm(mid, pick) + mm(low, pick)
+        COLS[r, 128:256] = d
+        ROWS[me, 16:32, r] = jnp.transpose(d)[0:16, :]
+        ROWS[me, 0:16, r] = jnp.transpose(COLS[r, 0:128])[0:16, :]
+        return 0
+    lax.fori_loop(0, rows // 128, delta, 0)
+    for j in range(1, nx):
+        r_x(j).start()
+    r_sib().start()
+    st2(6)
+    st2(7)
+    st2(8)
+    tick(0)
+
+    for k in (1, 2, 0):
+        for blk in range(nblk):
+            loads[("qkv", k, blk)].wait()
+    low_half = head_masks(QT)
+    lane128 = lax.broadcasted_iota(jnp.int32, (QT, 128), 1)
+    kpos = lax.broadcasted_iota(jnp.int32, (QT, QT), 1)
+    krow = lax.broadcasted_iota(jnp.int32, (QT, 128), 0)
+    nr = seq_rows // QT
+    ntile = rows // QT
+
+    def big(k, blk, r0, cols):
+        return BIG[pl.ds(pl.multiple_of((k * nblk + blk) * rows + r0, QT), QT), cols]
+
+    def pick_col(v, h):
+        return jnp.sum(jnp.where(lane128 == h, v, 0.0), 1, keepdims=True)
+
+    def zero_other(v, h):
+        return jnp.where(low_half == (h == 0), v, jnp.zeros_like(v))
+
+    def dq_one(tile, j):
+        s0 = tile // nr
+        q0 = pl.multiple_of(tile * QT, QT)
+        qr = pl.ds(q0, QT)
+        cols = pl.ds(pl.multiple_of(j * 128, 128), 128)
+        q = big(0, me, q0, cols)
+        do = DO[me, qr, cols]
+        length = lens[s0]
+        res = []
+        for h in range(2):
+            qh, doh = zero_other(q, h), zero_other(do, h)
+            lse = pick_col(COLS[qr, 0:128], 2 * j + h)
+            dl = pick_col(COLS[qr, 128:256], 2 * j + h)
+            acc = None
+            for blk in range(nblk):
+                for r in range(nr):
+                    k0 = s0 * seq_rows + r * QT
+                    kt = big(1, blk, k0, cols)
+                    p = jnp.exp(nt(qh, kt) - lse)
+                    p = jnp.where(kpos < length - (blk * seq_rows + r * QT), p, 0.0)
+                    ds = (p * (nt(doh, big(2, blk, k0, cols)) - dl)).astype(BF16)
+                    o = mm(ds, kt)
+                    acc = o if acc is None else acc + o
+            res.append(acc)
+        DQKV[0, qr, cols] = (jnp.where(low_half, res[0], res[1]) * 0.125).astype(BF16)
+
+    def dkv_one(tile, j):
+        s0 = tile // nr
+        k0 = pl.multiple_of(tile * QT, QT)
+        kr = pl.ds(k0, QT)
+        cols = pl.ds(pl.multiple_of(j * 128, 128), 128)
+        k, v = big(1, me, k0, cols), big(2, me, k0, cols)
+        live = krow < lens[s0] - (me * seq_rows + (tile - s0 * nr) * QT)
+        resk, resv = [], []
+        for h in range(2):
+            kh, vh = zero_other(k, h), zero_other(v, h)
+            ak = av = None
+            for blk in range(nblk):
+                for r in range(nr):
+                    q0 = pl.multiple_of(s0 * seq_rows + r * QT, QT)
+                    qr = pl.ds(q0, QT)
+                    qt, dt = big(0, blk, q0, cols), DO[blk, qr, cols]
+                    lse = ROWS[blk, pl.ds(2 * j + h, 1), qr]
+                    dl = ROWS[blk, pl.ds(16 + 2 * j + h, 1), qr]
+                    p = jnp.exp(nt(kh, qt) - lse)
+                    ds = (p * (nt(vh, dt) - dl)).astype(BF16)
+                    ov_, ok_ = mm(p.astype(BF16), dt), mm(ds, qt)
+                    av = ov_ if av is None else av + ov_
+                    ak = ok_ if ak is None else ak + ok_
+            resk.append(ak)
+            resv.append(av)
+        DQKV[1, kr, cols] = jnp.where(live, jnp.where(low_half, resk[0], resk[1]), 0.0).astype(BF16)
+        DQKV[2, kr, cols] = jnp.where(live, jnp.where(low_half, resv[0], resv[1]), 0.0).astype(BF16)
+
+    def segment(fn, groups, first):
+        per = ntile * 6 // groups
+
+        def group(g, _):
+            def one(i, _):
+                it = g * per + i
+                fn(it // 6, lax.rem(it, 6))
+                return 0
+            lax.fori_loop(0, per, one, 0)
+            tick(first + g)
+            return 0
+        lax.fori_loop(0, groups, group, 0)
+
+    segment(dq_one, 2, 1)
+    for j in range(1, nx):
+        d_x(j).wait_recv()
+        d_f(j).start()
+        r_x(j).wait_recv()
+        r_f(j).start()
+    d_sib().wait_recv()
+    r_sib().wait_recv()
+    for j in range(1, nx):
+        d_f(j).wait_recv()
+        r_f(j).wait_recv()
+    segment(dkv_one, 3, 3)
+
+    loads["tok"].wait()
+    for kk in (1, 0):
+        if kk == 1:
+            for i in (5, 6, 7):
+                for cp in c1s(i):
+                    cp.wait_send()
+        for i in range(3):
+            def wqkv(ff, kk=kk, i=i):
+                p = ccof(kk) * 3 + i
+                a = NB[:, pl.ds(pl.multiple_of(ff * U, U), U)]
+                fill(9 + i, kk, ff, tn(a, DQKV[p // 2, :, pl.ds(pl.multiple_of(lax.rem(p, 2) * U, U), U)]), 1)
+            each_f(wqkv)
+            if kk == 1:
+                st1(9 + i)
+
+    def bias_sum(k):
+        def one(i, acc):
+            return acc + fold8(DQKV[k, pl.ds(pl.multiple_of(i * RB, RB), RB), :].astype(F32))
+        return jnp.sum(lax.fori_loop(0, rows // RB, one, zero), 0, keepdims=True)
+    st2(9)
+    st2(10)
+    st2(11)
+    put_vec(0, bias_sum(0))
+    put_vec(2, bias_sum(2))
+    vst(0)
+    tick(6)
+    vst(1)
+    for b in range(3):
+        loads[("wq", b)].wait()
+    for t in range(3):
+        cs = slice(t * 256, (t + 1) * 256)
+        acc = DH[:, cs]
+        for b in range(3):
+            acc = acc + nt(DQKV[b], WQ[b, cs, :])
+        DM[:, cs] = acc.astype(BF16)
+    gout = pltpu.make_async_copy(DM, gin_o, s8.at[NCH])
+    gout.start()
+    vst(2)
+    st7(0)
+    st7(1)
+    tick(7)
+    vst(3)
+    for c in range(8, NCH + 4):
+        tick(c)
+        if c == 8:
+            vst(4)
+    for c in range(NCH):
+        c2(c).wait_send()
+        c7(c).wait()
+        c8(c).wait()
+        for j in range(1, nx):
+            c3(c, j).wait_send()
+            c6(c, j).wait_send()
+        for j in range(1, nd):
+            c4(c, j).wait_send()
+            c5(c, j).wait_send()
+    for i in (8, 9, 10, 11):
+        for cp in c1s(i):
+            cp.wait_send()
+    gout.wait()
+    v_core().wait_send()
+    v_y().wait_send()
+    d_sib().wait_send()
+    r_sib().wait_send()
+    for j in range(1, nx):
+        v_x(j).wait_send()
+        d_x(j).wait_send()
+        d_f(j).wait_send()
+        r_x(j).wait_send()
+        r_f(j).wait_send()
+    for j in range(1, nd):
+        v_z(j).wait_send()
+
+
+def backward_reduce(lens, vec, vg, qkv, att, lse, wq, wo, wu, wd, dh, hat, act, gp, tok, nx, nd, seqs, cid):
+    rows, d = att.shape
+    nblk = 2 * nx
+    CX, PZ = U // nx, U // nx // nd
+    N = 12
+    anyspec = pl.BlockSpec(memory_space=pl.ANY)
+    vspec = pl.BlockSpec(memory_space=pltpu.VMEM)
+    sspec = pl.BlockSpec(memory_space=pltpu.SMEM)
+    D = pltpu.SemaphoreType.DMA
+    V = pltpu.VMEM
+    S = jax.ShapeDtypeStruct
+    sems = [D((32,)), D((2,)), D((2,))] + [D((nx - 1, 2))] * 4 + [D((N, 2)), D((N, 2)), D((N,)), D((N,)), D((N, nx - 1)), D((N, nx - 1)),
+            D((N, nd - 1)), D((N, nd - 1)), D((N, nd - 1)), D((N, nd - 1)), D((N, nx - 1)), D((N, nx - 1)),
+            D((N,)), D((N,)), D((N + 1,)), D((nx + nd,)), D((nx + nd,))]
+    return pl.pallas_call(
+        functools.partial(bwd_kernel, nx, nd, seqs, rows // seqs),
+        out_shape=(S((1536, 768), BF16), S((U, 3072), BF16), S((U, 768), BF16), S((U, 2304), BF16), S((12, U), F32), S((rows, d), BF16)),
+        in_specs=[sspec, vspec, vspec] + [anyspec] * 12,
+        out_specs=(anyspec,) * 4 + (vspec, anyspec),
+        scratch_shapes=[V((6144, d), BF16), V((d, d), BF16), V((3, d, d), BF16), V((2, rows, d), F32), V((rows, 3072), BF16),
+                        V((rows, d), F32), V((rows, d), BF16), V((rows, d), F32), V((rows, d), BF16), V((nblk, rows, d), BF16),
+                        V((nblk, 32, rows), F32), V((rows, 256), F32), V((3, rows, d), BF16),
+                        V((N, 2, U, U), BF16), V((4, 2, U, U), BF16), V((N, 2, U, U), BF16), V((N, U, U), BF16),
+                        V((N, nx - 1, CX, U), BF16), V((N, nd - 1, PZ, U), BF16), V((N, U, U), BF16),
+                        V((24, U), F32), V((3, 24, U), F32), V((nx, 24, U), F32), V((nd, 24, U), F32)] + sems,
+        compiler_params=pltpu.CompilerParams(collective_id=cid, has_side_effects=True, vmem_limit_bytes=63 << 20),
+        name="backward_reduce",
+    )(lens, vec, vg, qkv, att, lse, wq, wo, wu, wd, dh, hat, act, gp, tok)
+
+
+def fast_body(
+    tokens, cotangent, lengths, w_qkv, bias_q, bias_v, w_out, bias_out, gain_one, shift_one,
+    w_up, bias_up, w_down, bias_down, gain_two, shift_two,
+):
+    seqs, seq_rows, width = tokens.shape
+    nx, nd = lax.axis_size("ctx") // 2, lax.axis_size("dp")
+    small = [bias_q, bias_v, bias_out, gain_one, shift_one, bias_up, bias_down, gain_two, shift_two]
+    (qkv, att, lse, wq, wo, wu, wd, vec, out, dh, hat, act, gp, vg) = forward_gather(
+        lengths, tokens, cotangent, w_qkv, w_out, w_up, w_down, small, nx, 2
+    )
+    t_down, t_up, t_out, t_qkv, t_vec, grad_in = backward_reduce(
+        lengths, vec, vg, qkv, att, lse, wq, wo, wu, wd, dh, hat, act, gp,
+        tokens.reshape(seqs * seq_rows, width), nx, nd, seqs, 3
+    )
+
+    def part(first, count):
+        return t_vec[first : first + count].reshape(-1)
+
+    return (
+        out.reshape(tokens.shape), grad_in.reshape(tokens.shape), t_qkv.astype(F32), part(0, 1), part(1, 1),
+        t_out.astype(F32), part(2, 1), part(3, 1), part(4, 1), t_up.astype(F32), part(5, 4),
+        t_down.astype(F32), part(9, 1), part(10, 1), part(11, 1),
+    )
+
+
 def solution(mesh):
     return jax.shard_map(
-        body,
+        fast_body if mesh.shape["ctx"] <= 4 else general_body,
         mesh=mesh,
         in_specs=(
             P(("dp", "fsdp"), "ctx", None),

time: 698 us -> 275 us (0.39)
  waiting for transfers between devices: 247 us -> 0 us
  matrix products: 138 us -> 0 us
  Pallas kernels: 133 us -> 246 us
  other arithmetic: 58.1 us -> 9.48 us
  local copies, waits for them, and re-layouts: 58.1 us -> 16.8 us
  blocking collectives: 30.1 us -> 0 us
  between operations: 15 us -> 0.68 us
  starting transfers between devices: 11.5 us -> 0 us
    all_gather x6 -> x0, waiting for transfers between devices: 152 us -> none  [the longest x1 51 us: body(): lax.all_gather(w_qkv, 'fsdp', axis=0, tiled=True)]
    dot_general x36 -> x0, matrix products: 138 us -> none  [the longest x4 33 us: row_dot(): return jnp.dot(left_op, right_op, preferred_element_type=jnp.float32)]
    pallas_call x1 -> x2, Pallas kernels: 133 us -> 246 us  [the longest x1 173 us: backward_reduce(): pl.pallas_call(functools.partial(bwd_kernel, nx, nd, seqs, rows // seqs),...]
    ppermute x16 -> x0, waiting for transfers between devices: 93.3 us -> none  [shifted(): return lax.ppermute(value, axis, pairs)]
    all_gather x9 -> x0, blocking collectives: 30.1 us -> none  [the longest x1 3.56 us: body(): lax.all_gather(bias_up, 'fsdp', axis=0, tiled=True)]
    while x57 -> x0, local copies, waits for them, and re-layouts: 25.7 us -> none
    convert_element_type x27 -> x4, other arithmetic: 35.2 us -> 9.48 us  [the longest x1 2.76 us: fast_body(): t_up.astype(F32)]
    reduce_sum x13 -> x0, other arithmetic: 22.3 us -> none  [the longest x2 15.1 us: visit(): jnp.sum(weights, -1)]
  transfers between devices with their start and end apart: 22 -> 0, of which waited for: 20 -> 0; matrix products, arithmetic and copies ran while one was open for 17% -> 0% of each run, Pallas kernels for 0% -> 0%
where the time goes in v3:
time: 275 us; the launch traced here: 273 us
  Pallas kernels  246 us (89%)
  local copies, waits for them, and re-layouts  16.8 us (6%)
  other arithmetic  9.48 us (3%)
    pallas_call x1, Pallas kernels, backward_reduce(): pl.pallas_call(functools.partial(bwd_kernel, nx, nd, seqs, rows // seqs),...  173 us
    pallas_call x1, Pallas kernels, forward_gather(): pl.pallas_call(functools.partial(fwd_kernel, nx, seqs, seq_rows), out_sha...  73.3 us
    reshape x9, local copies, waits for them, and re-layouts, forward_gather(): v.reshape(1, -1)  11.2 us

profile of v3, /device:TPU:5, one launch (start us, length us, event | category | flops | bytes accessed | tf_op | source)
XLA Modules:
  0.0 273.4 jit_solution(3700028488877977528)
XLA Ops:
  0.6 1.2 reshape.99.rest_0_
  1.9 1.2 reshape.100.rest_1_
  3.1 1.2 reshape.101.rest_2_
  4.4 1.2 reshape.102.rest_3_
  5.6 1.2 reshape.103.rest_4_
  6.9 1.2 reshape.105.rest_6_
  8.1 1.2 reshape.106.rest_7_
  9.3 1.2 reshape.107.rest_8_
  10.6 1.3 reshape.104.rest_5_
  11.9 73.3 %forward_gather.1 = (bf16[3,4,512,768]{3,2,1,0:T(8,128)(2,1)}, f32[512,768]{1,0:T(8,128)}, f32[512,256]{1,0:T(8,128)}, bf16[768,2304]{1,0:T(8,128)(2,1)}, bf16[7...) custom-call(s32[2]{0:T(128)} %lens.3, ...), custom_call_target="tpu_custom_call" | custom-call | tf_op jit(solution)/shard_map/forward_gather/pallas_call | solution.py:1020
  85.2 173.1 %backward_reduce.1 = (bf16[1536,768]{1,0:T(8,128)(2,1)}, bf16[384,3072]{1,0:T(8,128)(2,1)}, bf16[384,768]{1,0:T(8,128)(2,1)}, bf16[384,2304]{1,0:T(8,128)(2,1)},...) custom-call(s32[2]{0:T(128)} %lens.3, f32[2,12,384]{2,1,0:T(8,128)} %get-tuple-element.36.vec, ...), custom_call_target="tpu_custom_call" | custom-call | tf_op jit(solution)/shard_map/backward_reduce/pallas_call | solution.py:1625
  258.3 0.0 copy-start.2
  258.3 0.9 slice.32
  259.2 1.6 slice_reduce_fusion
  260.8 0.6 reshape.115
  261.4 2.2 convert_element_type.13
  263.5 0.0 copy-done.2
  263.5 2.0 convert_element_type.12
  265.6 0.8 copy-done.1
  266.4 2.8 %convert_element_type.14 = f32[384,3072]{1,0:T(8,128)} convert(bf16[384,3072]{1,0:T(8,128)(2,1)S(1)} %copy-done.1) | non-fusion elementwise | flops 1179648 | bytes 7077888 | tf_op jit(solution)/shard_map/convert_element_type | solution.py:1661
  269.1 2.5 convert_element_type.15
  271.7 0.9 copy.33
  272.6 0.0 copy-done.4
  272.6 0.9 copy.34
  (6 shorter events, 0.0 us)
Async XLA Ops:
  258.3 5.2 %copy-start.2 = (bf16[384,2304]{1,0:T(8,128)(2,1)S(1)}, bf16[384,2304]{1,0:T(8,128)(2,1)}, u32[]{:S(2)}) copy-start(bf16[384,2304]{1,0:T(8,128)(2,1)} %get-tuple-element.50) | copy-start | bytes 5308420
  263.5 2.8 %copy-start.1 = (bf16[384,3072]{1,0:T(8,128)(2,1)S(1)}, bf16[384,3072]{1,0:T(8,128)(2,1)}, u32[]{:S(2)}) copy-start(bf16[384,3072]{1,0:T(8,128)(2,1)} %get-tuple-element.53) | copy-start | bytes 7077892
  266.4 2.8 %copy-start = (bf16[1536,768]{1,0:T(8,128)(2,1)S(1)}, bf16[1536,768]{1,0:T(8,128)(2,1)}, u32[]{:S(2)}) copy-start(bf16[1536,768]{1,0:T(8,128)(2,1)} %get-tuple-element.54) | copy-start | bytes 7077892
  269.1 2.6 copy-start.3
  269.1 3.4 %copy-start.4 = (bf16[512,768]{1,0:T(8,128)(2,1)S(1)}, bf16[512,768]{1,0:T(8,128)(2,1)}, u32[]{:S(2)}) copy-start(bf16[512,768]{1,0:T(8,128)(2,1)} %get-tuple-element.49) | copy-start | bytes 2359300

commit v4 on v3

--- a/solution.py
+++ b/solution.py
@@ -744,8 +744,9 @@
         loc(b).start()
     row = 0
     for v in small:
-        for i in range(v.shape[1] // U):
-            vec_o[f, row:row + 1, :] = v[:, i * U:(i + 1) * U].astype(F32)
+        w = v[...].astype(F32).reshape(1, -1)
+        for i in range(v.shape[0] // U):
+            vec_o[f, row:row + 1, :] = w[:, i * U:(i + 1) * U]
             row += 1
     tc = pltpu.make_async_copy(cot, CT, lts.at[1])
     pl.semaphore_wait(bar, len(peers))
@@ -1030,7 +1031,7 @@
                         V((rows, d), BF16), V((rows, 3072), BF16), V((rows, 3072), F32), V((rows, d), BF16)] + sems,
         compiler_params=pltpu.CompilerParams(collective_id=cid, has_side_effects=True, vmem_limit_bytes=62 << 20),
         name="forward_gather",
-    )(lens, tok.reshape(rows, d), cot.reshape(rows, d), sq, so_, su, sd, *[v.reshape(1, -1) for v in small])
+    )(lens, tok.reshape(rows, d), cot.reshape(rows, d), sq, so_, su, sd, *small)
 
 
 def tn(a, b):
@@ -1050,7 +1051,7 @@
     nblk = 2 * nx
     rows = seqs * seq_rows
     CX, PZ = U // nx, U // nx // nd
-    NCH = 12
+    NCH, READY = 12, 8
     sib = {"ctx": x * 2 + 1 - core}
     yp = {"fsdp": 1 - f}
     xps = [{"ctx": lax.rem(x + j, nx) * 2 + core} for j in range(1, nx)]
@@ -1200,19 +1201,10 @@
         c8(c).start()
 
     def tick(c):
-        stages = ((4, st7), (3, st6), (2, st5), (1, st4), (0, st3))
-        if isinstance(c, int):
-            for lag, fn in stages:
-                if 0 <= c - lag < NCH:
-                    fn(c - lag)
-        else:
-            for lag, fn in stages[1:]:
-                if lag == 0:
-                    fn(c)
-                else:
-                    @pl.when(c >= lag)
-                    def _():
-                        fn(c - lag)
+        for lag, fn in ((7, st6), (6, st5), (4, st4), (0, st3)):
+            @pl.when(jnp.logical_and(c >= lag, c - lag <= READY))
+            def _(lag=lag, fn=fn):
+                fn(c - lag)
 
     def v_core():
         return remote(VV, V0.at[0], vs.at[0], vr.at[0], sib)
@@ -1433,7 +1425,8 @@
     st2(6)
     st2(7)
     st2(8)
-    tick(0)
+    st3(0)
+    st3(1)
 
     for k in (1, 2, 0):
         for blk in range(nblk):
@@ -1508,7 +1501,7 @@
         DQKV[1, kr, cols] = jnp.where(live, jnp.where(low_half, resk[0], resk[1]), 0.0).astype(BF16)
         DQKV[2, kr, cols] = jnp.where(live, jnp.where(low_half, resv[0], resv[1]), 0.0).astype(BF16)
 
-    def segment(fn, groups, first):
+    def segment(fn, groups, first, hook):
         per = ntile * 6 // groups
 
         def group(g, _):
@@ -1518,21 +1511,27 @@
                 return 0
             lax.fori_loop(0, per, one, 0)
             tick(first + g)
+            if hook is not None:
+                @pl.when(g == 2)
+                def _():
+                    hook()
             return 0
         lax.fori_loop(0, groups, group, 0)
 
-    segment(dq_one, 2, 1)
-    for j in range(1, nx):
-        d_x(j).wait_recv()
-        d_f(j).start()
-        r_x(j).wait_recv()
-        r_f(j).start()
+    def relay():
+        for j in range(1, nx):
+            d_x(j).wait_recv()
+            d_f(j).start()
+            r_x(j).wait_recv()
+            r_f(j).start()
+
+    segment(dq_one, 4, 2, relay)
     d_sib().wait_recv()
     r_sib().wait_recv()
     for j in range(1, nx):
         d_f(j).wait_recv()
         r_f(j).wait_recv()
-    segment(dkv_one, 3, 3)
+    segment(dkv_one, 4, 6, None)
 
     loads["tok"].wait()
     for kk in (1, 0):
@@ -1559,8 +1558,6 @@
     put_vec(0, bias_sum(0))
     put_vec(2, bias_sum(2))
     vst(0)
-    tick(6)
-    vst(1)
     for b in range(3):
         loads[("wq", b)].wait()
     for t in range(3):
@@ -1571,15 +1568,48 @@
         DM[:, cs] = acc.astype(BF16)
     gout = pltpu.make_async_copy(DM, gin_o, s8.at[NCH])
     gout.start()
-    vst(2)
+    st4(6)
+    st5(4)
+    st6(3)
+    vst(1)
+    st4(7)
+    st5(5)
+    st6(4)
     st7(0)
     st7(1)
-    tick(7)
+    st4(8)
+    st5(6)
+    st6(5)
+    vst(2)
+    st7(2)
+    st3(9)
+    st5(7)
+    st6(6)
     vst(3)
-    for c in range(8, NCH + 4):
-        tick(c)
-        if c == 8:
-            vst(4)
+    st7(3)
+    st5(8)
+    st6(7)
+    st4(9)
+    st3(10)
+    st6(8)
+    vst(4)
+    st7(4)
+    st7(5)
+    st5(9)
+    st4(10)
+    st3(11)
+    st6(9)
+    st7(6)
+    st7(7)
+    st5(10)
+    st4(11)
+    st6(10)
+    st7(8)
+    st5(11)
+    st7(9)
+    st6(11)
+    st7(10)
+    st7(11)
     for c in range(NCH):
         c2(c).wait_send()
         c7(c).wait()

time: 275 us -> 243 us (0.88)
  Pallas kernels: 246 us -> 224 us
  local copies, waits for them, and re-layouts: 16.8 us -> 5.62 us
    pallas_call x1, Pallas kernels: 173 us -> 150 us  [backward_reduce(): pl.pallas_call(functools.partial(bwd_kernel, nx, nd, seqs, rows // seqs),...]
    reshape x9 -> x0, local copies, waits for them, and re-layouts: 11.2 us -> none  [forward_gather(): v.reshape(1, -1)]
where the time goes in v4:
time: 243 us; the launch traced here: 239 us
  Pallas kernels  224 us (92%)
  other arithmetic  9.48 us (4%)
  local copies, waits for them, and re-layouts  5.62 us (2%)
    pallas_call x1, Pallas kernels, backward_reduce(): pl.pallas_call(functools.partial(bwd_kernel, nx, nd, seqs, rows // seqs),...  150 us
    pallas_call x1, Pallas kernels, forward_gather(): pl.pallas_call(functools.partial(fwd_kernel, nx, seqs, seq_rows), out_sha...  73.4 us

profile of v4, /device:TPU:5, one launch (start us, length us, event | category | flops | bytes accessed | tf_op | source)
XLA Modules:
  0.0 239.4 jit_solution(3319244255433081722)
XLA Ops:
  0.7 73.4 %forward_gather.1 = (bf16[3,4,512,768]{3,2,1,0:T(8,128)(2,1)}, f32[512,768]{1,0:T(8,128)}, f32[512,256]{1,0:T(8,128)}, bf16[768,2304]{1,0:T(8,128)(2,1)}, bf16[7...) custom-call(s32[2]{0:T(128)} %lens.3, ...), custom_call_target="tpu_custom_call" | custom-call | tf_op jit(solution)/shard_map/forward_gather/pallas_call | solution.py:1021
  74.0 150.2 %backward_reduce.1 = (bf16[1536,768]{1,0:T(8,128)(2,1)}, bf16[384,3072]{1,0:T(8,128)(2,1)}, bf16[384,768]{1,0:T(8,128)(2,1)}, bf16[384,2304]{1,0:T(8,128)(2,1)},...) custom-call(s32[2]{0:T(128)} %lens.3, f32[2,12,384]{2,1,0:T(8,128)} %get-tuple-element.36.vec, ...), custom_call_target="tpu_custom_call" | custom-call | tf_op jit(solution)/shard_map/backward_reduce/pallas_call | solution.py:1655
  224.2 0.0 copy-start.2
  224.3 0.9 slice.32
  225.1 1.6 slice_reduce_fusion
  226.7 0.6 reshape.79
  227.3 2.2 convert_element_type.13
  229.5 0.0 copy-done.2
  229.5 0.0 copy-start.1
  229.5 2.0 convert_element_type.12
  231.5 0.8 copy-done.1
  232.3 0.0 copy-start
  232.3 2.8 %convert_element_type.14 = f32[384,3072]{1,0:T(8,128)} convert(bf16[384,3072]{1,0:T(8,128)(2,1)S(1)} %copy-done.1) | non-fusion elementwise | flops 1179648 | bytes 7077888 | tf_op jit(solution)/shard_map/convert_element_type | solution.py:1691
  235.0 0.0 copy-done
  235.1 0.0 copy-start.3
  235.1 0.0 copy-start.4
  235.1 2.5 %convert_element_type.15 = f32[1536,768]{1,0:T(8,128)} convert(bf16[1536,768]{1,0:T(8,128)(2,1)S(1)} %copy-done) | non-fusion elementwise | flops 1179648 | bytes 7077888 | tf_op jit(solution)/shard_map/convert_element_type | solution.py:1692
  237.6 0.0 copy-done.3
  237.6 0.9 copy.33
  238.5 0.0 copy-done.4
  238.5 0.9 copy.34
Async XLA Ops:
  224.2 5.2 %copy-start.2 = (bf16[384,2304]{1,0:T(8,128)(2,1)S(1)}, bf16[384,2304]{1,0:T(8,128)(2,1)}, u32[]{:S(2)}) copy-start(bf16[384,2304]{1,0:T(8,128)(2,1)} %get-tuple-element.50) | copy-start | bytes 5308420
  229.5 2.8 %copy-start.1 = (bf16[384,3072]{1,0:T(8,128)(2,1)S(1)}, bf16[384,3072]{1,0:T(8,128)(2,1)}, u32[]{:S(2)}) copy-start(bf16[384,3072]{1,0:T(8,128)(2,1)} %get-tuple-element.53) | copy-start | bytes 7077892
  232.3 2.8 %copy-start = (bf16[1536,768]{1,0:T(8,128)(2,1)S(1)}, bf16[1536,768]{1,0:T(8,128)(2,1)}, u32[]{:S(2)}) copy-start(bf16[1536,768]{1,0:T(8,128)(2,1)} %get-tuple-element.54) | copy-start | bytes 7077892
  235.1 2.6 %copy-start.3 = (bf16[512,768]{1,0:T(8,128)(2,1)S(1)}, bf16[512,768]{1,0:T(8,128)(2,1)}, u32[]{:S(2)}) copy-start(bf16[512,768]{1,0:T(8,128)(2,1)} %get-tuple-element.35) | copy-start | bytes 2359300
  235.1 3.4 %copy-start.4 = (bf16[512,768]{1,0:T(8,128)(2,1)S(1)}, bf16[512,768]{1,0:T(8,128)(2,1)}, u32[]{:S(2)}) copy-start(bf16[512,768]{1,0:T(8,128)(2,1)} %get-tuple-element.49) | copy-start | bytes 2359300

commit v5 on v4

--- a/solution.py
+++ b/solution.py
@@ -764,73 +764,75 @@
     tc.start()
     tl.wait()
 
-    def qkv(b, blk):
-        fac = 0.125 if b == 0 else 1.0
-
-        def one(t, _):
-            c = pl.ds(pl.multiple_of(t * 256, 256), 256)
-            w = WB[b, :, :, c].reshape(768, 256)
-            QKV[b, blk, :, c] = mm(XT[blk], w).astype(BF16)
-            return 0
-        if b == 1:
-            lax.fori_loop(0, 3, one, 0)
-        else:
-            row = 0 if b == 0 else 1
-            for t in range(3):
-                w = WB[b, :, :, t * 256:(t + 1) * 256].reshape(768, 256)
+    def qkv(b, blk, h):
+        hr = pl.ds(pl.multiple_of(h * H, H), H)
+        row = 0 if b == 0 else 1
+        xr = XT[blk, hr, :]
+        for t in range(3):
+            w = WB[b, :, :, t * 256:(t + 1) * 256].reshape(768, 256)
+            r = mm(xr, w)
+            if b != 1:
                 if t == 0:
                     bias = vec_o[0, row:row + 1, 0:256]
                 elif t == 1:
                     bias = jnp.concatenate([vec_o[0, row:row + 1, 256:384], vec_o[1, row:row + 1, 0:128]], 1)
                 else:
                     bias = vec_o[1, row:row + 1, 128:384]
-                r = (mm(XT[blk], w) + bias).astype(BF16)
-                if b == 0:
-                    r = r * jnp.asarray(fac, BF16)
-                QKV[b, blk, :, t * 256:(t + 1) * 256] = r
-
-    seq = list(order)
-    A(seq[0])
-    A(seq[1])
-    B(seq[0])
+                r = r + bias
+            r = r.astype(BF16)
+            if b == 0:
+                r = r * jnp.asarray(0.125, BF16)
+            QKV[b, blk, hr, t * 256:(t + 1) * 256] = r
+
+    def far(h, bs):
+        for j in range(1, nx):
+            base = lax.rem(x + nx - j, nx) * 2
+
+            def pair(i, _):
+                for b in bs:
+                    qkv(b, base + i, h)
+                return 0
+            lax.fori_loop(0, 2, pair, 0)
+
+    def far_wait(h):
+        for j in range(1, nx):
+            t_f(j, h).wait_recv()
+
+    def relay(h):
+        for j in range(1, nx):
+            t_x(j, h).wait_recv()
+            t_f(j, h).start()
+
+    def near(b):
+        def both(i, _):
+            qkv(b, x * 2 + i // 2, lax.rem(i, 2))
+            return 0
+        lax.fori_loop(0, 4, both, 0)
+
+    A(1)
     for h in range(2):
         t_sib(h).wait_recv()
-    A(seq[2])
-    B(seq[1])
     vcp.wait_recv()
-    for n, b in enumerate(seq):
-        loc(b).wait()
-        C(b)
-
-        def both(i, _):
-            qkv(b, x * 2 + i)
-            return 0
-        lax.fori_loop(0, 2, both, 0)
-        if n == 0:
-            B(seq[2])
-            A(3)
-        if n == 1:
-            B(3)
-            A(4)
-    for j in range(1, nx):
-        for h in range(2):
-            t_x(j, h).wait_recv()
-            t_f(j, h).start()
-    B(4)
-    A(5)
-    for j in range(1, nx):
-        for h in range(2):
-            t_f(j, h).wait_recv()
-        base = lax.rem(x + nx - j, nx) * 2
-
-        def pair(i, _):
-            for b in seq:
-                qkv(b, base + i)
-            return 0
-        lax.fori_loop(0, 2, pair, 0)
-    B(5)
-    qo = pltpu.make_async_copy(QKV, qkv_o, outs.at[0])
-    qo.start()
+    loc(1).wait()
+    B(1)
+    A(2)
+    C(1)
+    near(1)
+    B(2)
+    A(0)
+    relay(0)
+    loc(2).wait()
+    C(2)
+    near(2)
+    B(0)
+    far_wait(0)
+    far(0, (1,))
+    A(3)
+    loc(0).wait()
+    C(0)
+    near(0)
+    A(4)
+    far(0, (2, 0))
 
     low_half = head_masks(QT)
     lane128 = lax.broadcasted_iota(jnp.int32, (QT, 128), 1)
@@ -874,21 +876,40 @@
         ATT[qr, cols] = jnp.where(low_half, outs_[0], outs_[1])
         LSE[qr, 0:128] = tot
 
-    ntile = rows // QT
-    per = ntile * 6 // 4
-
-    def group(g, _):
-        A(6 + g)
-
-        def one(i, _):
-            it = g * per + i
-            attend(it // 6, lax.rem(it, 6))
+    tiles = rows // QT // 2
+
+    def attend_half(h, hooks):
+        per = tiles * 6 // len(hooks)
+
+        def group(g, _):
+            def one(i, _):
+                it = g * per + i
+                attend(h * tiles + it // 6, lax.rem(it, 6))
+                return 0
+            lax.fori_loop(0, per, one, 0)
+            for k, hook in enumerate(hooks):
+                @pl.when(g == k)
+                def _(hook=hook):
+                    hook()
             return 0
-        lax.fori_loop(0, per, one, 0)
-        B(6 + g)
-        return 0
-    lax.fori_loop(0, 4, group, 0)
-    A(10)
+        lax.fori_loop(0, len(hooks), group, 0)
+
+    def step(a):
+        def fn():
+            A(a)
+            B(a - 2)
+        return fn
+
+    def last():
+        step(7)()
+        relay(1)
+    attend_half(0, (step(5), step(6), last))
+    far_wait(1)
+    far(1, order)
+    step(8)()
+    qo = pltpu.make_async_copy(QKV, qkv_o, outs.at[0])
+    qo.start()
+    attend_half(1, (step(9), step(10), step(11)))
     extra = []
 
     def send_out(src, dst):
@@ -945,7 +966,6 @@
     lax.fori_loop(0, rows // RB, ln1, 0)
     send_out(H1, hat_o)
     send_out(LSE, lse_o)
-    A(11)
     B(10)
     for b in range(4, 8):
         ready(b)
@@ -961,10 +981,12 @@
         return 0
     lax.fori_loop(0, 2, upblock, 0)
     B(11)
+    ready(8)
+    ready(9)
     lax.fori_loop(2, 4, upblock, 0)
     send_out(ACT, act_o)
     send_out(GP, gp_o)
-    for b in range(8, 12):
+    for b in range(10, 12):
         ready(b)
     bd = vector(9)
     for t in range(3):
@@ -1071,16 +1093,15 @@
 
     load("dh", dh_i, DH)
     load("act", act_i, ACT)
-    load("wd", wd_i, BIG.at[pl.ds(0, 3072)])
-    load("gp0", gp_i.at[:, pl.ds(0, 768)], GP.at[0])
+    for b in range(4):
+        load(("wd", b), wd_i.at[pl.ds(b * 768, 768)], BIG.at[pl.ds(b * 768, 768)])
+        if b < 2:
+            load("gp%d" % b, gp_i.at[:, pl.ds(b * 768, 768)], GP.at[b])
     load("hat", hat_i, HAT)
-    load("gp1", gp_i.at[:, pl.ds(768, 768)], GP.at[1])
     for b in range(4):
         load(("wu", b), wu_i.at[:, pl.ds(b * 768, 768)], BIG.at[pl.ds(3072 + b * 768, 768)])
     load("lse", lse_i, COLS.at[:, pl.ds(0, 256)])
     load("wo", wo_i, WO)
-    for b in range(3):
-        load(("wq", b), wq_i.at[:, pl.ds(b * 768, 768)], WQ.at[b])
 
     def vector(r):
         return jnp.concatenate([vec[0, r:r + 1, :], vec[1, r:r + 1, :]], 1)
@@ -1112,6 +1133,9 @@
     def c6(c, j):
         w = AX.at[c, pl.ds(pl.multiple_of(x * CX, CX), CX)]
         return remote(w, w, s6s.at[c, j - 1], s6r.at[c, j - 1], xps[j - 1])
+
+    def qpart(i, cc):
+        return cc if i == 9 else i - 8 + 2 * cc
 
     def orect(i):
         if i < 4:
@@ -1120,7 +1144,7 @@
             return ou.at[:, pl.ds(pl.multiple_of(core * 1536 + (i - 4) * U, 128), U)]
         if i < 9:
             return oo.at[:, pl.ds(pl.multiple_of(core * U, 128), U)]
-        return oq.at[:, pl.ds(pl.multiple_of(core * 1152 + (i - 9) * U, 128), U)]
+        return oq.at[:, pl.ds(pl.multiple_of(qpart(i, core) * U, 128), U)]
 
     def c7(c):
         return remote(AX.at[c], orect(c), s7s.at[c], s7r.at[c], sib)
@@ -1199,12 +1223,6 @@
             c6(c, j).wait_recv()
         c7(c).start()
         c8(c).start()
-
-    def tick(c):
-        for lag, fn in ((7, st6), (6, st5), (4, st4), (0, st3)):
-            @pl.when(jnp.logical_and(c >= lag, c - lag <= READY))
-            def _(lag=lag, fn=fn):
-                fn(c - lag)
 
     def v_core():
         return remote(VV, V0.at[0], vs.at[0], vr.at[0], sib)
@@ -1266,7 +1284,6 @@
         return acc + fold8(v.astype(F32))
     zero = jnp.zeros((8, 768), F32)
     put_vec(18, jnp.sum(lax.fori_loop(0, rows // RB, to_dm, zero), 0, keepdims=True))
-    loads["act"].wait()
 
     def fill(i0, kk, ff, val, wide):
         v = val.astype(BF16)
@@ -1285,6 +1302,8 @@
     def ccof(kk):
         return core if kk == 0 else 1 - core
 
+    pl.semaphore_wait(bar, len(peers))
+    loads["act"].wait()
     for ii in range(2):
         for kk in (1, 0):
             def wdown(ff, kk=kk, ii=ii):
@@ -1292,64 +1311,40 @@
                 fill(2 * ii, kk, ff, tn(ACT[:, pl.ds(h, U)], DM[...]), 2)
             each_f(wdown)
             if kk == 1:
-                if ii == 0:
-                    pl.semaphore_wait(bar, len(peers))
                 st1(2 * ii)
                 st1(2 * ii + 1)
-    st2(0)
-    st2(1)
-    loads["wd"].wait()
+                if ii == 1:
+                    st2(0)
+                    st2(1)
+    st2(2)
     for b in range(4):
+        loads[("wd", b)].wait()
         loads["gp%d" % b].wait()
         for t in range(3):
             h = b * 768 + t * 256
             du = (nt(DM[...], BIG[h:h + 256, :]) * GP[b % 2, :, t * 256:(t + 1) * 256]).astype(BF16)
-            ACT[:, h:h + 256] = du
+            WQ[b * rows:(b + 1) * rows, t * 256:(t + 1) * 256] = du
             s = colsum(du.astype(F32))
             for q in range(2):
                 o = h + q * 128
                 VV[10 + o // U:11 + o // U, o % U:o % U + 128] = s[:, q * 128:(q + 1) * 128]
         if b < 2:
             load("gp%d" % (b + 2), gp_i.at[:, pl.ds((b + 2) * 768, 768)], GP.at[b % 2])
-        if b == 1:
-            st2(2)
     st2(3)
     loads["hat"].wait()
     g1, s1 = vector(3), vector(4)
-
-    def to_nb(i, _):
-        r = pl.ds(pl.multiple_of(i * RB, RB), RB)
-        NB[r, :] = (HAT[r, :] * g1 + s1).astype(BF16)
-        return 0
-    lax.fori_loop(0, rows // RB, to_nb, 0)
-    for ii in range(2):
-        for kk in (1, 0):
-            if kk == 1:
-                for i in (2 * ii, 2 * ii + 1):
-                    for cp in c1s(i):
-                        cp.wait_send()
-
-            def wup(ff, kk=kk, ii=ii):
-                h = pl.multiple_of(ccof(kk) * 1536 + ii * 768, 768)
-                fill(4 + 2 * ii, kk, ff, tn(NB[:, pl.ds(pl.multiple_of(ff * U, U), U)], ACT[:, pl.ds(h, 768)]), 2)
-            each_f(wup)
-            if kk == 1:
-                st1(4 + 2 * ii)
-                st1(5 + 2 * ii)
-    load("tok", tok_i, NB)
     for b in range(4):
         loads[("wu", b)].wait()
     for t in range(3):
         cs = slice(t * 256, (t + 1) * 256)
         acc = DH[:, cs]
         for b in range(4):
-            acc = acc + nt(ACT[:, b * 768:(b + 1) * 768], BIG[3072 + b * 768 + t * 256:3072 + b * 768 + (t + 1) * 256, :])
+            acc = acc + nt(WQ[b * rows:(b + 1) * rows, :], BIG[3072 + b * 768 + t * 256:3072 + b * 768 + (t + 1) * 256, :])
         DH[:, cs] = acc
     for k in (1, 2, 0):
         for blk in range(nblk):
             load(("qkv", k, blk), qkv_i.at[k, blk], BIG.at[pl.ds((k * nblk + blk) * rows, rows)])
-    st2(4)
-    st2(5)
+    st3(0)
     loads["lse"].wait()
 
     def ln1(i, carry):
@@ -1358,7 +1353,8 @@
         d = normal_back(dn, hat, COLS[r, 128:129], g1)
         DH[r, :] = d
         da = d.astype(BF16)
-        DM[r, :] = da
+        DQKV[0, r, :] = da
+        NB[r, :] = (hat * g1 + s1).astype(BF16)
         return carry[0] + fold8(dn * hat), carry[1] + fold8(dn), carry[2] + fold8(da.astype(F32))
     sums = lax.fori_loop(0, rows // RB, ln1, (zero, zero, zero))
     for row, sv in zip((6, 8, 4), sums):
@@ -1366,7 +1362,7 @@
     load("att", att_i, HAT)
     loads["wo"].wait()
     for t in range(3):
-        DO[me, :, t * 256:(t + 1) * 256] = nt(DM[...], WO[t * 256:(t + 1) * 256, :]).astype(BF16)
+        DO[me, :, t * 256:(t + 1) * 256] = nt(DQKV[0], WO[t * 256:(t + 1) * 256, :]).astype(BF16)
 
     def d_sib():
         return remote(DO.at[me], DO.at[me], d0s.at[0], d0r.at[0], sib)
@@ -1392,17 +1388,6 @@
         d_x(j).start()
     d_sib().start()
     loads["att"].wait()
-    for kk in (1, 0):
-        if kk == 1:
-            for cp in c1s(4):
-                cp.wait_send()
-
-        def wout(ff, kk=kk):
-            a = HAT[:, pl.ds(pl.multiple_of(ff * U, U), U)].astype(BF16)
-            fill(8, kk, ff, tn(a, DM[:, pl.ds(pl.multiple_of(ccof(kk) * U, U), U)]), 1)
-        each_f(wout)
-        if kk == 1:
-            st1(8)
     head = lax.broadcasted_iota(jnp.int32, (768, 128), 0) // HW
     pick = (head == lax.broadcasted_iota(jnp.int32, (768, 128), 1)).astype(BF16)
 
@@ -1422,12 +1407,41 @@
     for j in range(1, nx):
         r_x(j).start()
     r_sib().start()
+    for ii in range(2):
+        for kk in (1, 0):
+            if kk == 1:
+                for i in (2 * ii, 2 * ii + 1):
+                    for cp in c1s(i):
+                        cp.wait_send()
+
+            def wup(ff, kk=kk, ii=ii):
+                h = pl.multiple_of((ccof(kk) * 2 + ii) * rows, rows)
+                fill(4 + 2 * ii, kk, ff, tn(NB[:, pl.ds(pl.multiple_of(ff * U, U), U)], WQ[pl.ds(h, rows), :]), 2)
+            each_f(wup)
+            if kk == 1:
+                st1(4 + 2 * ii)
+                st1(5 + 2 * ii)
+                if ii == 1:
+                    st2(4)
+                    st2(5)
+    load("tok", tok_i, NB)
+    for b in range(3):
+        load(("wq", b), wq_i.at[:, pl.ds(b * 768, 768)], WQ.at[pl.ds(b * 768, 768)])
+    st3(1)
     st2(6)
+    for kk in (1, 0):
+        if kk == 1:
+            for cp in c1s(4):
+                cp.wait_send()
+
+        def wout(ff, kk=kk):
+            a = HAT[:, pl.ds(pl.multiple_of(ff * U, U), U)].astype(BF16)
+            fill(8, kk, ff, tn(a, DQKV[0, :, pl.ds(pl.multiple_of(ccof(kk) * U, U), U)]), 1)
+        each_f(wout)
+        if kk == 1:
+            st1(8)
     st2(7)
     st2(8)
-    st3(0)
-    st3(1)
-
     for k in (1, 2, 0):
         for blk in range(nblk):
             loads[("qkv", k, blk)].wait()
@@ -1447,7 +1461,8 @@
     def zero_other(v, h):
         return jnp.where(low_half == (h == 0), v, jnp.zeros_like(v))
 
-    def dq_one(tile, j):
+    def dq_one(it):
+        tile, j = it // 6, lax.rem(it, 6)
         s0 = tile // nr
         q0 = pl.multiple_of(tile * QT, QT)
         qr = pl.ds(q0, QT)
@@ -1473,7 +1488,8 @@
             res.append(acc)
         DQKV[0, qr, cols] = (jnp.where(low_half, res[0], res[1]) * 0.125).astype(BF16)
 
-    def dkv_one(tile, j):
+    def dkv_one(it):
+        tile, j = lax.rem(it, ntile), it // ntile
         s0 = tile // nr
         k0 = pl.multiple_of(tile * QT, QT)
         kr = pl.ds(k0, QT)
@@ -1501,22 +1517,21 @@
         DQKV[1, kr, cols] = jnp.where(live, jnp.where(low_half, resk[0], resk[1]), 0.0).astype(BF16)
         DQKV[2, kr, cols] = jnp.where(live, jnp.where(low_half, resv[0], resv[1]), 0.0).astype(BF16)
 
-    def segment(fn, groups, first, hook):
-        per = ntile * 6 // groups
+    def segment(fn, base, count, hooks):
+        per = count // len(hooks)
 
         def group(g, _):
             def one(i, _):
-                it = g * per + i
-                fn(it // 6, lax.rem(it, 6))
+                fn(base + g * per + i)
                 return 0
             lax.fori_loop(0, per, one, 0)
-            tick(first + g)
-            if hook is not None:
-                @pl.when(g == 2)
-                def _():
-                    hook()
+            for k, steps in enumerate(hooks):
+                @pl.when(g == k)
+                def _(steps=steps):
+                    for step, arg in steps:
+                        step(*arg)
             return 0
-        lax.fori_loop(0, groups, group, 0)
+        lax.fori_loop(0, len(hooks), group, 0)
 
     def relay():
         for j in range(1, nx):
@@ -1525,89 +1540,93 @@
             r_x(j).wait_recv()
             r_f(j).start()
 
-    segment(dq_one, 4, 2, relay)
+    def bias_sum(k):
+        def one(i, acc):
+            return acc + fold8(DQKV[k, pl.ds(pl.multiple_of(i * RB, RB), RB), :].astype(F32))
+        return jnp.sum(lax.fori_loop(0, rows // RB, one, zero), 0, keepdims=True)
+
+    def project(i):
+        for cp in c1s(i - 4):
+            cp.wait_send()
+        for kk in (1, 0):
+            def wqkv(ff, kk=kk):
+                p = qpart(i, ccof(kk))
+                a = NB[:, pl.ds(pl.multiple_of(ff * U, U), U)]
+                fill(i, kk, ff, tn(a, DQKV[p // 2, :, pl.ds(pl.multiple_of(lax.rem(p, 2) * U, U), U)]), 1)
+            each_f(wqkv)
+            if kk == 1:
+                st1(i)
+
+    segment(dq_one, 0, ntile * 6, (((st3, (2,)), (st4, (0,)), ),
+             ((st3, (3,)), ),
+             (),
+             ((st5, (0,)), (relay, ()), ),
+             ((st3, (4,)), (st4, (1,)), ),
+             ((st3, (5,)), (st6, (0,)), (st4, (2,)), ),))
+    loads["tok"].wait()
+    project(9)
+    put_vec(0, bias_sum(0))
+    st2(9)
     d_sib().wait_recv()
     r_sib().wait_recv()
     for j in range(1, nx):
         d_f(j).wait_recv()
         r_f(j).wait_recv()
-    segment(dkv_one, 4, 6, None)
-
-    loads["tok"].wait()
-    for kk in (1, 0):
-        if kk == 1:
-            for i in (5, 6, 7):
-                for cp in c1s(i):
-                    cp.wait_send()
-        for i in range(3):
-            def wqkv(ff, kk=kk, i=i):
-                p = ccof(kk) * 3 + i
-                a = NB[:, pl.ds(pl.multiple_of(ff * U, U), U)]
-                fill(9 + i, kk, ff, tn(a, DQKV[p // 2, :, pl.ds(pl.multiple_of(lax.rem(p, 2) * U, U), U)]), 1)
-            each_f(wqkv)
-            if kk == 1:
-                st1(9 + i)
-
-    def bias_sum(k):
-        def one(i, acc):
-            return acc + fold8(DQKV[k, pl.ds(pl.multiple_of(i * RB, RB), RB), :].astype(F32))
-        return jnp.sum(lax.fori_loop(0, rows // RB, one, zero), 0, keepdims=True)
-    st2(9)
+    segment(dkv_one, 0, ntile * 3, (((st4, (3,)), (st5, (1,)), ),
+             ((st3, (6,)), (st5, (2,)), (st4, (4,)), ),
+             ((st3, (7,)), (st5, (3,)), (st6, (1,)), (st4, (5,)), ),))
+    project(10)
     st2(10)
-    st2(11)
-    put_vec(0, bias_sum(0))
+    segment(dkv_one, ntile * 3, ntile * 3, (((st6, (2,)), (st5, (4,)), ),
+             ((st3, (8,)), (st5, (5,)), (st4, (6,)), (st6, (3,)), ),
+             ((st3, (9,)), (st4, (7,)), (st6, (4,)), ),))
     put_vec(2, bias_sum(2))
     vst(0)
+    project(11)
+    vst(1)
+    st2(11)
+    st5(6)
+    st6(5)
     for b in range(3):
         loads[("wq", b)].wait()
     for t in range(3):
         cs = slice(t * 256, (t + 1) * 256)
         acc = DH[:, cs]
         for b in range(3):
-            acc = acc + nt(DQKV[b], WQ[b, cs, :])
+            acc = acc + nt(DQKV[b], WQ[b * 768 + t * 256:b * 768 + (t + 1) * 256, :])
         DM[:, cs] = acc.astype(BF16)
     gout = pltpu.make_async_copy(DM, gin_o, s8.at[NCH])
     gout.start()
-    st4(6)
-    st5(4)
-    st6(3)
-    vst(1)
-    st4(7)
-    st5(5)
-    st6(4)
+    st4(8)
+    st5(7)
+    st6(6)
+    vst(2)
+    st3(10)
+    st4(9)
     st7(0)
     st7(1)
-    st4(8)
-    st5(6)
-    st6(5)
-    vst(2)
     st7(2)
-    st3(9)
-    st5(7)
-    st6(6)
+    st5(8)
+    st6(7)
     vst(3)
     st7(3)
-    st5(8)
-    st6(7)
-    st4(9)
-    st3(10)
+    st7(4)
+    st3(11)
+    st4(10)
+    st5(9)
     st6(8)
     vst(4)
-    st7(4)
     st7(5)
-    st5(9)
-    st4(10)
-    st3(11)
+    st7(6)
+    st4(11)
+    st5(10)
     st6(9)
-    st7(6)
     st7(7)
-    st5(10)
-    st4(11)
+    st5(11)
     st6(10)
     st7(8)
-    st5(11)
+    st6(11)
     st7(9)
-    st6(11)
     st7(10)
     st7(11)
     for c in range(NCH):
@@ -1649,7 +1668,7 @@
     D = pltpu.SemaphoreType.DMA
     V = pltpu.VMEM
     S = jax.ShapeDtypeStruct
-    sems = [D((32,)), D((2,)), D((2,))] + [D((nx - 1, 2))] * 4 + [D((N, 2)), D((N, 2)), D((N,)), D((N,)), D((N, nx - 1)), D((N, nx - 1)),
+    sems = [D((40,)), D((2,)), D((2,))] + [D((nx - 1, 2))] * 4 + [D((N, 2)), D((N, 2)), D((N,)), D((N,)), D((N, nx - 1)), D((N, nx - 1)),
             D((N, nd - 1)), D((N, nd - 1)), D((N, nd - 1)), D((N, nd - 1)), D((N, nx - 1)), D((N, nx - 1)),
             D((N,)), D((N,)), D((N + 1,)), D((nx + nd,)), D((nx + nd,))]
     return pl.pallas_call(
@@ -1657,7 +1676,7 @@
         out_shape=(S((1536, 768), BF16), S((U, 3072), BF16), S((U, 768), BF16), S((U, 2304), BF16), S((12, U), F32), S((rows, d), BF16)),
         in_specs=[sspec, vspec, vspec] + [anyspec] * 12,
         out_specs=(anyspec,) * 4 + (vspec, anyspec),
-        scratch_shapes=[V((6144, d), BF16), V((d, d), BF16), V((3, d, d), BF16), V((2, rows, d), F32), V((rows, 3072), BF16),
+        scratch_shapes=[V((6144, d), BF16), V((d, d), BF16), V((3 * d, d), BF16), V((2, rows, d), F32), V((rows, 3072), BF16),
                         V((rows, d), F32), V((rows, d), BF16), V((rows, d), F32), V((rows, d), BF16), V((nblk, rows, d), BF16),
                         V((nblk, 32, rows), F32), V((rows, 256), F32), V((3, rows, d), BF16),
                         V((N, 2, U, U), BF16), V((4, 2, U, U), BF16), V((N, 2, U, U), BF16), V((N, U, U), BF16),

time: 243 us -> 219 us (0.901)
  Pallas kernels: 224 us -> 202 us
    pallas_call x1, Pallas kernels: 150 us -> 135 us  [backward_reduce(): pl.pallas_call(functools.partial(bwd_kernel, nx, nd, seqs, rows // seqs),...]
    pallas_call x1, Pallas kernels: 73.4 us -> 66.7 us  [forward_gather(): pl.pallas_call(functools.partial(fwd_kernel, nx, seqs, seq_rows), out_sha...]
where the time goes in v5:
time: 219 us; the launch traced here: 217 us
  Pallas kernels  202 us (92%)
  other arithmetic  9.48 us (4%)
  local copies, waits for them, and re-layouts  5.62 us (3%)
    pallas_call x1, Pallas kernels, backward_reduce(): pl.pallas_call(functools.partial(bwd_kernel, nx, nd, seqs, rows // seqs),...  135 us
    pallas_call x1, Pallas kernels, forward_gather(): pl.pallas_call(functools.partial(fwd_kernel, nx, seqs, seq_rows), out_sha...  66.7 us

profile of v5, /device:TPU:5, one launch (start us, length us, event | category | flops | bytes accessed | tf_op | source)
XLA Modules:
  0.0 217.3 jit_solution(11615390645633616025)
XLA Ops:
  0.7 66.7 %forward_gather.1 = (bf16[3,4,512,768]{3,2,1,0:T(8,128)(2,1)}, f32[512,768]{1,0:T(8,128)}, f32[512,256]{1,0:T(8,128)}, bf16[768,2304]{1,0:T(8,128)(2,1)}, bf16[7...) custom-call(s32[2]{0:T(128)} %lens.3, ...), custom_call_target="tpu_custom_call" | custom-call | tf_op jit(solution)/shard_map/forward_gather/pallas_call | solution.py:1043
  67.3 134.9 %backward_reduce.1 = (bf16[1536,768]{1,0:T(8,128)(2,1)}, bf16[384,3072]{1,0:T(8,128)(2,1)}, bf16[384,768]{1,0:T(8,128)(2,1)}, bf16[384,2304]{1,0:T(8,128)(2,1)},...) custom-call(s32[2]{0:T(128)} %lens.3, f32[2,12,384]{2,1,0:T(8,128)} %get-tuple-element.36.vec, ...), custom_call_target="tpu_custom_call" | custom-call | tf_op jit(solution)/shard_map/backward_reduce/pallas_call | solution.py:1674
  202.2 0.0 copy-start.2
  202.2 0.9 slice.32
  203.1 1.6 slice_reduce_fusion
  204.6 0.6 reshape.79
  205.2 2.2 convert_element_type.13
  207.4 0.0 copy-done.2
  207.4 0.0 copy-start.1
  207.4 2.0 convert_element_type.12
  209.4 0.8 copy-done.1
  210.2 0.0 copy-start
  210.2 2.8 %convert_element_type.14 = f32[384,3072]{1,0:T(8,128)} convert(bf16[384,3072]{1,0:T(8,128)(2,1)S(1)} %copy-done.1) | non-fusion elementwise | flops 1179648 | bytes 7077888 | tf_op jit(solution)/shard_map/convert_element_type | solution.py:1710
  213.0 0.0 copy-done
  213.0 0.0 copy-start.3
  213.0 0.0 copy-start.4
  213.0 2.5 %convert_element_type.15 = f32[1536,768]{1,0:T(8,128)} convert(bf16[1536,768]{1,0:T(8,128)(2,1)S(1)} %copy-done) | non-fusion elementwise | flops 1179648 | bytes 7077888 | tf_op jit(solution)/shard_map/convert_element_type | solution.py:1711
  215.5 0.0 copy-done.3
  215.5 0.9 copy.33
  216.4 0.0 copy-done.4
  216.4 0.9 copy.34
Async XLA Ops:
  202.2 5.2 %copy-start.2 = (bf16[384,2304]{1,0:T(8,128)(2,1)S(1)}, bf16[384,2304]{1,0:T(8,128)(2,1)}, u32[]{:S(2)}) copy-start(bf16[384,2304]{1,0:T(8,128)(2,1)} %get-tuple-element.50) | copy-start | bytes 5308420
  207.4 2.8 %copy-start.1 = (bf16[384,3072]{1,0:T(8,128)(2,1)S(1)}, bf16[384,3072]{1,0:T(8,128)(2,1)}, u32[]{:S(2)}) copy-start(bf16[384,3072]{1,0:T(8,128)(2,1)} %get-tuple-element.53) | copy-start | bytes 7077892
  210.2 2.8 %copy-start = (bf16[1536,768]{1,0:T(8,128)(2,1)S(1)}, bf16[1536,768]{1,0:T(8,128)(2,1)}, u32[]{:S(2)}) copy-start(bf16[1536,768]{1,0:T(8,128)(2,1)} %get-tuple-element.54) | copy-start | bytes 7077892
  213.0 2.6 %copy-start.3 = (bf16[512,768]{1,0:T(8,128)(2,1)S(1)}, bf16[512,768]{1,0:T(8,128)(2,1)}, u32[]{:S(2)}) copy-start(bf16[512,768]{1,0:T(8,128)(2,1)} %get-tuple-element.35) | copy-start | bytes 2359300
  213.0 3.4 %copy-start.4 = (bf16[512,768]{1,0:T(8,128)(2,1)S(1)}, bf16[512,768]{1,0:T(8,128)(2,1)}, u32[]{:S(2)}) copy-start(bf16[512,768]{1,0:T(8,128)(2,1)} %get-tuple-element.49) | copy-start | bytes 2359300

commit v6 on v5

--- a/solution.py
+++ b/solution.py
@@ -1066,14 +1066,14 @@
 
 def bwd_kernel(nx, nd, seqs, seq_rows, lens, vec, vg, qkv_i, att_i, lse_i, wq_i, wo_i, wu_i, wd_i, dh_i, hat_i, act_i, gp_i, tok_i,
                od, ou, oo, oq, ov, gin_o,
-               BIG, WO, WQ, GP, ACT, DH, DM, HAT, NB, DO, ROWS, COLS, DQKV, L, SB, R1, R2, R3, R4, AX, VV, V0, VX, VZ,
-               lds, d0s, d0r, d1s, d1r, d2s, d2r, s1s, s1r, s2s, s2r, s3s, s3r, s4s, s4r, s5s, s5r, s6s, s6r, s7s, s7r, s8, vs, vr):
+               BIG, WO, WQ, GP, ACT, DH, DM, HAT, NB, DO, ROWS, COLS, DQKV, L, SB, R1, R2, R3, R4, RH, AX, VV, V0, VX, VZ,
+               lds, d0s, d0r, d1s, d1r, d2s, d2r, s1s, s1r, s2s, s2r, s3s, s3r, s4s, s4r, s5s, s5r, s6s, s6r, s7s, s7r, s8, vs, vr, hs, hr):
     core, x, f, z = places()
     me = x * 2 + core
     nblk = 2 * nx
     rows = seqs * seq_rows
     CX, PZ = U // nx, U // nx // nd
-    NCH, READY = 12, 8
+    NCH, READY, QFIRST = 12, 8, 3
     sib = {"ctx": x * 2 + 1 - core}
     yp = {"fsdp": 1 - f}
     xps = [{"ctx": lax.rem(x + j, nx) * 2 + core} for j in range(1, nx)]
@@ -1117,14 +1117,42 @@
 
     def c3(c, j):
         xt = lax.rem(x + j, nx)
-        return remote(L.at[c, f, pl.ds(pl.multiple_of(xt * CX, CX), CX)], R3.at[c, j - 1], s3s.at[c, j - 1], s3r.at[c, j - 1], xps[j - 1])
+        return remote(L.at[c, f, pl.ds(pl.multiple_of(xt * CX, CX), CX)], R3.at[c - READY - 1, j - 1], s3s.at[c, j - 1], s3r.at[c, j - 1], xps[j - 1])
 
     def mine(zz):
-        return pl.ds(pl.multiple_of(x * CX + zz * PZ, PZ), PZ)
+        return pl.ds(pl.multiple_of(x * CX + (lax.rem(zz, 2) * 2 + zz // 2) * PZ, PZ), PZ)
+
+    zpar = lax.rem(z, 2)
+    ways = {"x": (x, xps[0]), "near": (zpar, {"dp": z + 1 - 2 * zpar}), "far": (z // 2, {"dp": lax.rem(z + 2, nd)})}
+
+    def level(c, k):
+        dims = ("near", "far", "x") if c < QFIRST else ("x", "near", "far")
+        base, n = 0, U
+        for d in dims[:k]:
+            n = n // 2
+            base = base + ways[d][0] * n
+        bit, dev = ways[dims[k]]
+        half = n // 2
+        at = (0, U // 2, 3 * U // 4)[k]
+        keep = pl.ds(pl.multiple_of(base + bit * half, half), half)
+        give = pl.ds(pl.multiple_of(base + (1 - bit) * half, half), half)
+        return keep, give, pl.ds(at, half), half, at, base + bit * half, base + (1 - bit) * half, dev
+
+    def down(c, k):
+        _, give, at, _, _, _, _, dev = level(c, k)
+        return remote(L.at[c, f, give], RH.at[c, at], hs.at[c, k], hr.at[c, k], dev)
+
+    def upw(c, k):
+        keep, _, _, _, _, _, _, dev = level(c, k)
+        w = AX.at[c, keep]
+        return remote(w, w, hs.at[c, 3 + k], hr.at[c, 3 + k], dev)
+
+    def direct(c):
+        return c > READY
 
     def c4(c, j):
         zt = lax.rem(z + j, nd)
-        return remote(L.at[c, f, mine(zt)], R4.at[c, j - 1], s4s.at[c, j - 1], s4r.at[c, j - 1], zps[j - 1])
+        return remote(L.at[c, f, mine(zt)], R4.at[c - READY - 1, j - 1], s4s.at[c, j - 1], s4r.at[c, j - 1], zps[j - 1])
 
     def c5(c, j):
         w = AX.at[c, mine(z)]
@@ -1196,18 +1224,64 @@
             s = pl.ds(pl.multiple_of(x * CX + r, B), B)
             t = up(L[c, f, s, :]) + up(R1[c, f, s, :]) + up(R2[c, s, :])
             for j in range(1, nx):
-                t = t + up(R3[c, j - 1, pl.ds(r, B), :])
+                t = t + up(R3[c - READY - 1, j - 1, pl.ds(r, B), :])
             L[c, f, s, :] = t.astype(BF16)
         rows_loop(CX, fn)
         for j in range(1, nd):
             c4(c, j).start()
+
+    def h0(c):
+        c1(c, f, 1).wait_recv()
+        c2(c).wait_recv()
+        _, _, _, half, _, _, off, _ = level(c, 0)
+
+        def fn(r):
+            s = pl.ds(pl.multiple_of(off + r, B), B)
+            L[c, f, s, :] = (up(L[c, f, s, :]) + up(R1[c, f, s, :]) + up(R2[c, s, :])).astype(BF16)
+        rows_loop(half, fn)
+        down(c, 0).start()
+
+    def h1(c):
+        down(c, 0).wait_recv()
+        _, _, _, half, at, off, _, _ = level(c, 0)
+
+        def fn(r):
+            s = pl.ds(pl.multiple_of(off + r, B), B)
+            t = up(L[c, f, s, :]) + up(R1[c, f, s, :]) + up(R2[c, s, :]) + up(RH[c, pl.ds(pl.multiple_of(at + r, B), B), :])
+            L[c, f, s, :] = t.astype(BF16)
+        rows_loop(half, fn)
+        down(c, 1).start()
+
+    def h2(c):
+        down(c, 1).wait_recv()
+        _, _, _, half, at, off, _, _ = level(c, 1)
+
+        def fn(r):
+            s = pl.ds(pl.multiple_of(off + r, B), B)
+            L[c, f, s, :] = (up(L[c, f, s, :]) + up(RH[c, pl.ds(pl.multiple_of(at + r, B), B), :])).astype(BF16)
+        rows_loop(half, fn)
+        down(c, 2).start()
+
+    def h3(c):
+        down(c, 2).wait_recv()
+        keep, _, at, _, _, _, _, _ = level(c, 2)
+        AX[c, keep, :] = (up(L[c, f, keep, :]) + up(RH[c, at, :])).astype(BF16)
+        upw(c, 2).start()
+
+    def h4(c):
+        upw(c, 2).wait_recv()
+        upw(c, 1).start()
+
+    def h5(c):
+        upw(c, 1).wait_recv()
+        upw(c, 0).start()
 
     def st5(c):
         for j in range(1, nd):
             c4(c, j).wait_recv()
         t = up(L[c, f, mine(z), :])
         for j in range(1, nd):
-            t = t + up(R4[c, j - 1])
+            t = t + up(R4[c - READY - 1, j - 1])
         AX[c, mine(z), :] = t.astype(BF16)
         for j in range(1, nd):
             c5(c, j).start()
@@ -1219,8 +1293,11 @@
             c6(c, j).start()
 
     def st7(c):
-        for j in range(1, nx):
-            c6(c, j).wait_recv()
+        if direct(c):
+            for j in range(1, nx):
+                c6(c, j).wait_recv()
+        else:
+            upw(c, 0).wait_recv()
         c7(c).start()
         c8(c).start()
 
@@ -1344,7 +1421,7 @@
     for k in (1, 2, 0):
         for blk in range(nblk):
             load(("qkv", k, blk), qkv_i.at[k, blk], BIG.at[pl.ds((k * nblk + blk) * rows, rows)])
-    st3(0)
+    h0(0)
     loads["lse"].wait()
 
     def ln1(i, carry):
@@ -1407,6 +1484,8 @@
     for j in range(1, nx):
         r_x(j).start()
     r_sib().start()
+    h1(0)
+    h0(1)
     for ii in range(2):
         for kk in (1, 0):
             if kk == 1:
@@ -1427,7 +1506,9 @@
     load("tok", tok_i, NB)
     for b in range(3):
         load(("wq", b), wq_i.at[:, pl.ds(b * 768, 768)], WQ.at[pl.ds(b * 768, 768)])
-    st3(1)
+    h2(0)
+    h1(1)
+    h0(2)
     st2(6)
     for kk in (1, 0):
         if kk == 1:
@@ -1557,36 +1638,38 @@
             if kk == 1:
                 st1(i)
 
-    segment(dq_one, 0, ntile * 6, (((st3, (2,)), (st4, (0,)), ),
-             ((st3, (3,)), ),
-             (),
-             ((st5, (0,)), (relay, ()), ),
-             ((st3, (4,)), (st4, (1,)), ),
-             ((st3, (5,)), (st6, (0,)), (st4, (2,)), ),))
+    segment(dq_one, 0, ntile * 6, (((h2, (1,)), (h1, (2,)), ),
+             ((h0, (3,)), ),
+             ((h2, (2,)), ),
+             ((relay, ()), (h0, (4,)), ),
+             ((h3, (0,)), (h3, (1,)), (h1, (3,)), ),
+             ((h0, (5,)), (h1, (4,)), (h4, (0,)), (h2, (3,)), (h3, (2,)), (h4, (1,)), ),))
     loads["tok"].wait()
     project(9)
     put_vec(0, bias_sum(0))
-    st2(9)
     d_sib().wait_recv()
     r_sib().wait_recv()
     for j in range(1, nx):
         d_f(j).wait_recv()
         r_f(j).wait_recv()
-    segment(dkv_one, 0, ntile * 3, (((st4, (3,)), (st5, (1,)), ),
-             ((st3, (6,)), (st5, (2,)), (st4, (4,)), ),
-             ((st3, (7,)), (st5, (3,)), (st6, (1,)), (st4, (5,)), ),))
+    segment(dkv_one, 0, ntile * 3, (((st2, (9,)), (h0, (6,)), (h5, (0,)), (h1, (5,)), (h4, (2,)), ),
+             ((h5, (1,)), (h2, (4,)), (h3, (3,)), ),
+             ((h0, (7,)), (h5, (2,)), (h1, (6,)), (h2, (5,)), ),))
     project(10)
-    st2(10)
-    segment(dkv_one, ntile * 3, ntile * 3, (((st6, (2,)), (st5, (4,)), ),
-             ((st3, (8,)), (st5, (5,)), (st4, (6,)), (st6, (3,)), ),
-             ((st3, (9,)), (st4, (7,)), (st6, (4,)), ),))
+    segment(dkv_one, ntile * 3, ntile * 3, (((st2, (10,)), (h0, (8,)), (h3, (4,)), (h4, (3,)), (h1, (7,)), ),
+             ((h2, (6,)), (h3, (5,)), (h4, (4,)), (h5, (3,)), ),
+             ((st3, (9,)), (h1, (8,)), (h4, (5,)), (h2, (7,)), ),))
     put_vec(2, bias_sum(2))
     vst(0)
     project(11)
     vst(1)
     st2(11)
-    st5(6)
-    st6(5)
+    h5(4)
+    h3(6)
+    h2(8)
+    st4(9)
+    h5(5)
+    h3(7)
     for b in range(3):
         loads[("wq", b)].wait()
     for t in range(3):
@@ -1597,33 +1680,33 @@
         DM[:, cs] = acc.astype(BF16)
     gout = pltpu.make_async_copy(DM, gin_o, s8.at[NCH])
     gout.start()
-    st4(8)
-    st5(7)
-    st6(6)
+    st3(10)
+    h4(6)
+    h4(7)
+    h3(8)
+    st5(9)
     vst(2)
-    st3(10)
-    st4(9)
+    st4(10)
+    h5(6)
+    h5(7)
+    h4(8)
+    st3(11)
+    st6(9)
+    vst(3)
+    st5(10)
+    h5(8)
+    st4(11)
+    vst(4)
     st7(0)
     st7(1)
     st7(2)
-    st5(8)
-    st6(7)
-    vst(3)
     st7(3)
     st7(4)
-    st3(11)
-    st4(10)
-    st5(9)
-    st6(8)
-    vst(4)
     st7(5)
+    st6(10)
+    st5(11)
     st7(6)
-    st4(11)
-    st5(10)
-    st6(9)
     st7(7)
-    st5(11)
-    st6(10)
     st7(8)
     st6(11)
     st7(9)
@@ -1633,12 +1716,17 @@
         c2(c).wait_send()
         c7(c).wait()
         c8(c).wait()
-        for j in range(1, nx):
-            c3(c, j).wait_send()
-            c6(c, j).wait_send()
-        for j in range(1, nd):
-            c4(c, j).wait_send()
-            c5(c, j).wait_send()
+        if direct(c):
+            for j in range(1, nx):
+                c3(c, j).wait_send()
+                c6(c, j).wait_send()
+            for j in range(1, nd):
+                c4(c, j).wait_send()
+                c5(c, j).wait_send()
+        else:
+            for k in range(3):
+                down(c, k).wait_send()
+                upw(c, k).wait_send()
     for i in (8, 9, 10, 11):
         for cp in c1s(i):
             cp.wait_send()
@@ -1670,7 +1758,7 @@
     S = jax.ShapeDtypeStruct
     sems = [D((40,)), D((2,)), D((2,))] + [D((nx - 1, 2))] * 4 + [D((N, 2)), D((N, 2)), D((N,)), D((N,)), D((N, nx - 1)), D((N, nx - 1)),
             D((N, nd - 1)), D((N, nd - 1)), D((N, nd - 1)), D((N, nd - 1)), D((N, nx - 1)), D((N, nx - 1)),
-            D((N,)), D((N,)), D((N + 1,)), D((nx + nd,)), D((nx + nd,))]
+            D((N,)), D((N,)), D((N + 1,)), D((nx + nd,)), D((nx + nd,)), D((9, 6)), D((9, 6))]
     return pl.pallas_call(
         functools.partial(bwd_kernel, nx, nd, seqs, rows // seqs),
         out_shape=(S((1536, 768), BF16), S((U, 3072), BF16), S((U, 768), BF16), S((U, 2304), BF16), S((12, U), F32), S((rows, d), BF16)),
@@ -1680,11 +1768,47 @@
                         V((rows, d), F32), V((rows, d), BF16), V((rows, d), F32), V((rows, d), BF16), V((nblk, rows, d), BF16),
                         V((nblk, 32, rows), F32), V((rows, 256), F32), V((3, rows, d), BF16),
                         V((N, 2, U, U), BF16), V((4, 2, U, U), BF16), V((N, 2, U, U), BF16), V((N, U, U), BF16),
-                        V((N, nx - 1, CX, U), BF16), V((N, nd - 1, PZ, U), BF16), V((N, U, U), BF16),
+                        V((3, nx - 1, CX, U), BF16), V((3, nd - 1, PZ, U), BF16), V((9, U - PZ, U), BF16), V((N, U, U), BF16),
                         V((24, U), F32), V((3, 24, U), F32), V((nx, 24, U), F32), V((nd, 24, U), F32)] + sems,
         compiler_params=pltpu.CompilerParams(collective_id=cid, has_side_effects=True, vmem_limit_bytes=63 << 20),
         name="backward_reduce",
     )(lens, vec, vg, qkv, att, lse, wq, wo, wu, wd, dh, hat, act, gp, tok)
+
+
+FIN = 4
+
+
+def finish_kernel(td, tu, to, tq, vec, y, gi, *outs):
+    fd, fu, fo, fq, fy, fg = outs[:6]
+    for src, dst in ((td, fd), (tu, fu), (to, fo), (tq, fq)):
+        dst[...] = src[...].astype(F32)
+    fy[...] = y[...]
+    fg[...] = gi[...]
+
+    @pl.when(pl.program_id(0) == 0)
+    def _():
+        row = 0
+        for dst in outs[6:]:
+            for i in range(dst.shape[0] // U):
+                dst[i * U:(i + 1) * U] = vec[row:row + 1, :].reshape(U)
+                row += 1
+
+
+def finish(td, tu, to, tq, vec, y, gi):
+    def spec(a):
+        return pl.BlockSpec((a.shape[0] // FIN, a.shape[1]), lambda i: (i, 0))
+
+    big = [td, tu, to, tq]
+    sizes = [U, U, U, U, U, 4 * U, U, U, U]
+    S = jax.ShapeDtypeStruct
+    return pl.pallas_call(
+        finish_kernel,
+        grid=(FIN,),
+        in_specs=[spec(a) for a in big] + [pl.BlockSpec(vec.shape, lambda i: (0, 0)), spec(y), spec(gi)],
+        out_specs=[spec(a) for a in big] + [spec(y), spec(gi)] + [pl.BlockSpec((n,), lambda i: (0,)) for n in sizes],
+        out_shape=[S(a.shape, F32) for a in big] + [S(y.shape, y.dtype), S(gi.shape, gi.dtype)] + [S((n,), F32) for n in sizes],
+        name="finish",
+    )(td, tu, to, tq, vec, y, gi)
 
 
 def fast_body(
@@ -1702,19 +1826,18 @@
         tokens.reshape(seqs * seq_rows, width), nx, nd, seqs, 3
     )
 
-    def part(first, count):
-        return t_vec[first : first + count].reshape(-1)
-
+    (f_down, f_up, f_out, f_qkv, out, grad_in, bq, bv, bo, g1, s1, bu, bd, g2, s2) = finish(
+        t_down, t_up, t_out, t_qkv, t_vec, out, grad_in
+    )
     return (
-        out.reshape(tokens.shape), grad_in.reshape(tokens.shape), t_qkv.astype(F32), part(0, 1), part(1, 1),
-        t_out.astype(F32), part(2, 1), part(3, 1), part(4, 1), t_up.astype(F32), part(5, 4),
-        t_down.astype(F32), part(9, 1), part(10, 1), part(11, 1),
+        out.reshape(tokens.shape), grad_in.reshape(tokens.shape), f_qkv, bq, bv,
+        f_out, bo, g1, s1, f_up, bu, f_down, bd, g2, s2,
     )
 
 
 def solution(mesh):
     return jax.shard_map(
-        fast_body if mesh.shape["ctx"] <= 4 else general_body,
+        fast_body if mesh.shape["ctx"] == 4 and mesh.shape["dp"] == 4 else general_body,
         mesh=mesh,
         in_specs=(
             P(("dp", "fsdp"), "ctx", None),

time: 219 us -> 212 us (0.968)
  other arithmetic: 9.48 us -> 0 us
  Pallas kernels: 202 us -> 210 us
  local copies, waits for them, and re-layouts: 5.62 us -> 0 us
    pallas_call x0 -> x1, Pallas kernels: none -> 9.93 us  [finish(): pl.pallas_call(finish_kernel, grid=(FIN,), in_specs=[spec(a) for a in big...]
    convert_element_type x4 -> x0, other arithmetic: 9.48 us -> none  [the longest x1 2.76 us: fast_body(): t_up.astype(F32)]
    unnamed x12 -> x0, local copies, waits for them, and re-layouts: 2.58 us -> none
    slice x2 -> x0, local copies, waits for them, and re-layouts: 2.44 us -> none  [part(): return t_vec[first:first + count].reshape(-1)]
where the time goes in v6:
time: 212 us; the launch traced here: 211 us
  Pallas kernels  210 us (99%)
    pallas_call x1, Pallas kernels, backward_reduce(): pl.pallas_call(functools.partial(bwd_kernel, nx, nd, seqs, rows // seqs),...  133 us
    pallas_call x1, Pallas kernels, forward_gather(): pl.pallas_call(functools.partial(fwd_kernel, nx, seqs, seq_rows), out_sha...  66.7 us
    pallas_call x1, Pallas kernels, finish(): pl.pallas_call(finish_kernel, grid=(FIN,), in_specs=[spec(a) for a in big...  9.93 us

profile of v6, /device:TPU:5, one launch (start us, length us, event | category | flops | bytes accessed | tf_op | source)
XLA Modules:
  0.0 210.5 jit_solution(392428014647939171)
XLA Ops:
  0.7 66.7 %forward_gather.1 = (bf16[3,4,512,768]{3,2,1,0:T(8,128)(2,1)}, f32[512,768]{1,0:T(8,128)}, f32[512,256]{1,0:T(8,128)}, bf16[768,2304]{1,0:T(8,128)(2,1)}, bf16[7...) custom-call(s32[2]{0:T(128)} %lens.3, ...), custom_call_target="tpu_custom_call" | custom-call | tf_op jit(solution)/shard_map/forward_gather/pallas_call | solution.py:1043
  67.3 133.1 %backward_reduce.1 = (bf16[1536,768]{1,0:T(8,128)(2,1)}, bf16[384,3072]{1,0:T(8,128)(2,1)}, bf16[384,768]{1,0:T(8,128)(2,1)}, bf16[384,2304]{1,0:T(8,128)(2,1)},...) custom-call(s32[2]{0:T(128)} %lens.3, f32[2,12,384]{2,1,0:T(8,128)} %get-tuple-element.50.vec, ...), custom_call_target="tpu_custom_call" | custom-call | tf_op jit(solution)/shard_map/backward_reduce/pallas_call | solution.py:1762
  200.4 9.9 %finish.1 = (f32[1536,768]{1,0:T(8,128)}, f32[384,3072]{1,0:T(8,128)}, f32[384,768]{1,0:T(8,128)}, f32[384,2304]{1,0:T(8,128)}, bf16[512,768]{1,0:T(8,128)(2,1)}...) custom-call(bf16[1536,768]{1,0:T(8,128)(2,1)} %get-tuple-element.63., ...), custom_call_target="tpu_custom_call" | custom-call | tf_op jit(solution)/shard_map/finish/pallas_call | solution.py:1804
